TPU v7x, 32 devices: a whole 2x2x4 slice. The times are simulated.
32 devices in a mesh: dp: 8 (over z, core), height: 4 (over y, x).
Axes of the slice: x: 2, y: 2, z: 4, core: 2. Of those that a mesh axis runs over, the one named last changes fastest.
Arguments:
- latents: bfloat16 [8, 16, 128, 640], P('dp', 'height'), parts along dimension 0, may hold values from -20 to 20
- latent_tangent: bfloat16 [8, 16, 128, 640], P('dp', 'height'), parts along dimension 0, may hold values from -20 to 20
- gain_first: float32 [640], replicated, may hold values from 0.5 to 2
- weight_first: bfloat16 [9, 640, 640], P(None, None, 'height'), may hold values from -0.078125 to 0.078125
- gain_second: float32 [640], replicated, may hold values from 0.5 to 2
- weight_second: bfloat16 [9, 640, 640], P(None, None, 'height'), may hold values from -0.078125 to 0.078125
Outputs:
- block_output: bfloat16 [8, 16, 128, 640], P('dp', 'height'), parts along dimension 0
- output_tangent: bfloat16 [8, 16, 128, 640], P('dp', 'height'), parts along dimension 0
There are 8 independent parts, one for each index of `dp`. A program takes and returns all parts, laid end to end along the dimension named above; an argument that names none is the same for every part. Nothing has to cross between parts.
All inputs are finite; a program needn't handle non-finite values.
Results may differ from a plain program's by a relative error of at most 0.006.
Values may be sent and summed in bfloat16 or wider, within the bound.
No kernel may reach another device: no remote copies, remote signals or barrier semaphores. Data moves between devices by JAX's collectives and lax.ppermute only.
A program may use at most 128 MiB of HBM per device.

v0:
```python
import functools

import jax
import jax.numpy as jnp
from jax import lax
from jax.experimental import pallas as pl
from jax.experimental.pallas import tpu as pltpu
from jax.sharding import PartitionSpec as P


GROUPS = 32
EPSILON = 1e-05
AXES = ("dp", "height")
BF = jnp.bfloat16
F32 = jnp.float32
STAT_ROWS = 16
VMEM_LIMIT = 32 * 1024 * 1024


def split3(x):
    hi = x.astype(BF)
    rest = x - hi.astype(F32)
    mid = rest.astype(BF)
    low = (rest - mid.astype(F32)).astype(BF)
    return hi, mid, low


def pack_stats(v_sum, t_sum, v_sq, vt):
    rows = jnp.concatenate([v_sum, t_sum, v_sq, vt], axis=0)
    hi, mid, low = split3(rows)
    pad = jnp.zeros((STAT_ROWS - 12, rows.shape[1]), F32)
    return jnp.concatenate([hi.astype(F32), mid.astype(F32), low.astype(F32), pad], axis=0).astype(BF)


def unpack_stats(packed):
    f = packed.astype(F32)
    return f[0:4] + (f[4:8] + f[8:12])


def local_stats(v_rows, t_rows, count):
    v_sum = sum(jnp.sum(v(), axis=0, keepdims=True) for v in v_rows)
    t_sum = sum(jnp.sum(t(), axis=0, keepdims=True) for t in t_rows)
    v_mean = v_sum / count
    t_mean = t_sum / count
    v_sq = 0.0
    vt = 0.0
    for v, t in zip(v_rows, t_rows):
        vc = v() - v_mean
        tc = t() - t_mean
        v_sq = v_sq + jnp.sum(vc * vc, axis=0, keepdims=True)
        vt = vt + jnp.sum(vc * tc, axis=0, keepdims=True)
    return pack_stats(v_sum, t_sum, v_sq, vt)


def group_matrix(chans):
    size = chans // GROUPS
    r = lax.broadcasted_iota(jnp.int32, (chans, 1), 0)
    c = lax.broadcasted_iota(jnp.int32, (1, chans), 1)
    rg = jnp.floor((r.astype(F32) + 0.5) / size)
    cg = jnp.floor((c.astype(F32) + 0.5) / size)
    return jnp.where(rg == cg, 1.0, 0.0).astype(BF)


def group_sum(rows, matrix):
    hi, mid, low = split3(rows)
    dot = functools.partial(jnp.dot, preferred_element_type=F32)
    return dot(hi, matrix) + (dot(mid, matrix) + dot(low, matrix))


def coefficients(stats, gain, count, total):
    chans = gain.shape[1]
    matrix = group_matrix(chans)
    first = stats[0][0:2]
    for s in stats[1:]:
        first = first + s[0:2]
    pad6 = jnp.zeros((6, chans), F32)
    means = group_sum(jnp.concatenate([first, pad6], 0), matrix)[0:2] / total
    mean = means[0:1]
    tmean = means[1:2]
    sq = 0.0
    cross = 0.0
    for s in stats:
        dm = s[0:1] / count - mean
        dt = s[1:2] / count - tmean
        sq = sq + (s[2:3] + count * dm * dm)
        cross = cross + (s[3:4] + count * dm * dt)
    seconds = group_sum(jnp.concatenate([sq, cross, pad6], 0), matrix)[0:2] / total
    inverse = lax.rsqrt(seconds[0:1] + EPSILON)
    scale = gain * inverse
    slope = gain * (seconds[1:2] * (inverse * inverse * inverse))
    return mean, tmean, scale, slope


def activate(v, t, coeff):
    mean, tmean, scale, slope = coeff
    vc = v - mean
    a = vc * scale
    da = (t - tmean) * scale - vc * slope
    s = 0.5 * jnp.tanh(0.5 * a) + 0.5
    h = a * s
    dh = da * (s + h * (1.0 - s))
    return h, dh


def shifted(x):
    cols = x.shape[0]
    idx = lax.broadcasted_iota(jnp.int32, (cols, 1), 0)
    left = jnp.where(idx == 0, 0.0, pltpu.roll(x, 1, 0))
    right = jnp.where(idx == cols - 1, 0.0, pltpu.roll(x, cols - 1, 0))
    return left, right


def send_rows(info, first, last, hx, hd):
    odd = info[ODD] == 1
    for k in range(2):
        hx[k] = jnp.where(odd, first[k], last[k])
        hd[k] = jnp.where(odd, last[k], first[k])


def sums_kernel(info, lat, tan, sums, hx, hd):
    rows, cols, _ = lat.shape
    sums[...] = local_stats(
        [functools.partial(lambda r: lat[r].astype(F32), r) for r in range(rows)],
        [functools.partial(lambda r: tan[r].astype(F32), r) for r in range(rows)],
        float(rows * cols),
    )
    send_rows(info, (lat[0], tan[0]), (lat[rows - 1], tan[rows - 1]), hx, hd)


def put(xs, row, h, dh):
    chans = h.shape[1]
    for k, value in enumerate((h, dh)):
        left, right = shifted(value)
        xs[row, k, :, 0:chans] = left.astype(BF)
        xs[row, k, :, chans : 2 * chans] = value.astype(BF)
        xs[row, k, :, 2 * chans : 3 * chans] = right.astype(BF)


def act_kernel(n_devices, joined, *refs):
    refs = list(refs)
    if joined:
        both = refs.pop(0)
        rows, cols, chans = both.shape[0], both.shape[2], both.shape[3]
        load = lambda r: (both[r, 0].astype(F32), both[r, 1].astype(F32))
    else:
        lat, tan = refs.pop(0), refs.pop(0)
        rows, cols, chans = lat.shape
        load = lambda r: (lat[r].astype(F32), tan[r].astype(F32))
    s0, s1, s2, s3, gain, xs, coeff_out = refs
    count = float(rows * cols)
    total = count * n_devices * (chans // GROUPS)
    coeff = coefficients([unpack_stats(s[...]) for s in (s0, s1, s2, s3)], gain[...], count, total)
    coeff_out[...] = jnp.concatenate(list(coeff) + [jnp.zeros((4, chans), F32)], 0)
    for r in range(rows):
        put(xs, r, *activate(*load(r), coeff))


def fill(wv, piece, tap, offset):
    height, chans = piece.shape[1], piece.shape[2]
    offset = pl.multiple_of(offset, 16)
    for q in range(3):
        wv[pl.ds(offset, height), q * chans : (q + 1) * chans] = piece[tap + q]


def product(x, w):
    return lax.dot_general(x, w, (((1,), (1,)), ((), ())), preferred_element_type=F32)


def rows_product(xs, start, count, wv):
    cols, wide = xs.shape[2], xs.shape[3]
    x = xs[pl.ds(start, count)].reshape(count * 2 * cols, wide)
    return product(x, wv[...]).reshape(count, 2, cols, wv.shape[0])


def main_kernel(info, xs, *refs):
    pieces = refs[:7]
    acc, w0, w2, w1 = refs[7:]
    rows = xs.shape[0]
    for p, wv in ((1, w1), (0, w0), (2, w2)):
        for k, piece in enumerate(pieces):
            fill(wv, piece, 3 * p, info[OFFSETS + k])
        if p == 1:
            acc[...] = rows_product(xs, 0, rows, wv)
        elif p == 0:
            acc[1:rows] = acc[1:rows] + rows_product(xs, 0, rows - 1, wv)
        else:
            acc[0 : rows - 1] = acc[0 : rows - 1] + rows_product(xs, 1, rows - 1, wv)


def edge_kernel(final, info, acc_in, w0, w2, hx, hd, coeff, *refs):
    if final:
        lat, tan, out_p, out_t, halo, acc = refs
    else:
        mid, sums, sx, sd, halo, acc = refs
    rows, cols = acc_in.shape[0], acc_in.shape[2]
    co = tuple(coeff[k : k + 1] for k in range(4))
    odd = info[ODD] == 1
    for slot in range(2):
        pick = odd if slot == 0 else jnp.logical_not(odd)
        flag = info[VALID + slot]
        v = jnp.where(pick, hx[0], hd[0]).astype(F32)
        t = jnp.where(pick, hx[1], hd[1]).astype(F32)
        h, dh = activate(v, t, co)
        put(halo, slot, jnp.where(flag == 1, h, 0.0), jnp.where(flag == 1, dh, 0.0))
    acc[...] = acc_in[...]
    acc[0] = acc[0] + rows_product(halo, 0, 1, w0)[0]
    acc[rows - 1] = acc[rows - 1] + rows_product(halo, 1, 1, w2)[0]
    if final:
        for r in range(rows):
            out_p[r] = (lat[r].astype(F32) + acc[r, 0]).astype(BF)
            out_t[r] = (tan[r].astype(F32) + acc[r, 1]).astype(BF)
    else:
        mid[...] = acc[...].astype(BF)
        sums[...] = local_stats(
            [functools.partial(lambda r: mid[r, 0].astype(F32), r) for r in range(rows)],
            [functools.partial(lambda r: mid[r, 1].astype(F32), r) for r in range(rows)],
            float(rows * cols),
        )
        send_rows(info, (mid[0, 0], mid[0, 1]), (mid[rows - 1, 0], mid[rows - 1, 1]), sx, sd)


VM = functools.partial(pl.BlockSpec, memory_space=pltpu.VMEM)
SM = functools.partial(pl.BlockSpec, memory_space=pltpu.SMEM)
ODD, VALID, OFFSETS = 0, 1, 3


def call(kernel, args, outs, scratch=(), flops=0):
    return pl.pallas_call(
        kernel,
        out_shape=tuple(jax.ShapeDtypeStruct(s, d) for s, d in outs),
        in_specs=[SM() if a.dtype == jnp.int32 else VM() for a in args],
        out_specs=tuple(VM() for _ in outs),
        scratch_shapes=list(scratch),
        compiler_params=pltpu.CompilerParams(vmem_limit_bytes=VMEM_LIMIT),
        cost_estimate=pl.CostEstimate(flops=flops, bytes_accessed=0, transcendentals=0),
    )(*args)


def fast_device(latents, latent_tangent, gain_first, weight_first, gain_second, weight_second):
    n = lax.axis_size("height")
    nd = lax.axis_size("dp")
    h = lax.axis_index("height")
    d = lax.axis_index("dp")
    core = d % 2
    plane = (d // 2) % 2
    rows, cols, chans = latents.shape[1:]
    shard = weight_first.shape[2]
    half = shard // 2

    def permute(x, target, keep=lambda a, i: True):
        pairs = []
        for a in range(nd):
            for i in range(n):
                if keep(a, i):
                    ta, ti = target(a, i)
                    pairs.append((a * n + i, ta * n + ti))
        return lax.ppermute(x, AXES, pairs)

    plane_to = lambda a, i: (a ^ 2, i)
    core_to = lambda a, i: (a ^ 1, i)

    def gather(weight):
        w = jnp.swapaxes(weight, 1, 2)
        role = lambda a: (a % 2) ^ (a // 2 % 2)
        part = lax.dynamic_slice_in_dim(w, half * core, half, axis=1)
        first = permute(part, lambda a, i: (a, i ^ (1 + role(a))))
        relay = permute(first, lambda a, i: (a, i ^ (2 - role(a))))
        plane = permute(first, plane_to)
        first_s = permute(first, core_to)
        relay_s = permute(relay, core_to)
        plane_s = permute(plane, core_to)
        return [w, first, first_s, relay, relay_s, plane, plane_s]

    def exchange(sums, hx, hd):
        xs = permute(sums, lambda a, i: (a, i ^ 1))
        ds = permute(sums, lambda a, i: (a, i ^ 3))
        ys = permute(sums, lambda a, i: (a, i ^ 2))
        xr = permute(hx, lambda a, i: (a, i ^ 1))
        dr = permute(hd, lambda a, i: (a, i ^ 3), lambda a, i: 0 < i < n - 1)
        return (sums, xs, ys, ds), (xr, dr)

    role = core ^ plane
    here, there = half * core, half * (1 - core)
    info = jnp.stack(
        [
            h % 2,
            (h > 0).astype(jnp.int32),
            (h < n - 1).astype(jnp.int32),
            shard * h,
            shard * (h ^ (1 + role)) + here,
            shard * (h ^ (2 - role)) + there,
            shard * (h ^ 3) + here,
            shard * (h ^ 3) + there,
            shard * (h ^ (2 - role)) + here,
            shard * (h ^ (1 + role)) + there,
        ]
    ).astype(jnp.int32)

    lat = latents[0]
    tan = latent_tangent[0]
    edge = ((2, cols, chans), BF)
    small = ((STAT_ROWS, chans), BF)
    wide = ((rows, 2, cols, 3 * chans), BF)
    acc_t = ((rows, 2, cols, chans), F32)
    wrow = ((chans, 3 * chans), BF)
    work = 2 * rows * 2 * cols * 3 * chans * chans

    def block(k, source, gain, sums, hx, hd, pieces, extra, outs):
        stats, edges = exchange(sums, hx, hd)
        xs, coeff = call(
            functools.partial(act_kernel, n, len(source) == 1),
            [*source, *stats, gain[None]],
            [wide, ((8, chans), F32)],
            flops=work // 4,
        )
        acc, w0, w2 = call(main_kernel, [info, xs, *pieces], [acc_t, wrow, wrow], [pltpu.VMEM(*wrow)], flops=2 * work)
        return call(
            functools.partial(edge_kernel, k == 2),
            [info, acc, w0, w2, *edges, coeff, *extra],
            outs,
            [pltpu.VMEM((2, 2, cols, 3 * chans), BF), pltpu.VMEM(*acc_t)],
            flops=work,
        )

    pieces1 = gather(weight_first)
    pieces2 = gather(weight_second)
    sums, hx, hd = call(sums_kernel, [info, lat, tan], [small, edge, edge], flops=work // 4)
    middle, sums, hx, hd = block(
        1, [lat, tan], gain_first, sums, hx, hd, pieces1, [], [((rows, 2, cols, chans), BF), small, edge, edge]
    )
    out = ((rows, cols, chans), BF)
    result, dresult = block(2, [middle], gain_second, sums, hx, hd, pieces2, [lat, tan], [out, out])
    return result[None], dresult[None]


def extended(cells, width):
    count = lax.axis_size("height")
    head = lax.slice_in_dim(cells, 0, width, axis=1)
    tail = lax.slice_in_dim(cells, cells.shape[1] - width, cells.shape[1], axis=1)
    up = lax.ppermute(tail, "height", [(i, i + 1) for i in range(count - 1)])
    down = lax.ppermute(head, "height", [(i + 1, i) for i in range(count - 1)])
    return jnp.concatenate([up, cells, down], axis=1)


def plain_normalize(stacked, gain):
    rows, cols, chans = stacked.shape[1:]
    size = chans // GROUPS
    positions = float(rows * cols * size * lax.axis_size("height"))
    grouped = stacked.reshape(2, rows * cols, GROUPS, size)
    mean = lax.psum(jnp.sum(grouped, axis=(1, 3)), "height") / positions
    centered = grouped - mean[:, None, :, None]
    second = lax.psum(jnp.sum(centered * centered[0:1], axis=(1, 3)), "height") / positions
    inverse = lax.rsqrt(second[0] + EPSILON)[None, :, None]
    normed = centered[0] * inverse
    dnormed = centered[1] * inverse - centered[0] * (second[1][None, :, None] * inverse**3)
    a = normed.reshape(rows, cols, chans) * gain
    da = dnormed.reshape(rows, cols, chans) * gain
    s = jax.nn.sigmoid(a)
    return jnp.stack([a * s, da * s * (1.0 + a * (1.0 - s))], 0).astype(BF)


def plain_convolve(hidden, weight):
    rows, cols, chans = hidden.shape[1:]
    padded = jnp.pad(extended(hidden, 1), ((0, 0), (0, 0), (1, 1), (0, 0)))
    full = lax.all_gather(weight, "height", axis=2, tiled=True)
    acc = 0.0
    for t in range(9):
        p, q = t // 3, t % 3
        window = padded[:, p : p + rows, q : q + cols, :].reshape(-1, chans)
        acc = acc + jnp.dot(window, full[t], preferred_element_type=F32)
    return acc.reshape(2, rows, cols, -1)


def plain_device(latents, latent_tangent, gain_first, weight_first, gain_second, weight_second):
    stacked = jnp.concatenate([latents, latent_tangent], 0).astype(F32)
    middle = plain_convolve(plain_normalize(stacked, gain_first), weight_first).astype(BF)
    second = plain_normalize(middle.astype(F32), gain_second)
    result = (stacked + plain_convolve(second, weight_second)).astype(BF)
    return (result[0:1], result[1:2])


def solution(mesh):
    square = mesh.shape["height"] == 4 and mesh.shape["dp"] % 4 == 0
    placed = (
        P("dp", "height", None, None),
        P("dp", "height", None, None),
        P(),
        P(None, None, "height"),
        P(),
        P(None, None, "height"),
    )
    return jax.shard_map(
        fast_device if square else plain_device,
        mesh=mesh,
        in_specs=placed,
        out_specs=(P("dp", "height", None, None), P("dp", "height", None, None)),
        check_vma=False,
    )
```

profile of v0, /device:TPU:0, one launch (start us, length us, event | category | flops | bytes accessed | tf_op | source)
XLA Modules:
  0.0 116.1 jit_solution(7859042272007983062)
XLA Ops:
  0.6 0.0 copy-start.3
  0.6 0.0 copy-start
  0.7 0.0 copy-start.1
  0.7 1.4 %dynamic-slice_bitcast_fusion.1 = bf16[9,80,640]{2,1,0:T(8,128)(2,1)S(1)} fusion(bf16[9,640,160]{1,2,0:T(8,128)(2,1)} %param.9, s32[]{:T(128)S(6)} %select_n.27), kind=kLoop, calls=%fused_computation.1 | loop fusion | bytes 1843204 | tf_op jit(solution)/shard_map/dynamic_slice | solution.py:265
  2.1 0.0 copy-start.5
  2.1 3.0 %collective-permute-start.3 = (bf16[9,80,640]{2,1,0:T(8,128)(2,1)S(1)}, bf16[9,80,640]{2,1,0:T(8,128)(2,1)}, u32[]{:S(2)}, u32[]{:S(2)}) collective-permute-start(bf16[9,80,640]{2,1,0:T(8,128)(2,1)S(1)} %dynamic-slice_bitcast_fusion.1), channel_id=1, source_target_pairs={{0,1},{1,0},{2,3},{3,2},{4,6},{5,7},{6,4},{7,5},{8,10},{9,11},{10,... | collective-permute-start | bytes 2764808 | tf_op jit(solution)/shard_map/ppermute | solution.py:257
  5.2 0.0 copy-done.3
  5.2 1.0 dynamic-slice_bitcast_fusion
  6.2 0.2 collective-permute-start.14
  6.4 10.3 %collective-permute-done.3.refs_1_ = bf16[9,80,640]{2,1,0:T(8,128)(2,1)} collective-permute-done((bf16[9,80,640]{2,1,0:T(8,128)(2,1)S(1)}, bf16[9,80,640]{2,1,0:T(8,128)(2,1)}, u32[]{:S(2)}, u32[]{:S(2)}) %collective-permute-start.3) | collective-permute-done | bytes 921632 | tf_op jit(solution)/shard_map/ppermute | solution.py:257
  16.7 2.0 %collective-permute-start.5 = (bf16[9,80,640]{2,1,0:T(8,128)(2,1)}, bf16[9,80,640]{2,1,0:T(8,128)(2,1)}, u32[]{:S(2)}, u32[]{:S(2)}) collective-permute-start(bf16[9,80,640]{2,1,0:T(8,128)(2,1)} %collective-permute-done.3.refs_1_), channel_id=1, source_target_pairs={{0,2},{1,3},{2,0},{3,1},{4,5},{5,4},{6,7},{7,6},{8,9},{9,8},{10,11... | collective-permute-start | bytes 2764808 | tf_op jit(solution)/shard_map/ppermute | solution.py:257
  18.7 1.5 %collective-permute-start.7 = (bf16[9,80,640]{2,1,0:T(8,128)(2,1)}, bf16[9,80,640]{2,1,0:T(8,128)(2,1)}, u32[]{:S(2)}, u32[]{:S(2)}) collective-permute-start(bf16[9,80,640]{2,1,0:T(8,128)(2,1)} %collective-permute-done.3.refs_1_), channel_id=1, source_target_pairs={{0,8},{1,9},{2,10},{3,11},{4,12},{5,13},{6,14},{7,15},{8,0},{9,1},... | collective-permute-start | bytes 2764808 | tf_op jit(solution)/shard_map/ppermute | solution.py:257
  20.3 0.1 stack.51.info
  20.4 0.0 copy-done
  20.4 0.0 copy-done.1
  20.4 1.3 %shard_map.77 = (bf16[16,640]{1,0:T(8,128)(2,1)S(1)}, bf16[2,128,640]{2,1,0:T(8,128)(2,1)S(1)}, bf16[2,128,640]{2,1,0:T(8,128)(2,1)S(1)}) custom-call(s32[10]{0:T(128)S(1)} %stack.51.info, bf16[4,128,640]{2,1,0:T(8,128)(2,1)S(1)} %bitcast.20, bf16[4,128,640]{2,1,0:T(8,128)(2,1)S(1)} %bitcast.23), custom_call_target="tpu_custom_call" | custom-call | flops 629145600 | tf_op jit(solution)/shard_map/pallas_call | solution.py:228
  21.7 0.6 collective-permute-start
  22.3 1.5 %collective-permute-start.1 = (bf16[16,640]{1,0:T(8,128)(2,1)S(1)}, bf16[16,640]{1,0:T(8,128)(2,1)S(1)}, u32[]{:S(2)}, u32[]{:S(2)}) collective-permute-start(bf16[16,640]{1,0:T(8,128)(2,1)S(1)} %get-tuple-element.21.refs_2_), channel_id=1, source_target_pairs={{0,2},{1,3},{2,0},{3,1},{4,6},{5,7},{6,4},{7,5},{8,10},{9,11},{10,... | collective-permute-start | bytes 61448 | tf_op jit(solution)/shard_map/ppermute | solution.py:257
  23.8 10.8 %collective-permute-done.refs_3_ = bf16[16,640]{1,0:T(8,128)(2,1)S(1)} collective-permute-done((bf16[16,640]{1,0:T(8,128)(2,1)S(1)}, bf16[16,640]{1,0:T(8,128)(2,1)S(1)}, u32[]{:S(2)}, u32[]{:S(2)}) %collective-permute-start) | collective-permute-done | bytes 20512 | tf_op jit(solution)/shard_map/ppermute | solution.py:257
  34.6 3.3 %collective-permute-start.2 = (bf16[16,640]{1,0:T(8,128)(2,1)S(1)}, bf16[16,640]{1,0:T(8,128)(2,1)S(1)}, u32[]{:S(2)}, u32[]{:S(2)}) collective-permute-start(bf16[16,640]{1,0:T(8,128)(2,1)S(1)} %get-tuple-element.21.refs_2_), channel_id=1, source_target_pairs={{0,3},{1,2},{2,1},{3,0},{4,7},{5,6},{6,5},{7,4},{8,11},{9,10},{10,... | collective-permute-start | bytes 61448 | tf_op jit(solution)/shard_map/ppermute | solution.py:257
  37.8 0.0 collective-permute-done.1.refs_4_
  37.8 1.8 %collective-permute-start.4 = (bf16[9,80,640]{2,1,0:T(8,128)(2,1)}, bf16[9,80,640]{2,1,0:T(8,128)(2,1)S(1)}, u32[]{:S(2)}, u32[]{:S(2)}) collective-permute-start(bf16[9,80,640]{2,1,0:T(8,128)(2,1)} %collective-permute-done.3.refs_1_), channel_id=1, source_target_pairs={{0,4},{1,5},{2,6},{3,7},{4,0},{5,1},{6,2},{7,3},{8,12},{9,13},{10,... | collective-permute-start | bytes 2764808 | tf_op jit(solution)/shard_map/ppermute | solution.py:257
  39.7 0.0 collective-permute-done.14.refs_1_
  39.7 0.5 collective-permute-start.16
  40.2 0.0 collective-permute-done.2.refs_5_
  40.2 2.4 %collective-permute-start.18 = (bf16[9,80,640]{2,1,0:T(8,128)(2,1)}, bf16[9,80,640]{2,1,0:T(8,128)(2,1)S(1)}, u32[]{:S(2)}, u32[]{:S(2)}) collective-permute-start(bf16[9,80,640]{2,1,0:T(8,128)(2,1)} %collective-permute-done.14.refs_1_), channel_id=1, source_target_pairs={{0,8},{1,9},{2,10},{3,11},{4,12},{5,13},{6,14},{7,15},{8,0},{9,1},... | collective-permute-start | bytes 2764808 | tf_op jit(solution)/shard_map/ppermute | solution.py:257
  42.6 0.0 collective-permute-done.5.refs_3_
  42.6 0.0 collective-permute-start.6
  42.6 0.0 collective-permute-done.7.refs_5_
  42.6 0.5 collective-permute-start.8
  43.1 0.0 collective-permute-done.4.refs_2_
  43.2 0.1 collective-permute-start.15
  43.2 10.1 %collective-permute-done.16.refs_3_ = bf16[9,80,640]{2,1,0:T(8,128)(2,1)S(1)} collective-permute-done((bf16[9,80,640]{2,1,0:T(8,128)(2,1)}, bf16[9,80,640]{2,1,0:T(8,128)(2,1)S(1)}, u32[]{:S(2)}, u32[]{:S(2)}) %collective-permute-start.16) | collective-permute-done | bytes 921632 | tf_op jit(solution)/shard_map/ppermute | solution.py:257
  53.3 0.0 collective-permute-start.17
  53.3 10.1 %collective-permute-done.18.refs_5_ = bf16[9,80,640]{2,1,0:T(8,128)(2,1)S(1)} collective-permute-done((bf16[9,80,640]{2,1,0:T(8,128)(2,1)}, bf16[9,80,640]{2,1,0:T(8,128)(2,1)S(1)}, u32[]{:S(2)}, u32[]{:S(2)}) %collective-permute-start.18) | collective-permute-done | bytes 921632 | tf_op jit(solution)/shard_map/ppermute | solution.py:257
  63.4 0.0 collective-permute-start.19
  63.4 0.0 copy-done.5
  63.4 3.0 %shard_map.78 = (bf16[4,2,128,1920]{3,2,1,0:T(8,128)(2,1)S(1)}, f32[8,640]{1,0:T(8,128)S(1)}) custom-call(bf16[4,128,640]{2,1,0:T(8,128)(2,1)S(1)} %bitcast.21, bf16[4,128,640]{2,1,0:T(8,128)(2,1)S(1)} %bitcast.24, bf16[16,640]{1,0:T(8,128)(2,1)S(1)} %get-tuple-element.21.refs_2_, bf16[16,640]{1,0:T(8,128)(2,1)S(1)} %collective-permute-done.refs_3_, ...), custom_call_target="tpu_custom_call" | custom-call | flops 629145600 | tf_op jit(solution)/shard_map/pallas_call | solution.py:228
  66.4 0.0 collective-permute-done.6.refs_4_
  66.4 0.9 collective-permute-start.10
  67.3 0.0 collective-permute-done.8.refs_6_
  67.3 4.5 %collective-permute-start.9 = (bf16[2,128,640]{2,1,0:T(8,128)(2,1)S(1)}, bf16[2,128,640]{2,1,0:T(8,128)(2,1)S(1)}, u32[]{:S(2)}, u32[]{:S(2)}) collective-permute-start(bf16[2,128,640]{2,1,0:T(8,128)(2,1)S(1)} %get-tuple-element.26), channel_id=1, source_target_pairs={{0,1},{1,0},{2,3},{3,2},{4,5},{5,4},{6,7},{7,6},{8,9},{9,8},{10,11... | collective-permute-start | bytes 983048 | tf_op jit(solution)/shard_map/ppermute | solution.py:257
  71.8 0.0 copy-done.2
  71.8 10.4 %shard_map.79 = (f32[4,2,128,640]{3,2,1,0:T(8,128)S(1)}, bf16[640,1920]{1,0:T(8,128)(2,1)S(1)}, bf16[640,1920]{1,0:T(8,128)(2,1)S(1)}) custom-call(s32[10]{0:T(128)S(1)} %stack.51.info, bf16[4,2,128,1920]{3,2,1,0:T(8,128)(2,1)S(1)} %get-tuple-element.22.xs, bf16[9,160,640]{2,1,0:T(8,128)(2,1)S(1)} %bitcast.26, ...), custom_call_target="tpu_custom_call" | custom-call | flops 5033164800 | tf_op jit(solution)/shard_map/pallas_call | solution.py:228
  82.1 0.0 collective-permute-done.10.hd
  82.1 4.5 %collective-permute-done.9.hx = bf16[2,128,640]{2,1,0:T(8,128)(2,1)S(1)} collective-permute-done((bf16[2,128,640]{2,1,0:T(8,128)(2,1)S(1)}, bf16[2,128,640]{2,1,0:T(8,128)(2,1)S(1)}, u32[]{:S(2)}, u32[]{:S(2)}) %collective-permute-start.9) | collective-permute-done | bytes 327712 | tf_op jit(solution)/shard_map/ppermute | solution.py:257
  86.6 3.1 %shard_map.80 = (bf16[4,2,128,640]{3,2,1,0:T(8,128)(2,1)S(1)}, bf16[16,640]{1,0:T(8,128)(2,1)S(1)}, bf16[2,128,640]{2,1,0:T(8,128)(2,1)S(1)}, bf16[2,128,640]{2,1,0:T(8,128)(2,1)S(1)}) custom-call(s32[10]{0:T(128)S(1)} %stack.51.info, f32[4,2,128,640]{3,2,1,0:T(8,128)S(1)} %get-tuple-element.23.acc_in, bf16[640,1920]{1,0:T(8,128)(2,1)S(1)} %get-tuple-element.24.w0, ...), custom_call_target="tpu_custom_call" | custom-call | flops 2516582400 | tf_op jit(solution)/shard_map/pallas_call | solution.py:228
  89.7 0.1 collective-permute-start.11
  89.8 2.0 %collective-permute-start.12 = (bf16[16,640]{1,0:T(8,128)(2,1)S(1)}, bf16[16,640]{1,0:T(8,128)(2,1)S(1)}, u32[]{:S(2)}, u32[]{:S(2)}) collective-permute-start(bf16[16,640]{1,0:T(8,128)(2,1)S(1)} %get-tuple-element.30.refs_1_), channel_id=1, source_target_pairs={{0,2},{1,3},{2,0},{3,1},{4,6},{5,7},{6,4},{7,5},{8,10},{9,11},{10,... | collective-permute-start | bytes 61448 | tf_op jit(solution)/shard_map/ppermute | solution.py:257
  91.8 1.8 %collective-permute-done.11.refs_2_ = bf16[16,640]{1,0:T(8,128)(2,1)S(1)} collective-permute-done((bf16[16,640]{1,0:T(8,128)(2,1)S(1)}, bf16[16,640]{1,0:T(8,128)(2,1)S(1)}, u32[]{:S(2)}, u32[]{:S(2)}) %collective-permute-start.11) | collective-permute-done | bytes 20512 | tf_op jit(solution)/shard_map/ppermute | solution.py:257
  93.6 1.4 %collective-permute-start.13 = (bf16[16,640]{1,0:T(8,128)(2,1)S(1)}, bf16[16,640]{1,0:T(8,128)(2,1)S(1)}, u32[]{:S(2)}, u32[]{:S(2)}) collective-permute-start(bf16[16,640]{1,0:T(8,128)(2,1)S(1)} %get-tuple-element.30.refs_1_), channel_id=1, source_target_pairs={{0,3},{1,2},{2,1},{3,0},{4,7},{5,6},{6,5},{7,4},{8,11},{9,10},{10,... | collective-permute-start | bytes 61448 | tf_op jit(solution)/shard_map/ppermute | solution.py:257
  95.0 0.0 copy-done.6
  95.0 0.0 collective-permute-done.12.refs_3_
  95.0 0.6 collective-permute-start.20
  95.6 2.9 %collective-permute-done.13.refs_4_ = bf16[16,640]{1,0:T(8,128)(2,1)S(1)} collective-permute-done((bf16[16,640]{1,0:T(8,128)(2,1)S(1)}, bf16[16,640]{1,0:T(8,128)(2,1)S(1)}, u32[]{:S(2)}, u32[]{:S(2)}) %collective-permute-start.13) | collective-permute-done | bytes 20512 | tf_op jit(solution)/shard_map/ppermute | solution.py:257
  98.5 0.9 collective-permute-start.21
  99.4 3.0 %shard_map.81 = (bf16[4,2,128,1920]{3,2,1,0:T(8,128)(2,1)S(1)}, f32[8,640]{1,0:T(8,128)S(1)}) custom-call(bf16[4,2,128,640]{3,2,1,0:T(8,128)(2,1)S(1)} %get-tuple-element.29.refs_0_, bf16[16,640]{1,0:T(8,128)(2,1)S(1)} %get-tuple-element.30.refs_1_, bf16[16,640]{1,0:T(8,128)(2,1)S(1)} %collective-permute-done.11.refs_2_, ...), custom_call_target="tpu_custom_call" | custom-call | flops 629145600 | tf_op jit(solution)/shard_map/pallas_call | solution.py:228
  102.4 0.0 collective-permute-done.15.refs_2_
  102.4 0.0 collective-permute-done.17.refs_4_
  102.4 0.0 collective-permute-done.19.refs_6_
  102.4 9.8 %shard_map.82 = (f32[4,2,128,640]{3,2,1,0:T(8,128)S(1)}, bf16[640,1920]{1,0:T(8,128)(2,1)S(1)}, bf16[640,1920]{1,0:T(8,128)(2,1)S(1)}) custom-call(s32[10]{0:T(128)S(1)} %stack.51.info, bf16[4,2,128,1920]{3,2,1,0:T(8,128)(2,1)S(1)} %get-tuple-element.31.xs, bf16[9,160,640]{2,1,0:T(8,128)(2,1)S(1)} %bitcast.27, ...), custom_call_target="tpu_custom_call" | custom-call | flops 5033164800 | tf_op jit(solution)/shard_map/pallas_call | solution.py:228
  112.2 0.0 collective-permute-done.20.hx
  112.2 0.0 collective-permute-done.21.hd
  112.2 3.9 %shard_map.83 = (bf16[4,128,640]{2,1,0:T(8,128)(2,1)}, bf16[4,128,640]{2,1,0:T(8,128)(2,1)}) custom-call(s32[10]{0:T(128)S(1)} %stack.51.info, f32[4,2,128,640]{3,2,1,0:T(8,128)S(1)} %get-tuple-element.32.acc_in, bf16[640,1920]{1,0:T(8,128)(2,1)S(1)} %get-tuple-element.33.w0, bf16[640,1920]{1,0:T(8,128)(2,1)S(1)} %get-tuple-element.34.w2, ...), custom_call_target="tpu_custom_call" | custom-call | flops 2516582400 | tf_op jit(solution)/shard_map/pallas_call | solution.py:228
  (6 shorter events, 0.0 us)
Async XLA Ops:
  0.6 4.5 %copy-start.3 = (bf16[9,640,160]{1,2,0:T(8,128)(2,1)S(1)}, bf16[9,640,160]{1,2,0:T(8,128)(2,1)}, u32[]{:S(2)}) copy-start(bf16[9,640,160]{1,2,0:T(8,128)(2,1)} %param.11) | copy-start | bytes 5529604
  0.6 19.7 %copy-start = (bf16[1,4,128,640]{3,2,1,0:T(8,128)(2,1)S(1)}, bf16[1,4,128,640]{3,2,1,0:T(8,128)(2,1)}, u32[]{:S(2)}) copy-start(bf16[1,4,128,640]{3,2,1,0:T(8,128)(2,1)} %param.6) | copy-start | bytes 1966084
  0.7 19.7 %copy-start.1 = (bf16[1,4,128,640]{3,2,1,0:T(8,128)(2,1)S(1)}, bf16[1,4,128,640]{3,2,1,0:T(8,128)(2,1)}, u32[]{:S(2)}) copy-start(bf16[1,4,128,640]{3,2,1,0:T(8,128)(2,1)} %param.7) | copy-start | bytes 1966084
  2.1 61.3 %copy-start.5 = (f32[640]{0:T(1024)S(1)}, f32[640]{0:T(1024)}, u32[]{:S(2)}) copy-start(f32[640]{0:T(1024)} %param.8) | copy-start | bytes 7684
  2.1 14.6 %collective-permute-start.3 = (bf16[9,80,640]{2,1,0:T(8,128)(2,1)S(1)}, bf16[9,80,640]{2,1,0:T(8,128)(2,1)}, u32[]{:S(2)}, u32[]{:S(2)}) collective-permute-start(bf16[9,80,640]{2,1,0:T(8,128)(2,1)S(1)} %dynamic-slice_bitcast_fusion.1), channel_id=1, source_target_pairs={{0,1},{1,0},{2,3},{3,2},{4,6},{5,7},{6,4},{7,5},{8,10},{9,11},{10,... | collective-permute-start | bytes 2764808 | tf_op jit(solution)/shard_map/ppermute | solution.py:257
  6.2 65.6 %copy-start.2 = (bf16[9,640,160]{1,2,0:T(8,128)(2,1)S(1)}, bf16[9,640,160]{1,2,0:T(8,128)(2,1)}, u32[]{:S(2)}) copy-start(bf16[9,640,160]{1,2,0:T(8,128)(2,1)} %param.9) | copy-start | bytes 5529604
  6.2 33.5 %collective-permute-start.14 = (bf16[9,80,640]{2,1,0:T(8,128)(2,1)}, bf16[9,80,640]{2,1,0:T(8,128)(2,1)}, u32[]{:S(2)}, u32[]{:S(2)}) collective-permute-start(bf16[9,80,640]{2,1,0:T(8,128)(2,1)} %dynamic-slice_bitcast_fusion), channel_id=1, source_target_pairs={{0,1},{1,0},{2,3},{3,2},{4,6},{5,7},{6,4},{7,5},{8,10},{9,11},{10,... | collective-permute-start | bytes 2764808 | tf_op jit(solution)/shard_map/ppermute | solution.py:257
  16.7 26.0 %collective-permute-start.5 = (bf16[9,80,640]{2,1,0:T(8,128)(2,1)}, bf16[9,80,640]{2,1,0:T(8,128)(2,1)}, u32[]{:S(2)}, u32[]{:S(2)}) collective-permute-start(bf16[9,80,640]{2,1,0:T(8,128)(2,1)} %collective-permute-done.3.refs_1_), channel_id=1, source_target_pairs={{0,2},{1,3},{2,0},{3,1},{4,5},{5,4},{6,7},{7,6},{8,9},{9,8},{10,11... | collective-permute-start | bytes 2764808 | tf_op jit(solution)/shard_map/ppermute | solution.py:257
  18.7 23.9 %collective-permute-start.7 = (bf16[9,80,640]{2,1,0:T(8,128)(2,1)}, bf16[9,80,640]{2,1,0:T(8,128)(2,1)}, u32[]{:S(2)}, u32[]{:S(2)}) collective-permute-start(bf16[9,80,640]{2,1,0:T(8,128)(2,1)} %collective-permute-done.3.refs_1_), channel_id=1, source_target_pairs={{0,8},{1,9},{2,10},{3,11},{4,12},{5,13},{6,14},{7,15},{8,0},{9,1},... | collective-permute-start | bytes 2764808 | tf_op jit(solution)/shard_map/ppermute | solution.py:257
  21.7 12.9 %collective-permute-start = (bf16[16,640]{1,0:T(8,128)(2,1)S(1)}, bf16[16,640]{1,0:T(8,128)(2,1)S(1)}, u32[]{:S(2)}, u32[]{:S(2)}) collective-permute-start(bf16[16,640]{1,0:T(8,128)(2,1)S(1)} %get-tuple-element.21.refs_2_), channel_id=1, source_target_pairs={{0,1},{1,0},{2,3},{3,2},{4,5},{5,4},{6,7},{7,6},{8,9},{9,8},{10,11... | collective-permute-start | bytes 61448 | tf_op jit(solution)/shard_map/ppermute | solution.py:257
  22.3 15.6 %collective-permute-start.1 = (bf16[16,640]{1,0:T(8,128)(2,1)S(1)}, bf16[16,640]{1,0:T(8,128)(2,1)S(1)}, u32[]{:S(2)}, u32[]{:S(2)}) collective-permute-start(bf16[16,640]{1,0:T(8,128)(2,1)S(1)} %get-tuple-element.21.refs_2_), channel_id=1, source_target_pairs={{0,2},{1,3},{2,0},{3,1},{4,6},{5,7},{6,4},{7,5},{8,10},{9,11},{10,... | collective-permute-start | bytes 61448 | tf_op jit(solution)/shard_map/ppermute | solution.py:257
  34.6 5.6 %collective-permute-start.2 = (bf16[16,640]{1,0:T(8,128)(2,1)S(1)}, bf16[16,640]{1,0:T(8,128)(2,1)S(1)}, u32[]{:S(2)}, u32[]{:S(2)}) collective-permute-start(bf16[16,640]{1,0:T(8,128)(2,1)S(1)} %get-tuple-element.21.refs_2_), channel_id=1, source_target_pairs={{0,3},{1,2},{2,1},{3,0},{4,7},{5,6},{6,5},{7,4},{8,11},{9,10},{10,... | collective-permute-start | bytes 61448 | tf_op jit(solution)/shard_map/ppermute | solution.py:257
  37.8 5.3 %collective-permute-start.4 = (bf16[9,80,640]{2,1,0:T(8,128)(2,1)}, bf16[9,80,640]{2,1,0:T(8,128)(2,1)S(1)}, u32[]{:S(2)}, u32[]{:S(2)}) collective-permute-start(bf16[9,80,640]{2,1,0:T(8,128)(2,1)} %collective-permute-done.3.refs_1_), channel_id=1, source_target_pairs={{0,4},{1,5},{2,6},{3,7},{4,0},{5,1},{6,2},{7,3},{8,12},{9,13},{10,... | collective-permute-start | bytes 2764808 | tf_op jit(solution)/shard_map/ppermute | solution.py:257
  39.7 13.6 %collective-permute-start.16 = (bf16[9,80,640]{2,1,0:T(8,128)(2,1)}, bf16[9,80,640]{2,1,0:T(8,128)(2,1)S(1)}, u32[]{:S(2)}, u32[]{:S(2)}) collective-permute-start(bf16[9,80,640]{2,1,0:T(8,128)(2,1)} %collective-permute-done.14.refs_1_), channel_id=1, source_target_pairs={{0,2},{1,3},{2,0},{3,1},{4,5},{5,4},{6,7},{7,6},{8,9},{9,8},{10,11... | collective-permute-start | bytes 2764808 | tf_op jit(solution)/shard_map/ppermute | solution.py:257
  40.2 23.2 %collective-permute-start.18 = (bf16[9,80,640]{2,1,0:T(8,128)(2,1)}, bf16[9,80,640]{2,1,0:T(8,128)(2,1)S(1)}, u32[]{:S(2)}, u32[]{:S(2)}) collective-permute-start(bf16[9,80,640]{2,1,0:T(8,128)(2,1)} %collective-permute-done.14.refs_1_), channel_id=1, source_target_pairs={{0,8},{1,9},{2,10},{3,11},{4,12},{5,13},{6,14},{7,15},{8,0},{9,1},... | collective-permute-start | bytes 2764808 | tf_op jit(solution)/shard_map/ppermute | solution.py:257
  42.6 23.8 %collective-permute-start.6 = (bf16[9,80,640]{2,1,0:T(8,128)(2,1)}, bf16[9,80,640]{2,1,0:T(8,128)(2,1)S(1)}, u32[]{:S(2)}, u32[]{:S(2)}) collective-permute-start(bf16[9,80,640]{2,1,0:T(8,128)(2,1)} %collective-permute-done.5.refs_3_), channel_id=1, source_target_pairs={{0,4},{1,5},{2,6},{3,7},{4,0},{5,1},{6,2},{7,3},{8,12},{9,13},{10,... | collective-permute-start | bytes 2764808 | tf_op jit(solution)/shard_map/ppermute | solution.py:257
  42.6 24.6 %collective-permute-start.8 = (bf16[9,80,640]{2,1,0:T(8,128)(2,1)}, bf16[9,80,640]{2,1,0:T(8,128)(2,1)S(1)}, u32[]{:S(2)}, u32[]{:S(2)}) collective-permute-start(bf16[9,80,640]{2,1,0:T(8,128)(2,1)} %collective-permute-done.7.refs_5_), channel_id=1, source_target_pairs={{0,4},{1,5},{2,6},{3,7},{4,0},{5,1},{6,2},{7,3},{8,12},{9,13},{10,... | collective-permute-start | bytes 2764808 | tf_op jit(solution)/shard_map/ppermute | solution.py:257
  43.2 59.2 %collective-permute-start.15 = (bf16[9,80,640]{2,1,0:T(8,128)(2,1)}, bf16[9,80,640]{2,1,0:T(8,128)(2,1)S(1)}, u32[]{:S(2)}, u32[]{:S(2)}) collective-permute-start(bf16[9,80,640]{2,1,0:T(8,128)(2,1)} %collective-permute-done.14.refs_1_), channel_id=1, source_target_pairs={{0,4},{1,5},{2,6},{3,7},{4,0},{5,1},{6,2},{7,3},{8,12},{9,13},{10,... | collective-permute-start | bytes 2764808 | tf_op jit(solution)/shard_map/ppermute | solution.py:257
  53.3 49.1 %collective-permute-start.17 = (bf16[9,80,640]{2,1,0:T(8,128)(2,1)S(1)}, bf16[9,80,640]{2,1,0:T(8,128)(2,1)S(1)}, u32[]{:S(2)}, u32[]{:S(2)}) collective-permute-start(bf16[9,80,640]{2,1,0:T(8,128)(2,1)S(1)} %collective-permute-done.16.refs_3_), channel_id=1, source_target_pairs={{0,4},{1,5},{2,6},{3,7},{4,0},{5,1},{6,2},{7,3},{8,12},{9,13},{10,... | collective-permute-start | bytes 2764808 | tf_op jit(solution)/shard_map/ppermute | solution.py:257
  63.4 39.0 %collective-permute-start.19 = (bf16[9,80,640]{2,1,0:T(8,128)(2,1)S(1)}, bf16[9,80,640]{2,1,0:T(8,128)(2,1)S(1)}, u32[]{:S(2)}, u32[]{:S(2)}) collective-permute-start(bf16[9,80,640]{2,1,0:T(8,128)(2,1)S(1)} %collective-permute-done.18.refs_5_), channel_id=1, source_target_pairs={{0,4},{1,5},{2,6},{3,7},{4,0},{5,1},{6,2},{7,3},{8,12},{9,13},{10,... | collective-permute-start | bytes 2764808 | tf_op jit(solution)/shard_map/ppermute | solution.py:257
  66.4 15.7 %collective-permute-start.10 = (bf16[2,128,640]{2,1,0:T(8,128)(2,1)S(1)}, bf16[2,128,640]{2,1,0:T(8,128)(2,1)S(1)}, u32[]{:S(2)}, u32[]{:S(2)}) collective-permute-start(bf16[2,128,640]{2,1,0:T(8,128)(2,1)S(1)} %get-tuple-element.27), channel_id=1, source_target_pairs={{1,2},{2,1},{5,6},{6,5},{9,10},{10,9},{13,14},{14,13},{17,18},{18,... | collective-permute-start | bytes 983048 | tf_op jit(solution)/shard_map/ppermute | solution.py:257
  67.3 19.3 %collective-permute-start.9 = (bf16[2,128,640]{2,1,0:T(8,128)(2,1)S(1)}, bf16[2,128,640]{2,1,0:T(8,128)(2,1)S(1)}, u32[]{:S(2)}, u32[]{:S(2)}) collective-permute-start(bf16[2,128,640]{2,1,0:T(8,128)(2,1)S(1)} %get-tuple-element.26), channel_id=1, source_target_pairs={{0,1},{1,0},{2,3},{3,2},{4,5},{5,4},{6,7},{7,6},{8,9},{9,8},{10,11... | collective-permute-start | bytes 983048 | tf_op jit(solution)/shard_map/ppermute | solution.py:257
  86.6 8.4 %copy-start.6 = (f32[640]{0:T(1024)S(1)}, f32[640]{0:T(1024)}, u32[]{:S(2)}) copy-start(f32[640]{0:T(1024)} %param.10) | copy-start | bytes 7684
  86.6 15.8 %copy-start.4 = (bf16[9,640,160]{1,2,0:T(8,128)(2,1)S(1)}, bf16[9,640,160]{1,2,0:T(8,128)(2,1)}, u32[]{:S(2)}) copy-start(bf16[9,640,160]{1,2,0:T(8,128)(2,1)} %param.11) | copy-start | bytes 5529604
  89.7 3.8 %collective-permute-start.11 = (bf16[16,640]{1,0:T(8,128)(2,1)S(1)}, bf16[16,640]{1,0:T(8,128)(2,1)S(1)}, u32[]{:S(2)}, u32[]{:S(2)}) collective-permute-start(bf16[16,640]{1,0:T(8,128)(2,1)S(1)} %get-tuple-element.30.refs_1_), channel_id=1, source_target_pairs={{0,1},{1,0},{2,3},{3,2},{4,5},{5,4},{6,7},{7,6},{8,9},{9,8},{10,11... | collective-permute-start | bytes 61448 | tf_op jit(solution)/shard_map/ppermute | solution.py:257
  89.8 5.2 %collective-permute-start.12 = (bf16[16,640]{1,0:T(8,128)(2,1)S(1)}, bf16[16,640]{1,0:T(8,128)(2,1)S(1)}, u32[]{:S(2)}, u32[]{:S(2)}) collective-permute-start(bf16[16,640]{1,0:T(8,128)(2,1)S(1)} %get-tuple-element.30.refs_1_), channel_id=1, source_target_pairs={{0,2},{1,3},{2,0},{3,1},{4,6},{5,7},{6,4},{7,5},{8,10},{9,11},{10,... | collective-permute-start | bytes 61448 | tf_op jit(solution)/shard_map/ppermute | solution.py:257
  93.6 4.9 %collective-permute-start.13 = (bf16[16,640]{1,0:T(8,128)(2,1)S(1)}, bf16[16,640]{1,0:T(8,128)(2,1)S(1)}, u32[]{:S(2)}, u32[]{:S(2)}) collective-permute-start(bf16[16,640]{1,0:T(8,128)(2,1)S(1)} %get-tuple-element.30.refs_1_), channel_id=1, source_target_pairs={{0,3},{1,2},{2,1},{3,0},{4,7},{5,6},{6,5},{7,4},{8,11},{9,10},{10,... | collective-permute-start | bytes 61448 | tf_op jit(solution)/shard_map/ppermute | solution.py:257
  95.0 17.2 %collective-permute-start.20 = (bf16[2,128,640]{2,1,0:T(8,128)(2,1)S(1)}, bf16[2,128,640]{2,1,0:T(8,128)(2,1)S(1)}, u32[]{:S(2)}, u32[]{:S(2)}) collective-permute-start(bf16[2,128,640]{2,1,0:T(8,128)(2,1)S(1)} %get-tuple-element.35), channel_id=1, source_target_pairs={{0,1},{1,0},{2,3},{3,2},{4,5},{5,4},{6,7},{7,6},{8,9},{9,8},{10,11... | collective-permute-start | bytes 983048 | tf_op jit(solution)/shard_map/ppermute | solution.py:257
  98.5 13.7 %collective-permute-start.21 = (bf16[2,128,640]{2,1,0:T(8,128)(2,1)S(1)}, bf16[2,128,640]{2,1,0:T(8,128)(2,1)S(1)}, u32[]{:S(2)}, u32[]{:S(2)}) collective-permute-start(bf16[2,128,640]{2,1,0:T(8,128)(2,1)S(1)} %get-tuple-element.36), channel_id=1, source_target_pairs={{1,2},{2,1},{5,6},{6,5},{9,10},{10,9},{13,14},{14,13},{17,18},{18,... | collective-permute-start | bytes 983048 | tf_op jit(solution)/shard_map/ppermute | solution.py:257
where the time goes:
time: 116 us
  waiting for transfers between devices  50.4 us (43%)
  Pallas kernels  34.4 us (30%)
  starting transfers between devices  27.9 us (24%)
  local copies, waits for them, and re-layouts  2.56 us (2%)
    ppermute x22, waiting for transfers between devices, permute(): return lax.ppermute(x, AXES, pairs)  50.4 us
    pallas_call x7, Pallas kernels, call(): pl.pallas_call(kernel, out_shape=tuple((jax.ShapeDtypeStruct(s, d) for s,...  34.4 us
    ppermute x22, starting transfers between devices, permute(): return lax.ppermute(x, AXES, pairs)  27.9 us
    dynamic_slice x2, local copies, waits for them, and re-layouts, gather(): part = lax.dynamic_slice_in_dim(w, half * core, half, axis=1)  2.43 us
  transfers between devices with their start and end apart: 22, of which 7 were waited for; matrix products, arithmetic and copies ran while one was open for 1% of the time, Pallas kernels for 26%

commit v1 on v0

--- a/solution.py
+++ b/solution.py
@@ -14,7 +14,7 @@
 BF = jnp.bfloat16
 F32 = jnp.float32
 STAT_ROWS = 16
-VMEM_LIMIT = 32 * 1024 * 1024
+VMEM_LIMIT = 18 * 1024 * 1024
 
 
 def split3(x):
@@ -62,9 +62,9 @@
 
 
 def group_sum(rows, matrix):
-    hi, mid, low = split3(rows)
-    dot = functools.partial(jnp.dot, preferred_element_type=F32)
-    return dot(hi, matrix) + (dot(mid, matrix) + dot(low, matrix))
+    parts = jnp.concatenate([p.astype(F32) for p in split3(rows)] + [jnp.zeros_like(rows)], 0).astype(BF)
+    sums = jnp.dot(parts, matrix, preferred_element_type=F32)
+    return sums[0:8] + (sums[8:16] + sums[16:24])
 
 
 def coefficients(stats, gain, count, total):

time: 116 us -> 116 us (level)
  no operation moved by 1% of the time
where the time goes in v1:
time: 116 us; the launch traced here: 115 us
  waiting for transfers between devices  50.4 us (43%)
  Pallas kernels  33.6 us (29%)
  starting transfers between devices  27.9 us (24%)
  local copies, waits for them, and re-layouts  2.56 us (2%)
    ppermute x22, waiting for transfers between devices, permute(): return lax.ppermute(x, AXES, pairs)  50.4 us
    pallas_call x7, Pallas kernels, call(): pl.pallas_call(kernel, out_shape=tuple((jax.ShapeDtypeStruct(s, d) for s,...  33.6 us
    ppermute x22, starting transfers between devices, permute(): return lax.ppermute(x, AXES, pairs)  27.9 us
    dynamic_slice x2, local copies, waits for them, and re-layouts, gather(): part = lax.dynamic_slice_in_dim(w, half * core, half, axis=1)  2.43 us
  transfers between devices with their start and end apart: 22, of which 7 were waited for; matrix products, arithmetic and copies ran while one was open for 1% of the time, Pallas kernels for 26%

profile of v1, /device:TPU:0, one launch (start us, length us, event | category | flops | bytes accessed | tf_op | source)
XLA Modules:
  0.0 115.3 jit_solution(10573237287701665972)
XLA Ops:
  0.6 0.0 copy-start.3
  0.6 0.0 copy-start
  0.7 0.0 copy-start.1
  0.7 1.4 %dynamic-slice_bitcast_fusion.1 = bf16[9,80,640]{2,1,0:T(8,128)(2,1)S(1)} fusion(bf16[9,640,160]{1,2,0:T(8,128)(2,1)} %param.9, s32[]{:T(128)S(6)} %select_n.27), kind=kLoop, calls=%fused_computation.1 | loop fusion | bytes 1843204 | tf_op jit(solution)/shard_map/dynamic_slice | solution.py:265
  2.1 0.0 copy-start.5
  2.1 3.0 %collective-permute-start.3 = (bf16[9,80,640]{2,1,0:T(8,128)(2,1)S(1)}, bf16[9,80,640]{2,1,0:T(8,128)(2,1)}, u32[]{:S(2)}, u32[]{:S(2)}) collective-permute-start(bf16[9,80,640]{2,1,0:T(8,128)(2,1)S(1)} %dynamic-slice_bitcast_fusion.1), channel_id=1, source_target_pairs={{0,1},{1,0},{2,3},{3,2},{4,6},{5,7},{6,4},{7,5},{8,10},{9,11},{10,... | collective-permute-start | bytes 2764808 | tf_op jit(solution)/shard_map/ppermute | solution.py:257
  5.2 0.0 copy-done.3
  5.2 1.0 dynamic-slice_bitcast_fusion
  6.2 0.2 collective-permute-start.14
  6.4 10.3 %collective-permute-done.3.refs_1_ = bf16[9,80,640]{2,1,0:T(8,128)(2,1)} collective-permute-done((bf16[9,80,640]{2,1,0:T(8,128)(2,1)S(1)}, bf16[9,80,640]{2,1,0:T(8,128)(2,1)}, u32[]{:S(2)}, u32[]{:S(2)}) %collective-permute-start.3) | collective-permute-done | bytes 921632 | tf_op jit(solution)/shard_map/ppermute | solution.py:257
  16.7 2.0 %collective-permute-start.5 = (bf16[9,80,640]{2,1,0:T(8,128)(2,1)}, bf16[9,80,640]{2,1,0:T(8,128)(2,1)}, u32[]{:S(2)}, u32[]{:S(2)}) collective-permute-start(bf16[9,80,640]{2,1,0:T(8,128)(2,1)} %collective-permute-done.3.refs_1_), channel_id=1, source_target_pairs={{0,2},{1,3},{2,0},{3,1},{4,5},{5,4},{6,7},{7,6},{8,9},{9,8},{10,11... | collective-permute-start | bytes 2764808 | tf_op jit(solution)/shard_map/ppermute | solution.py:257
  18.7 1.5 %collective-permute-start.7 = (bf16[9,80,640]{2,1,0:T(8,128)(2,1)}, bf16[9,80,640]{2,1,0:T(8,128)(2,1)}, u32[]{:S(2)}, u32[]{:S(2)}) collective-permute-start(bf16[9,80,640]{2,1,0:T(8,128)(2,1)} %collective-permute-done.3.refs_1_), channel_id=1, source_target_pairs={{0,8},{1,9},{2,10},{3,11},{4,12},{5,13},{6,14},{7,15},{8,0},{9,1},... | collective-permute-start | bytes 2764808 | tf_op jit(solution)/shard_map/ppermute | solution.py:257
  20.3 0.1 stack.51.info
  20.4 0.0 copy-done
  20.4 0.0 copy-done.1
  20.4 1.3 %shard_map.77 = (bf16[16,640]{1,0:T(8,128)(2,1)S(1)}, bf16[2,128,640]{2,1,0:T(8,128)(2,1)S(1)}, bf16[2,128,640]{2,1,0:T(8,128)(2,1)S(1)}) custom-call(s32[10]{0:T(128)S(1)} %stack.51.info, bf16[4,128,640]{2,1,0:T(8,128)(2,1)S(1)} %bitcast.20, bf16[4,128,640]{2,1,0:T(8,128)(2,1)S(1)} %bitcast.23), custom_call_target="tpu_custom_call" | custom-call | flops 629145600 | tf_op jit(solution)/shard_map/pallas_call | solution.py:228
  21.7 0.6 collective-permute-start
  22.3 1.5 %collective-permute-start.1 = (bf16[16,640]{1,0:T(8,128)(2,1)S(1)}, bf16[16,640]{1,0:T(8,128)(2,1)S(1)}, u32[]{:S(2)}, u32[]{:S(2)}) collective-permute-start(bf16[16,640]{1,0:T(8,128)(2,1)S(1)} %get-tuple-element.21.refs_2_), channel_id=1, source_target_pairs={{0,2},{1,3},{2,0},{3,1},{4,6},{5,7},{6,4},{7,5},{8,10},{9,11},{10,... | collective-permute-start | bytes 61448 | tf_op jit(solution)/shard_map/ppermute | solution.py:257
  23.8 10.8 %collective-permute-done.refs_3_ = bf16[16,640]{1,0:T(8,128)(2,1)S(1)} collective-permute-done((bf16[16,640]{1,0:T(8,128)(2,1)S(1)}, bf16[16,640]{1,0:T(8,128)(2,1)S(1)}, u32[]{:S(2)}, u32[]{:S(2)}) %collective-permute-start) | collective-permute-done | bytes 20512 | tf_op jit(solution)/shard_map/ppermute | solution.py:257
  34.6 3.3 %collective-permute-start.2 = (bf16[16,640]{1,0:T(8,128)(2,1)S(1)}, bf16[16,640]{1,0:T(8,128)(2,1)S(1)}, u32[]{:S(2)}, u32[]{:S(2)}) collective-permute-start(bf16[16,640]{1,0:T(8,128)(2,1)S(1)} %get-tuple-element.21.refs_2_), channel_id=1, source_target_pairs={{0,3},{1,2},{2,1},{3,0},{4,7},{5,6},{6,5},{7,4},{8,11},{9,10},{10,... | collective-permute-start | bytes 61448 | tf_op jit(solution)/shard_map/ppermute | solution.py:257
  37.8 0.0 collective-permute-done.1.refs_4_
  37.8 1.8 %collective-permute-start.4 = (bf16[9,80,640]{2,1,0:T(8,128)(2,1)}, bf16[9,80,640]{2,1,0:T(8,128)(2,1)S(1)}, u32[]{:S(2)}, u32[]{:S(2)}) collective-permute-start(bf16[9,80,640]{2,1,0:T(8,128)(2,1)} %collective-permute-done.3.refs_1_), channel_id=1, source_target_pairs={{0,4},{1,5},{2,6},{3,7},{4,0},{5,1},{6,2},{7,3},{8,12},{9,13},{10,... | collective-permute-start | bytes 2764808 | tf_op jit(solution)/shard_map/ppermute | solution.py:257
  39.7 0.0 collective-permute-done.14.refs_1_
  39.7 0.5 collective-permute-start.16
  40.2 0.0 collective-permute-done.2.refs_5_
  40.2 2.4 %collective-permute-start.18 = (bf16[9,80,640]{2,1,0:T(8,128)(2,1)}, bf16[9,80,640]{2,1,0:T(8,128)(2,1)S(1)}, u32[]{:S(2)}, u32[]{:S(2)}) collective-permute-start(bf16[9,80,640]{2,1,0:T(8,128)(2,1)} %collective-permute-done.14.refs_1_), channel_id=1, source_target_pairs={{0,8},{1,9},{2,10},{3,11},{4,12},{5,13},{6,14},{7,15},{8,0},{9,1},... | collective-permute-start | bytes 2764808 | tf_op jit(solution)/shard_map/ppermute | solution.py:257
  42.6 0.0 collective-permute-done.5.refs_3_
  42.6 0.0 collective-permute-start.6
  42.6 0.0 collective-permute-done.7.refs_5_
  42.6 0.5 collective-permute-start.8
  43.1 0.0 collective-permute-done.4.refs_2_
  43.2 0.1 collective-permute-start.15
  43.2 10.1 %collective-permute-done.16.refs_3_ = bf16[9,80,640]{2,1,0:T(8,128)(2,1)S(1)} collective-permute-done((bf16[9,80,640]{2,1,0:T(8,128)(2,1)}, bf16[9,80,640]{2,1,0:T(8,128)(2,1)S(1)}, u32[]{:S(2)}, u32[]{:S(2)}) %collective-permute-start.16) | collective-permute-done | bytes 921632 | tf_op jit(solution)/shard_map/ppermute | solution.py:257
  53.3 0.0 collective-permute-start.17
  53.3 10.1 %collective-permute-done.18.refs_5_ = bf16[9,80,640]{2,1,0:T(8,128)(2,1)S(1)} collective-permute-done((bf16[9,80,640]{2,1,0:T(8,128)(2,1)}, bf16[9,80,640]{2,1,0:T(8,128)(2,1)S(1)}, u32[]{:S(2)}, u32[]{:S(2)}) %collective-permute-start.18) | collective-permute-done | bytes 921632 | tf_op jit(solution)/shard_map/ppermute | solution.py:257
  63.4 0.0 collective-permute-start.19
  63.4 0.0 copy-done.5
  63.4 2.6 %shard_map.78 = (bf16[4,2,128,1920]{3,2,1,0:T(8,128)(2,1)S(1)}, f32[8,640]{1,0:T(8,128)S(1)}) custom-call(bf16[4,128,640]{2,1,0:T(8,128)(2,1)S(1)} %bitcast.21, bf16[4,128,640]{2,1,0:T(8,128)(2,1)S(1)} %bitcast.24, bf16[16,640]{1,0:T(8,128)(2,1)S(1)} %get-tuple-element.21.refs_2_, bf16[16,640]{1,0:T(8,128)(2,1)S(1)} %collective-permute-done.refs_3_, ...), custom_call_target="tpu_custom_call" | custom-call | flops 629145600 | tf_op jit(solution)/shard_map/pallas_call | solution.py:228
  66.0 0.0 collective-permute-done.6.refs_4_
  66.0 0.9 collective-permute-start.10
  66.9 0.0 collective-permute-done.8.refs_6_
  66.9 4.5 %collective-permute-start.9 = (bf16[2,128,640]{2,1,0:T(8,128)(2,1)S(1)}, bf16[2,128,640]{2,1,0:T(8,128)(2,1)S(1)}, u32[]{:S(2)}, u32[]{:S(2)}) collective-permute-start(bf16[2,128,640]{2,1,0:T(8,128)(2,1)S(1)} %get-tuple-element.26), channel_id=1, source_target_pairs={{0,1},{1,0},{2,3},{3,2},{4,5},{5,4},{6,7},{7,6},{8,9},{9,8},{10,11... | collective-permute-start | bytes 983048 | tf_op jit(solution)/shard_map/ppermute | solution.py:257
  71.4 0.0 copy-done.2
  71.4 10.4 %shard_map.79 = (f32[4,2,128,640]{3,2,1,0:T(8,128)S(1)}, bf16[640,1920]{1,0:T(8,128)(2,1)S(1)}, bf16[640,1920]{1,0:T(8,128)(2,1)S(1)}) custom-call(s32[10]{0:T(128)S(1)} %stack.51.info, bf16[4,2,128,1920]{3,2,1,0:T(8,128)(2,1)S(1)} %get-tuple-element.22.xs, bf16[9,160,640]{2,1,0:T(8,128)(2,1)S(1)} %bitcast.26, ...), custom_call_target="tpu_custom_call" | custom-call | flops 5033164800 | tf_op jit(solution)/shard_map/pallas_call | solution.py:228
  81.7 0.0 collective-permute-done.10.hd
  81.7 4.5 %collective-permute-done.9.hx = bf16[2,128,640]{2,1,0:T(8,128)(2,1)S(1)} collective-permute-done((bf16[2,128,640]{2,1,0:T(8,128)(2,1)S(1)}, bf16[2,128,640]{2,1,0:T(8,128)(2,1)S(1)}, u32[]{:S(2)}, u32[]{:S(2)}) %collective-permute-start.9) | collective-permute-done | bytes 327712 | tf_op jit(solution)/shard_map/ppermute | solution.py:257
  86.2 3.1 %shard_map.80 = (bf16[4,2,128,640]{3,2,1,0:T(8,128)(2,1)S(1)}, bf16[16,640]{1,0:T(8,128)(2,1)S(1)}, bf16[2,128,640]{2,1,0:T(8,128)(2,1)S(1)}, bf16[2,128,640]{2,1,0:T(8,128)(2,1)S(1)}) custom-call(s32[10]{0:T(128)S(1)} %stack.51.info, f32[4,2,128,640]{3,2,1,0:T(8,128)S(1)} %get-tuple-element.23.acc_in, bf16[640,1920]{1,0:T(8,128)(2,1)S(1)} %get-tuple-element.24.w0, ...), custom_call_target="tpu_custom_call" | custom-call | flops 2516582400 | tf_op jit(solution)/shard_map/pallas_call | solution.py:228
  89.4 0.1 collective-permute-start.11
  89.4 2.0 %collective-permute-start.12 = (bf16[16,640]{1,0:T(8,128)(2,1)S(1)}, bf16[16,640]{1,0:T(8,128)(2,1)S(1)}, u32[]{:S(2)}, u32[]{:S(2)}) collective-permute-start(bf16[16,640]{1,0:T(8,128)(2,1)S(1)} %get-tuple-element.30.refs_1_), channel_id=1, source_target_pairs={{0,2},{1,3},{2,0},{3,1},{4,6},{5,7},{6,4},{7,5},{8,10},{9,11},{10,... | collective-permute-start | bytes 61448 | tf_op jit(solution)/shard_map/ppermute | solution.py:257
  91.4 1.8 %collective-permute-done.11.refs_2_ = bf16[16,640]{1,0:T(8,128)(2,1)S(1)} collective-permute-done((bf16[16,640]{1,0:T(8,128)(2,1)S(1)}, bf16[16,640]{1,0:T(8,128)(2,1)S(1)}, u32[]{:S(2)}, u32[]{:S(2)}) %collective-permute-start.11) | collective-permute-done | bytes 20512 | tf_op jit(solution)/shard_map/ppermute | solution.py:257
  93.2 1.4 %collective-permute-start.13 = (bf16[16,640]{1,0:T(8,128)(2,1)S(1)}, bf16[16,640]{1,0:T(8,128)(2,1)S(1)}, u32[]{:S(2)}, u32[]{:S(2)}) collective-permute-start(bf16[16,640]{1,0:T(8,128)(2,1)S(1)} %get-tuple-element.30.refs_1_), channel_id=1, source_target_pairs={{0,3},{1,2},{2,1},{3,0},{4,7},{5,6},{6,5},{7,4},{8,11},{9,10},{10,... | collective-permute-start | bytes 61448 | tf_op jit(solution)/shard_map/ppermute | solution.py:257
  94.7 0.0 collective-permute-done.12.refs_3_
  94.7 0.6 collective-permute-start.20
  95.2 2.9 %collective-permute-done.13.refs_4_ = bf16[16,640]{1,0:T(8,128)(2,1)S(1)} collective-permute-done((bf16[16,640]{1,0:T(8,128)(2,1)S(1)}, bf16[16,640]{1,0:T(8,128)(2,1)S(1)}, u32[]{:S(2)}, u32[]{:S(2)}) %collective-permute-start.13) | collective-permute-done | bytes 20512 | tf_op jit(solution)/shard_map/ppermute | solution.py:257
  98.1 0.9 collective-permute-start.21
  99.0 2.6 %shard_map.81 = (bf16[4,2,128,1920]{3,2,1,0:T(8,128)(2,1)S(1)}, f32[8,640]{1,0:T(8,128)S(1)}) custom-call(bf16[4,2,128,640]{3,2,1,0:T(8,128)(2,1)S(1)} %get-tuple-element.29.refs_0_, bf16[16,640]{1,0:T(8,128)(2,1)S(1)} %get-tuple-element.30.refs_1_, bf16[16,640]{1,0:T(8,128)(2,1)S(1)} %collective-permute-done.11.refs_2_, ...), custom_call_target="tpu_custom_call" | custom-call | flops 629145600 | tf_op jit(solution)/shard_map/pallas_call | solution.py:228
  101.6 0.0 collective-permute-done.15.refs_2_
  101.6 0.0 collective-permute-done.17.refs_4_
  101.6 0.0 collective-permute-done.19.refs_6_
  101.6 0.0 copy-done.4
  101.7 9.8 %shard_map.82 = (f32[4,2,128,640]{3,2,1,0:T(8,128)S(1)}, bf16[640,1920]{1,0:T(8,128)(2,1)S(1)}, bf16[640,1920]{1,0:T(8,128)(2,1)S(1)}) custom-call(s32[10]{0:T(128)S(1)} %stack.51.info, bf16[4,2,128,1920]{3,2,1,0:T(8,128)(2,1)S(1)} %get-tuple-element.31.xs, bf16[9,160,640]{2,1,0:T(8,128)(2,1)S(1)} %bitcast.27, ...), custom_call_target="tpu_custom_call" | custom-call | flops 5033164800 | tf_op jit(solution)/shard_map/pallas_call | solution.py:228
  111.4 0.0 collective-permute-done.20.hx
  111.4 0.0 collective-permute-done.21.hd
  111.4 3.9 %shard_map.83 = (bf16[4,128,640]{2,1,0:T(8,128)(2,1)}, bf16[4,128,640]{2,1,0:T(8,128)(2,1)}) custom-call(s32[10]{0:T(128)S(1)} %stack.51.info, f32[4,2,128,640]{3,2,1,0:T(8,128)S(1)} %get-tuple-element.32.acc_in, bf16[640,1920]{1,0:T(8,128)(2,1)S(1)} %get-tuple-element.33.w0, bf16[640,1920]{1,0:T(8,128)(2,1)S(1)} %get-tuple-element.34.w2, ...), custom_call_target="tpu_custom_call" | custom-call | flops 2516582400 | tf_op jit(solution)/shard_map/pallas_call | solution.py:228
  (6 shorter events, 0.0 us)
Async XLA Ops:
  0.6 4.5 %copy-start.3 = (bf16[9,640,160]{1,2,0:T(8,128)(2,1)S(1)}, bf16[9,640,160]{1,2,0:T(8,128)(2,1)}, u32[]{:S(2)}) copy-start(bf16[9,640,160]{1,2,0:T(8,128)(2,1)} %param.11) | copy-start | bytes 5529604
  0.6 19.7 %copy-start = (bf16[1,4,128,640]{3,2,1,0:T(8,128)(2,1)S(1)}, bf16[1,4,128,640]{3,2,1,0:T(8,128)(2,1)}, u32[]{:S(2)}) copy-start(bf16[1,4,128,640]{3,2,1,0:T(8,128)(2,1)} %param.6) | copy-start | bytes 1966084
  0.7 19.7 %copy-start.1 = (bf16[1,4,128,640]{3,2,1,0:T(8,128)(2,1)S(1)}, bf16[1,4,128,640]{3,2,1,0:T(8,128)(2,1)}, u32[]{:S(2)}) copy-start(bf16[1,4,128,640]{3,2,1,0:T(8,128)(2,1)} %param.7) | copy-start | bytes 1966084
  2.1 61.3 %copy-start.5 = (f32[640]{0:T(1024)S(1)}, f32[640]{0:T(1024)}, u32[]{:S(2)}) copy-start(f32[640]{0:T(1024)} %param.8) | copy-start | bytes 7684
  2.1 14.6 %collective-permute-start.3 = (bf16[9,80,640]{2,1,0:T(8,128)(2,1)S(1)}, bf16[9,80,640]{2,1,0:T(8,128)(2,1)}, u32[]{:S(2)}, u32[]{:S(2)}) collective-permute-start(bf16[9,80,640]{2,1,0:T(8,128)(2,1)S(1)} %dynamic-slice_bitcast_fusion.1), channel_id=1, source_target_pairs={{0,1},{1,0},{2,3},{3,2},{4,6},{5,7},{6,4},{7,5},{8,10},{9,11},{10,... | collective-permute-start | bytes 2764808 | tf_op jit(solution)/shard_map/ppermute | solution.py:257
  6.2 65.2 %copy-start.2 = (bf16[9,640,160]{1,2,0:T(8,128)(2,1)S(1)}, bf16[9,640,160]{1,2,0:T(8,128)(2,1)}, u32[]{:S(2)}) copy-start(bf16[9,640,160]{1,2,0:T(8,128)(2,1)} %param.9) | copy-start | bytes 5529604
  6.2 33.5 %collective-permute-start.14 = (bf16[9,80,640]{2,1,0:T(8,128)(2,1)}, bf16[9,80,640]{2,1,0:T(8,128)(2,1)}, u32[]{:S(2)}, u32[]{:S(2)}) collective-permute-start(bf16[9,80,640]{2,1,0:T(8,128)(2,1)} %dynamic-slice_bitcast_fusion), channel_id=1, source_target_pairs={{0,1},{1,0},{2,3},{3,2},{4,6},{5,7},{6,4},{7,5},{8,10},{9,11},{10,... | collective-permute-start | bytes 2764808 | tf_op jit(solution)/shard_map/ppermute | solution.py:257
  16.7 26.0 %collective-permute-start.5 = (bf16[9,80,640]{2,1,0:T(8,128)(2,1)}, bf16[9,80,640]{2,1,0:T(8,128)(2,1)}, u32[]{:S(2)}, u32[]{:S(2)}) collective-permute-start(bf16[9,80,640]{2,1,0:T(8,128)(2,1)} %collective-permute-done.3.refs_1_), channel_id=1, source_target_pairs={{0,2},{1,3},{2,0},{3,1},{4,5},{5,4},{6,7},{7,6},{8,9},{9,8},{10,11... | collective-permute-start | bytes 2764808 | tf_op jit(solution)/shard_map/ppermute | solution.py:257
  18.7 23.9 %collective-permute-start.7 = (bf16[9,80,640]{2,1,0:T(8,128)(2,1)}, bf16[9,80,640]{2,1,0:T(8,128)(2,1)}, u32[]{:S(2)}, u32[]{:S(2)}) collective-permute-start(bf16[9,80,640]{2,1,0:T(8,128)(2,1)} %collective-permute-done.3.refs_1_), channel_id=1, source_target_pairs={{0,8},{1,9},{2,10},{3,11},{4,12},{5,13},{6,14},{7,15},{8,0},{9,1},... | collective-permute-start | bytes 2764808 | tf_op jit(solution)/shard_map/ppermute | solution.py:257
  21.7 12.9 %collective-permute-start = (bf16[16,640]{1,0:T(8,128)(2,1)S(1)}, bf16[16,640]{1,0:T(8,128)(2,1)S(1)}, u32[]{:S(2)}, u32[]{:S(2)}) collective-permute-start(bf16[16,640]{1,0:T(8,128)(2,1)S(1)} %get-tuple-element.21.refs_2_), channel_id=1, source_target_pairs={{0,1},{1,0},{2,3},{3,2},{4,5},{5,4},{6,7},{7,6},{8,9},{9,8},{10,11... | collective-permute-start | bytes 61448 | tf_op jit(solution)/shard_map/ppermute | solution.py:257
  22.3 15.6 %collective-permute-start.1 = (bf16[16,640]{1,0:T(8,128)(2,1)S(1)}, bf16[16,640]{1,0:T(8,128)(2,1)S(1)}, u32[]{:S(2)}, u32[]{:S(2)}) collective-permute-start(bf16[16,640]{1,0:T(8,128)(2,1)S(1)} %get-tuple-element.21.refs_2_), channel_id=1, source_target_pairs={{0,2},{1,3},{2,0},{3,1},{4,6},{5,7},{6,4},{7,5},{8,10},{9,11},{10,... | collective-permute-start | bytes 61448 | tf_op jit(solution)/shard_map/ppermute | solution.py:257
  34.6 5.6 %collective-permute-start.2 = (bf16[16,640]{1,0:T(8,128)(2,1)S(1)}, bf16[16,640]{1,0:T(8,128)(2,1)S(1)}, u32[]{:S(2)}, u32[]{:S(2)}) collective-permute-start(bf16[16,640]{1,0:T(8,128)(2,1)S(1)} %get-tuple-element.21.refs_2_), channel_id=1, source_target_pairs={{0,3},{1,2},{2,1},{3,0},{4,7},{5,6},{6,5},{7,4},{8,11},{9,10},{10,... | collective-permute-start | bytes 61448 | tf_op jit(solution)/shard_map/ppermute | solution.py:257
  37.8 5.3 %collective-permute-start.4 = (bf16[9,80,640]{2,1,0:T(8,128)(2,1)}, bf16[9,80,640]{2,1,0:T(8,128)(2,1)S(1)}, u32[]{:S(2)}, u32[]{:S(2)}) collective-permute-start(bf16[9,80,640]{2,1,0:T(8,128)(2,1)} %collective-permute-done.3.refs_1_), channel_id=1, source_target_pairs={{0,4},{1,5},{2,6},{3,7},{4,0},{5,1},{6,2},{7,3},{8,12},{9,13},{10,... | collective-permute-start | bytes 2764808 | tf_op jit(solution)/shard_map/ppermute | solution.py:257
  39.7 13.6 %collective-permute-start.16 = (bf16[9,80,640]{2,1,0:T(8,128)(2,1)}, bf16[9,80,640]{2,1,0:T(8,128)(2,1)S(1)}, u32[]{:S(2)}, u32[]{:S(2)}) collective-permute-start(bf16[9,80,640]{2,1,0:T(8,128)(2,1)} %collective-permute-done.14.refs_1_), channel_id=1, source_target_pairs={{0,2},{1,3},{2,0},{3,1},{4,5},{5,4},{6,7},{7,6},{8,9},{9,8},{10,11... | collective-permute-start | bytes 2764808 | tf_op jit(solution)/shard_map/ppermute | solution.py:257
  40.2 23.2 %collective-permute-start.18 = (bf16[9,80,640]{2,1,0:T(8,128)(2,1)}, bf16[9,80,640]{2,1,0:T(8,128)(2,1)S(1)}, u32[]{:S(2)}, u32[]{:S(2)}) collective-permute-start(bf16[9,80,640]{2,1,0:T(8,128)(2,1)} %collective-permute-done.14.refs_1_), channel_id=1, source_target_pairs={{0,8},{1,9},{2,10},{3,11},{4,12},{5,13},{6,14},{7,15},{8,0},{9,1},... | collective-permute-start | bytes 2764808 | tf_op jit(solution)/shard_map/ppermute | solution.py:257
  42.6 23.4 %collective-permute-start.6 = (bf16[9,80,640]{2,1,0:T(8,128)(2,1)}, bf16[9,80,640]{2,1,0:T(8,128)(2,1)S(1)}, u32[]{:S(2)}, u32[]{:S(2)}) collective-permute-start(bf16[9,80,640]{2,1,0:T(8,128)(2,1)} %collective-permute-done.5.refs_3_), channel_id=1, source_target_pairs={{0,4},{1,5},{2,6},{3,7},{4,0},{5,1},{6,2},{7,3},{8,12},{9,13},{10,... | collective-permute-start | bytes 2764808 | tf_op jit(solution)/shard_map/ppermute | solution.py:257
  42.6 24.3 %collective-permute-start.8 = (bf16[9,80,640]{2,1,0:T(8,128)(2,1)}, bf16[9,80,640]{2,1,0:T(8,128)(2,1)S(1)}, u32[]{:S(2)}, u32[]{:S(2)}) collective-permute-start(bf16[9,80,640]{2,1,0:T(8,128)(2,1)} %collective-permute-done.7.refs_5_), channel_id=1, source_target_pairs={{0,4},{1,5},{2,6},{3,7},{4,0},{5,1},{6,2},{7,3},{8,12},{9,13},{10,... | collective-permute-start | bytes 2764808 | tf_op jit(solution)/shard_map/ppermute | solution.py:257
  43.2 58.5 %collective-permute-start.15 = (bf16[9,80,640]{2,1,0:T(8,128)(2,1)}, bf16[9,80,640]{2,1,0:T(8,128)(2,1)S(1)}, u32[]{:S(2)}, u32[]{:S(2)}) collective-permute-start(bf16[9,80,640]{2,1,0:T(8,128)(2,1)} %collective-permute-done.14.refs_1_), channel_id=1, source_target_pairs={{0,4},{1,5},{2,6},{3,7},{4,0},{5,1},{6,2},{7,3},{8,12},{9,13},{10,... | collective-permute-start | bytes 2764808 | tf_op jit(solution)/shard_map/ppermute | solution.py:257
  53.3 48.3 %collective-permute-start.17 = (bf16[9,80,640]{2,1,0:T(8,128)(2,1)S(1)}, bf16[9,80,640]{2,1,0:T(8,128)(2,1)S(1)}, u32[]{:S(2)}, u32[]{:S(2)}) collective-permute-start(bf16[9,80,640]{2,1,0:T(8,128)(2,1)S(1)} %collective-permute-done.16.refs_3_), channel_id=1, source_target_pairs={{0,4},{1,5},{2,6},{3,7},{4,0},{5,1},{6,2},{7,3},{8,12},{9,13},{10,... | collective-permute-start | bytes 2764808 | tf_op jit(solution)/shard_map/ppermute | solution.py:257
  63.4 38.2 %collective-permute-start.19 = (bf16[9,80,640]{2,1,0:T(8,128)(2,1)S(1)}, bf16[9,80,640]{2,1,0:T(8,128)(2,1)S(1)}, u32[]{:S(2)}, u32[]{:S(2)}) collective-permute-start(bf16[9,80,640]{2,1,0:T(8,128)(2,1)S(1)} %collective-permute-done.18.refs_5_), channel_id=1, source_target_pairs={{0,4},{1,5},{2,6},{3,7},{4,0},{5,1},{6,2},{7,3},{8,12},{9,13},{10,... | collective-permute-start | bytes 2764808 | tf_op jit(solution)/shard_map/ppermute | solution.py:257
  66.0 15.7 %collective-permute-start.10 = (bf16[2,128,640]{2,1,0:T(8,128)(2,1)S(1)}, bf16[2,128,640]{2,1,0:T(8,128)(2,1)S(1)}, u32[]{:S(2)}, u32[]{:S(2)}) collective-permute-start(bf16[2,128,640]{2,1,0:T(8,128)(2,1)S(1)} %get-tuple-element.27), channel_id=1, source_target_pairs={{1,2},{2,1},{5,6},{6,5},{9,10},{10,9},{13,14},{14,13},{17,18},{18,... | collective-permute-start | bytes 983048 | tf_op jit(solution)/shard_map/ppermute | solution.py:257
  66.9 19.3 %collective-permute-start.9 = (bf16[2,128,640]{2,1,0:T(8,128)(2,1)S(1)}, bf16[2,128,640]{2,1,0:T(8,128)(2,1)S(1)}, u32[]{:S(2)}, u32[]{:S(2)}) collective-permute-start(bf16[2,128,640]{2,1,0:T(8,128)(2,1)S(1)} %get-tuple-element.26), channel_id=1, source_target_pairs={{0,1},{1,0},{2,3},{3,2},{4,5},{5,4},{6,7},{7,6},{8,9},{9,8},{10,11... | collective-permute-start | bytes 983048 | tf_op jit(solution)/shard_map/ppermute | solution.py:257
  86.2 8.4 %copy-start.6 = (f32[640]{0:T(1024)S(1)}, f32[640]{0:T(1024)}, u32[]{:S(2)}) copy-start(f32[640]{0:T(1024)} %param.10) | copy-start | bytes 7684
  86.2 15.4 %copy-start.4 = (bf16[9,640,160]{1,2,0:T(8,128)(2,1)S(1)}, bf16[9,640,160]{1,2,0:T(8,128)(2,1)}, u32[]{:S(2)}) copy-start(bf16[9,640,160]{1,2,0:T(8,128)(2,1)} %param.11) | copy-start | bytes 5529604
  89.4 3.8 %collective-permute-start.11 = (bf16[16,640]{1,0:T(8,128)(2,1)S(1)}, bf16[16,640]{1,0:T(8,128)(2,1)S(1)}, u32[]{:S(2)}, u32[]{:S(2)}) collective-permute-start(bf16[16,640]{1,0:T(8,128)(2,1)S(1)} %get-tuple-element.30.refs_1_), channel_id=1, source_target_pairs={{0,1},{1,0},{2,3},{3,2},{4,5},{5,4},{6,7},{7,6},{8,9},{9,8},{10,11... | collective-permute-start | bytes 61448 | tf_op jit(solution)/shard_map/ppermute | solution.py:257
  89.4 5.2 %collective-permute-start.12 = (bf16[16,640]{1,0:T(8,128)(2,1)S(1)}, bf16[16,640]{1,0:T(8,128)(2,1)S(1)}, u32[]{:S(2)}, u32[]{:S(2)}) collective-permute-start(bf16[16,640]{1,0:T(8,128)(2,1)S(1)} %get-tuple-element.30.refs_1_), channel_id=1, source_target_pairs={{0,2},{1,3},{2,0},{3,1},{4,6},{5,7},{6,4},{7,5},{8,10},{9,11},{10,... | collective-permute-start | bytes 61448 | tf_op jit(solution)/shard_map/ppermute | solution.py:257
  93.2 4.9 %collective-permute-start.13 = (bf16[16,640]{1,0:T(8,128)(2,1)S(1)}, bf16[16,640]{1,0:T(8,128)(2,1)S(1)}, u32[]{:S(2)}, u32[]{:S(2)}) collective-permute-start(bf16[16,640]{1,0:T(8,128)(2,1)S(1)} %get-tuple-element.30.refs_1_), channel_id=1, source_target_pairs={{0,3},{1,2},{2,1},{3,0},{4,7},{5,6},{6,5},{7,4},{8,11},{9,10},{10,... | collective-permute-start | bytes 61448 | tf_op jit(solution)/shard_map/ppermute | solution.py:257
  94.7 16.8 %collective-permute-start.20 = (bf16[2,128,640]{2,1,0:T(8,128)(2,1)S(1)}, bf16[2,128,640]{2,1,0:T(8,128)(2,1)S(1)}, u32[]{:S(2)}, u32[]{:S(2)}) collective-permute-start(bf16[2,128,640]{2,1,0:T(8,128)(2,1)S(1)} %get-tuple-element.35), channel_id=1, source_target_pairs={{0,1},{1,0},{2,3},{3,2},{4,5},{5,4},{6,7},{7,6},{8,9},{9,8},{10,11... | collective-permute-start | bytes 983048 | tf_op jit(solution)/shard_map/ppermute | solution.py:257
  98.1 13.3 %collective-permute-start.21 = (bf16[2,128,640]{2,1,0:T(8,128)(2,1)S(1)}, bf16[2,128,640]{2,1,0:T(8,128)(2,1)S(1)}, u32[]{:S(2)}, u32[]{:S(2)}) collective-permute-start(bf16[2,128,640]{2,1,0:T(8,128)(2,1)S(1)} %get-tuple-element.36), channel_id=1, source_target_pairs={{1,2},{2,1},{5,6},{6,5},{9,10},{10,9},{13,14},{14,13},{17,18},{18,... | collective-permute-start | bytes 983048 | tf_op jit(solution)/shard_map/ppermute | solution.py:257

commit v2 on v1

--- a/solution.py
+++ b/solution.py
@@ -187,12 +187,7 @@
             acc[0 : rows - 1] = acc[0 : rows - 1] + rows_product(xs, 1, rows - 1, wv)
 
 
-def edge_kernel(final, info, acc_in, w0, w2, hx, hd, coeff, *refs):
-    if final:
-        lat, tan, out_p, out_t, halo, acc = refs
-    else:
-        mid, sums, sx, sd, halo, acc = refs
-    rows, cols = acc_in.shape[0], acc_in.shape[2]
+def edge_products(info, hx, hd, coeff, w0, w2, halo):
     co = tuple(coeff[k : k + 1] for k in range(4))
     odd = info[ODD] == 1
     for slot in range(2):
@@ -202,34 +197,56 @@
         t = jnp.where(pick, hx[1], hd[1]).astype(F32)
         h, dh = activate(v, t, co)
         put(halo, slot, jnp.where(flag == 1, h, 0.0), jnp.where(flag == 1, dh, 0.0))
-    acc[...] = acc_in[...]
-    acc[0] = acc[0] + rows_product(halo, 0, 1, w0)[0]
-    acc[rows - 1] = acc[rows - 1] + rows_product(halo, 1, 1, w2)[0]
-    if final:
-        for r in range(rows):
-            out_p[r] = (lat[r].astype(F32) + acc[r, 0]).astype(BF)
-            out_t[r] = (tan[r].astype(F32) + acc[r, 1]).astype(BF)
-    else:
-        mid[...] = acc[...].astype(BF)
-        sums[...] = local_stats(
-            [functools.partial(lambda r: mid[r, 0].astype(F32), r) for r in range(rows)],
-            [functools.partial(lambda r: mid[r, 1].astype(F32), r) for r in range(rows)],
-            float(rows * cols),
-        )
-        send_rows(info, (mid[0, 0], mid[0, 1]), (mid[rows - 1, 0], mid[rows - 1, 1]), sx, sd)
+    return rows_product(halo, 0, 1, w0)[0], rows_product(halo, 1, 1, w2)[0]
+
+
+def first_edge_kernel(info, acc, w0, w2, hx, hd, coeff, mid, sums, sx, sd, halo):
+    rows, cols = acc.shape[0], acc.shape[2]
+    for r in range(1, rows - 1):
+        mid[r] = acc[r].astype(BF)
+    head, tail = edge_products(info, hx, hd, coeff, w0, w2, halo)
+    mid[0] = (acc[0] + head).astype(BF)
+    mid[rows - 1] = (acc[rows - 1] + tail).astype(BF)
+    sums[...] = local_stats(
+        [functools.partial(lambda r: mid[r, 0].astype(F32), r) for r in range(rows)],
+        [functools.partial(lambda r: mid[r, 1].astype(F32), r) for r in range(rows)],
+        float(rows * cols),
+    )
+    send_rows(info, (mid[0, 0], mid[0, 1]), (mid[rows - 1, 0], mid[rows - 1, 1]), sx, sd)
+
+
+def last_edge_kernel(info, acc, w0, w2, hx, hd, coeff, lat, tan, out_p, out_t, halo, done, sems):
+    rows = acc.shape[0]
+    copies = []
+
+    def leave(r, value):
+        for k, (source, out) in enumerate(((lat, out_p), (tan, out_t))):
+            done[k, r] = (source[r].astype(F32) + value[k]).astype(BF)
+            copy = pltpu.make_async_copy(done.at[k, r], out.at[r], sems.at[k, r])
+            copy.start()
+            copies.append(copy)
+
+    for r in range(1, rows - 1):
+        leave(r, acc[r])
+    head, tail = edge_products(info, hx, hd, coeff, w0, w2, halo)
+    leave(0, acc[0] + head)
+    leave(rows - 1, acc[rows - 1] + tail)
+    for copy in copies:
+        copy.wait()
 
 
 VM = functools.partial(pl.BlockSpec, memory_space=pltpu.VMEM)
 SM = functools.partial(pl.BlockSpec, memory_space=pltpu.SMEM)
+HB = functools.partial(pl.BlockSpec, memory_space=pl.ANY)
 ODD, VALID, OFFSETS = 0, 1, 3
 
 
-def call(kernel, args, outs, scratch=(), flops=0):
+def call(kernel, args, outs, scratch=(), flops=0, place=VM):
     return pl.pallas_call(
         kernel,
         out_shape=tuple(jax.ShapeDtypeStruct(s, d) for s, d in outs),
         in_specs=[SM() if a.dtype == jnp.int32 else VM() for a in args],
-        out_specs=tuple(VM() for _ in outs),
+        out_specs=tuple(place() for _ in outs),
         scratch_shapes=list(scratch),
         compiler_params=pltpu.CompilerParams(vmem_limit_bytes=VMEM_LIMIT),
         cost_estimate=pl.CostEstimate(flops=flops, bytes_accessed=0, transcendentals=0),
@@ -276,7 +293,7 @@
         ds = permute(sums, lambda a, i: (a, i ^ 3))
         ys = permute(sums, lambda a, i: (a, i ^ 2))
         xr = permute(hx, lambda a, i: (a, i ^ 1))
-        dr = permute(hd, lambda a, i: (a, i ^ 3), lambda a, i: 0 < i < n - 1)
+        dr = permute(hd, lambda a, i: (a, i ^ 3))
         return (sums, xs, ys, ds), (xr, dr)
 
     role = core ^ plane
@@ -314,13 +331,14 @@
             flops=work // 4,
         )
         acc, w0, w2 = call(main_kernel, [info, xs, *pieces], [acc_t, wrow, wrow], [pltpu.VMEM(*wrow)], flops=2 * work)
-        return call(
-            functools.partial(edge_kernel, k == 2),
-            [info, acc, w0, w2, *edges, coeff, *extra],
-            outs,
-            [pltpu.VMEM((2, 2, cols, 3 * chans), BF), pltpu.VMEM(*acc_t)],
-            flops=work,
-        )
+        halo = pltpu.VMEM((2, 2, cols, 3 * chans), BF)
+        if k == 2:
+            kernel, place = last_edge_kernel, HB
+            scratch = [halo, pltpu.VMEM((2, rows, cols, chans), BF), pltpu.SemaphoreType.DMA((2, rows))]
+        else:
+            kernel, place, scratch = first_edge_kernel, VM, [halo]
+        args = [info, acc, w0, w2, *edges, coeff, *extra]
+        return call(kernel, args, outs, scratch, work, place)
 
     pieces1 = gather(weight_first)
     pieces2 = gather(weight_second)

time: 116 us -> 114 us (0.983)
  starting transfers between devices: 27.9 us -> 26.3 us
    ppermute x22, starting transfers between devices: 27.9 us -> 26.3 us  [permute(): return lax.ppermute(x, AXES, pairs)]
  transfers between devices with their start and end apart: 22 -> 22, of which waited for: 7 -> 8; matrix products, arithmetic and copies ran while one was open for 1% -> 1% of each run, Pallas kernels for 26% -> 26%
where the time goes in v2:
time: 114 us
  waiting for transfers between devices  50.7 us (44%)
  Pallas kernels  33.7 us (30%)
  starting transfers between devices  26.3 us (23%)
  local copies, waits for them, and re-layouts  2.56 us (2%)
    ppermute x22, waiting for transfers between devices, permute(): return lax.ppermute(x, AXES, pairs)  50.7 us
    pallas_call x7, Pallas kernels, call(): pl.pallas_call(kernel, out_shape=tuple((jax.ShapeDtypeStruct(s, d) for s,...  33.7 us
    ppermute x22, starting transfers between devices, permute(): return lax.ppermute(x, AXES, pairs)  26.3 us
    dynamic_slice x2, local copies, waits for them, and re-layouts, gather(): part = lax.dynamic_slice_in_dim(w, half * core, half, axis=1)  2.43 us
  transfers between devices with their start and end apart: 22, of which 8 were waited for; matrix products, arithmetic and copies ran while one was open for 1% of the time, Pallas kernels for 26%

profile of v2, /device:TPU:0, one launch (start us, length us, event | category | flops | bytes accessed | tf_op | source)
XLA Modules:
  0.0 114.2 jit_solution(4471700594509956726)
XLA Ops:
  0.6 0.0 copy-start.3
  0.6 0.0 copy-start
  0.7 0.0 copy-start.1
  0.7 1.4 %dynamic-slice_bitcast_fusion.1 = bf16[9,80,640]{2,1,0:T(8,128)(2,1)S(1)} fusion(bf16[9,640,160]{1,2,0:T(8,128)(2,1)} %param.9, s32[]{:T(128)S(6)} %select_n.27), kind=kLoop, calls=%fused_computation.1 | loop fusion | bytes 1843204 | tf_op jit(solution)/shard_map/dynamic_slice | solution.py:282
  2.1 0.0 copy-start.5
  2.1 3.0 %collective-permute-start.3 = (bf16[9,80,640]{2,1,0:T(8,128)(2,1)S(1)}, bf16[9,80,640]{2,1,0:T(8,128)(2,1)}, u32[]{:S(2)}, u32[]{:S(2)}) collective-permute-start(bf16[9,80,640]{2,1,0:T(8,128)(2,1)S(1)} %dynamic-slice_bitcast_fusion.1), channel_id=1, source_target_pairs={{0,1},{1,0},{2,3},{3,2},{4,6},{5,7},{6,4},{7,5},{8,10},{9,11},{10,... | collective-permute-start | bytes 2764808 | tf_op jit(solution)/shard_map/ppermute | solution.py:274
  5.2 0.0 copy-done.3
  5.2 1.0 dynamic-slice_bitcast_fusion
  6.2 0.2 collective-permute-start.14
  6.4 10.3 %collective-permute-done.3.refs_1_ = bf16[9,80,640]{2,1,0:T(8,128)(2,1)} collective-permute-done((bf16[9,80,640]{2,1,0:T(8,128)(2,1)S(1)}, bf16[9,80,640]{2,1,0:T(8,128)(2,1)}, u32[]{:S(2)}, u32[]{:S(2)}) %collective-permute-start.3) | collective-permute-done | bytes 921632 | tf_op jit(solution)/shard_map/ppermute | solution.py:274
  16.7 2.0 %collective-permute-start.5 = (bf16[9,80,640]{2,1,0:T(8,128)(2,1)}, bf16[9,80,640]{2,1,0:T(8,128)(2,1)}, u32[]{:S(2)}, u32[]{:S(2)}) collective-permute-start(bf16[9,80,640]{2,1,0:T(8,128)(2,1)} %collective-permute-done.3.refs_1_), channel_id=1, source_target_pairs={{0,2},{1,3},{2,0},{3,1},{4,5},{5,4},{6,7},{7,6},{8,9},{9,8},{10,11... | collective-permute-start | bytes 2764808 | tf_op jit(solution)/shard_map/ppermute | solution.py:274
  18.7 1.5 %collective-permute-start.7 = (bf16[9,80,640]{2,1,0:T(8,128)(2,1)}, bf16[9,80,640]{2,1,0:T(8,128)(2,1)}, u32[]{:S(2)}, u32[]{:S(2)}) collective-permute-start(bf16[9,80,640]{2,1,0:T(8,128)(2,1)} %collective-permute-done.3.refs_1_), channel_id=1, source_target_pairs={{0,8},{1,9},{2,10},{3,11},{4,12},{5,13},{6,14},{7,15},{8,0},{9,1},... | collective-permute-start | bytes 2764808 | tf_op jit(solution)/shard_map/ppermute | solution.py:274
  20.3 0.1 stack.51.info
  20.4 0.0 copy-done
  20.4 0.0 copy-done.1
  20.4 1.3 %shard_map.77 = (bf16[16,640]{1,0:T(8,128)(2,1)S(1)}, bf16[2,128,640]{2,1,0:T(8,128)(2,1)S(1)}, bf16[2,128,640]{2,1,0:T(8,128)(2,1)S(1)}) custom-call(s32[10]{0:T(128)S(1)} %stack.51.info, bf16[4,128,640]{2,1,0:T(8,128)(2,1)S(1)} %bitcast.20, bf16[4,128,640]{2,1,0:T(8,128)(2,1)S(1)} %bitcast.23), custom_call_target="tpu_custom_call" | custom-call | flops 629145600 | tf_op jit(solution)/shard_map/pallas_call | solution.py:245
  21.7 0.6 collective-permute-start
  22.3 1.5 %collective-permute-start.1 = (bf16[16,640]{1,0:T(8,128)(2,1)S(1)}, bf16[16,640]{1,0:T(8,128)(2,1)S(1)}, u32[]{:S(2)}, u32[]{:S(2)}) collective-permute-start(bf16[16,640]{1,0:T(8,128)(2,1)S(1)} %get-tuple-element.21.refs_2_), channel_id=1, source_target_pairs={{0,2},{1,3},{2,0},{3,1},{4,6},{5,7},{6,4},{7,5},{8,10},{9,11},{10,... | collective-permute-start | bytes 61448 | tf_op jit(solution)/shard_map/ppermute | solution.py:274
  23.8 10.8 %collective-permute-done.refs_3_ = bf16[16,640]{1,0:T(8,128)(2,1)S(1)} collective-permute-done((bf16[16,640]{1,0:T(8,128)(2,1)S(1)}, bf16[16,640]{1,0:T(8,128)(2,1)S(1)}, u32[]{:S(2)}, u32[]{:S(2)}) %collective-permute-start) | collective-permute-done | bytes 20512 | tf_op jit(solution)/shard_map/ppermute | solution.py:274
  34.6 3.3 %collective-permute-start.2 = (bf16[16,640]{1,0:T(8,128)(2,1)S(1)}, bf16[16,640]{1,0:T(8,128)(2,1)S(1)}, u32[]{:S(2)}, u32[]{:S(2)}) collective-permute-start(bf16[16,640]{1,0:T(8,128)(2,1)S(1)} %get-tuple-element.21.refs_2_), channel_id=1, source_target_pairs={{0,3},{1,2},{2,1},{3,0},{4,7},{5,6},{6,5},{7,4},{8,11},{9,10},{10,... | collective-permute-start | bytes 61448 | tf_op jit(solution)/shard_map/ppermute | solution.py:274
  37.8 0.0 collective-permute-done.1.refs_4_
  37.8 1.8 %collective-permute-start.4 = (bf16[9,80,640]{2,1,0:T(8,128)(2,1)}, bf16[9,80,640]{2,1,0:T(8,128)(2,1)S(1)}, u32[]{:S(2)}, u32[]{:S(2)}) collective-permute-start(bf16[9,80,640]{2,1,0:T(8,128)(2,1)} %collective-permute-done.3.refs_1_), channel_id=1, source_target_pairs={{0,4},{1,5},{2,6},{3,7},{4,0},{5,1},{6,2},{7,3},{8,12},{9,13},{10,... | collective-permute-start | bytes 2764808 | tf_op jit(solution)/shard_map/ppermute | solution.py:274
  39.7 0.0 collective-permute-done.14.refs_1_
  39.7 0.5 collective-permute-start.16
  40.2 0.0 collective-permute-done.2.refs_5_
  40.2 2.4 %collective-permute-start.18 = (bf16[9,80,640]{2,1,0:T(8,128)(2,1)}, bf16[9,80,640]{2,1,0:T(8,128)(2,1)S(1)}, u32[]{:S(2)}, u32[]{:S(2)}) collective-permute-start(bf16[9,80,640]{2,1,0:T(8,128)(2,1)} %collective-permute-done.14.refs_1_), channel_id=1, source_target_pairs={{0,8},{1,9},{2,10},{3,11},{4,12},{5,13},{6,14},{7,15},{8,0},{9,1},... | collective-permute-start | bytes 2764808 | tf_op jit(solution)/shard_map/ppermute | solution.py:274
  42.6 0.0 collective-permute-done.5.refs_3_
  42.6 0.0 collective-permute-start.6
  42.6 0.0 collective-permute-done.7.refs_5_
  42.6 0.5 collective-permute-start.8
  43.1 0.0 collective-permute-done.4.refs_2_
  43.2 0.1 collective-permute-start.15
  43.2 10.1 %collective-permute-done.16.refs_3_ = bf16[9,80,640]{2,1,0:T(8,128)(2,1)S(1)} collective-permute-done((bf16[9,80,640]{2,1,0:T(8,128)(2,1)}, bf16[9,80,640]{2,1,0:T(8,128)(2,1)S(1)}, u32[]{:S(2)}, u32[]{:S(2)}) %collective-permute-start.16) | collective-permute-done | bytes 921632 | tf_op jit(solution)/shard_map/ppermute | solution.py:274
  53.3 0.0 collective-permute-start.17
  53.3 10.1 %collective-permute-done.18.refs_5_ = bf16[9,80,640]{2,1,0:T(8,128)(2,1)S(1)} collective-permute-done((bf16[9,80,640]{2,1,0:T(8,128)(2,1)}, bf16[9,80,640]{2,1,0:T(8,128)(2,1)S(1)}, u32[]{:S(2)}, u32[]{:S(2)}) %collective-permute-start.18) | collective-permute-done | bytes 921632 | tf_op jit(solution)/shard_map/ppermute | solution.py:274
  63.4 0.0 collective-permute-start.19
  63.4 0.0 copy-done.5
  63.4 2.6 %shard_map.78 = (bf16[4,2,128,1920]{3,2,1,0:T(8,128)(2,1)S(1)}, f32[8,640]{1,0:T(8,128)S(1)}) custom-call(bf16[4,128,640]{2,1,0:T(8,128)(2,1)S(1)} %bitcast.21, bf16[4,128,640]{2,1,0:T(8,128)(2,1)S(1)} %bitcast.24, bf16[16,640]{1,0:T(8,128)(2,1)S(1)} %get-tuple-element.21.refs_2_, bf16[16,640]{1,0:T(8,128)(2,1)S(1)} %collective-permute-done.refs_3_, ...), custom_call_target="tpu_custom_call" | custom-call | flops 629145600 | tf_op jit(solution)/shard_map/pallas_call | solution.py:245
  66.0 0.0 collective-permute-done.6.refs_4_
  66.0 2.7 %collective-permute-start.10 = (bf16[2,128,640]{2,1,0:T(8,128)(2,1)S(1)}, bf16[2,128,640]{2,1,0:T(8,128)(2,1)S(1)}, u32[]{:S(2)}, u32[]{:S(2)}) collective-permute-start(bf16[2,128,640]{2,1,0:T(8,128)(2,1)S(1)} %get-tuple-element.27), channel_id=1, source_target_pairs={{0,3},{1,2},{2,1},{3,0},{4,7},{5,6},{6,5},{7,4},{8,11},{9,10},{10,... | collective-permute-start | bytes 983048 | tf_op jit(solution)/shard_map/ppermute | solution.py:274
  68.7 0.0 collective-permute-done.8.refs_6_
  68.7 0.5 collective-permute-start.9
  69.3 10.4 %shard_map.79 = (f32[4,2,128,640]{3,2,1,0:T(8,128)S(1)}, bf16[640,1920]{1,0:T(8,128)(2,1)S(1)}, bf16[640,1920]{1,0:T(8,128)(2,1)S(1)}) custom-call(s32[10]{0:T(128)S(1)} %stack.51.info, bf16[4,2,128,1920]{3,2,1,0:T(8,128)(2,1)S(1)} %get-tuple-element.22.xs, bf16[9,160,640]{2,1,0:T(8,128)(2,1)S(1)} %bitcast.26, ...), custom_call_target="tpu_custom_call" | custom-call | flops 5033164800 | tf_op jit(solution)/shard_map/pallas_call | solution.py:245
  79.6 0.0 collective-permute-done.10.hd
  79.6 4.7 %collective-permute-done.9.hx = bf16[2,128,640]{2,1,0:T(8,128)(2,1)S(1)} collective-permute-done((bf16[2,128,640]{2,1,0:T(8,128)(2,1)S(1)}, bf16[2,128,640]{2,1,0:T(8,128)(2,1)S(1)}, u32[]{:S(2)}, u32[]{:S(2)}) %collective-permute-start.9) | collective-permute-done | bytes 327712 | tf_op jit(solution)/shard_map/ppermute | solution.py:274
  84.4 3.3 %shard_map.80 = (bf16[4,2,128,640]{3,2,1,0:T(8,128)(2,1)S(1)}, bf16[16,640]{1,0:T(8,128)(2,1)S(1)}, bf16[2,128,640]{2,1,0:T(8,128)(2,1)S(1)}, bf16[2,128,640]{2,1,0:T(8,128)(2,1)S(1)}) custom-call(s32[10]{0:T(128)S(1)} %stack.51.info, f32[4,2,128,640]{3,2,1,0:T(8,128)S(1)} %get-tuple-element.23.acc, bf16[640,1920]{1,0:T(8,128)(2,1)S(1)} %get-tuple-element.24.w0, ...), custom_call_target="tpu_custom_call" | custom-call | flops 2516582400 | tf_op jit(solution)/shard_map/pallas_call | solution.py:245
  87.7 1.6 %collective-permute-start.11 = (bf16[16,640]{1,0:T(8,128)(2,1)S(1)}, bf16[16,640]{1,0:T(8,128)(2,1)S(1)}, u32[]{:S(2)}, u32[]{:S(2)}) collective-permute-start(bf16[16,640]{1,0:T(8,128)(2,1)S(1)} %get-tuple-element.30.refs_1_), channel_id=1, source_target_pairs={{0,1},{1,0},{2,3},{3,2},{4,5},{5,4},{6,7},{7,6},{8,9},{9,8},{10,11... | collective-permute-start | bytes 61448 | tf_op jit(solution)/shard_map/ppermute | solution.py:274
  89.3 0.5 collective-permute-start.12
  89.8 1.8 %collective-permute-done.11.refs_2_ = bf16[16,640]{1,0:T(8,128)(2,1)S(1)} collective-permute-done((bf16[16,640]{1,0:T(8,128)(2,1)S(1)}, bf16[16,640]{1,0:T(8,128)(2,1)S(1)}, u32[]{:S(2)}, u32[]{:S(2)}) %collective-permute-start.11) | collective-permute-done | bytes 20512 | tf_op jit(solution)/shard_map/ppermute | solution.py:274
  91.6 1.4 %collective-permute-start.13 = (bf16[16,640]{1,0:T(8,128)(2,1)S(1)}, bf16[16,640]{1,0:T(8,128)(2,1)S(1)}, u32[]{:S(2)}, u32[]{:S(2)}) collective-permute-start(bf16[16,640]{1,0:T(8,128)(2,1)S(1)} %get-tuple-element.30.refs_1_), channel_id=1, source_target_pairs={{0,3},{1,2},{2,1},{3,0},{4,7},{5,6},{6,5},{7,4},{8,11},{9,10},{10,... | collective-permute-start | bytes 61448 | tf_op jit(solution)/shard_map/ppermute | solution.py:274
  93.0 0.0 copy-done.6
  93.0 0.1 collective-permute-done.12.refs_3_
  93.1 0.5 collective-permute-start.20
  93.6 2.9 %collective-permute-done.13.refs_4_ = bf16[16,640]{1,0:T(8,128)(2,1)S(1)} collective-permute-done((bf16[16,640]{1,0:T(8,128)(2,1)S(1)}, bf16[16,640]{1,0:T(8,128)(2,1)S(1)}, u32[]{:S(2)}, u32[]{:S(2)}) %collective-permute-start.13) | collective-permute-done | bytes 20512 | tf_op jit(solution)/shard_map/ppermute | solution.py:274
  96.5 1.4 %collective-permute-start.21 = (bf16[2,128,640]{2,1,0:T(8,128)(2,1)S(1)}, bf16[2,128,640]{2,1,0:T(8,128)(2,1)S(1)}, u32[]{:S(2)}, u32[]{:S(2)}) collective-permute-start(bf16[2,128,640]{2,1,0:T(8,128)(2,1)S(1)} %get-tuple-element.36), channel_id=1, source_target_pairs={{0,3},{1,2},{2,1},{3,0},{4,7},{5,6},{6,5},{7,4},{8,11},{9,10},{10,... | collective-permute-start | bytes 983048 | tf_op jit(solution)/shard_map/ppermute | solution.py:274
  97.9 2.6 %shard_map.81 = (bf16[4,2,128,1920]{3,2,1,0:T(8,128)(2,1)S(1)}, f32[8,640]{1,0:T(8,128)S(1)}) custom-call(bf16[4,2,128,640]{3,2,1,0:T(8,128)(2,1)S(1)} %get-tuple-element.29.refs_0_, bf16[16,640]{1,0:T(8,128)(2,1)S(1)} %get-tuple-element.30.refs_1_, bf16[16,640]{1,0:T(8,128)(2,1)S(1)} %collective-permute-done.11.refs_2_, ...), custom_call_target="tpu_custom_call" | custom-call | flops 629145600 | tf_op jit(solution)/shard_map/pallas_call | solution.py:245
  100.5 0.0 collective-permute-done.15.refs_2_
  100.5 0.0 collective-permute-done.17.refs_4_
  100.5 0.0 collective-permute-done.19.refs_6_
  100.5 0.0 copy-done.4
  100.5 9.8 %shard_map.82 = (f32[4,2,128,640]{3,2,1,0:T(8,128)S(1)}, bf16[640,1920]{1,0:T(8,128)(2,1)S(1)}, bf16[640,1920]{1,0:T(8,128)(2,1)S(1)}) custom-call(s32[10]{0:T(128)S(1)} %stack.51.info, bf16[4,2,128,1920]{3,2,1,0:T(8,128)(2,1)S(1)} %get-tuple-element.31.xs, bf16[9,160,640]{2,1,0:T(8,128)(2,1)S(1)} %bitcast.27, ...), custom_call_target="tpu_custom_call" | custom-call | flops 5033164800 | tf_op jit(solution)/shard_map/pallas_call | solution.py:245
  110.3 0.0 collective-permute-done.20.hx
  110.3 0.0 collective-permute-done.21.hd
  110.3 3.7 %shard_map.83 = (bf16[4,128,640]{2,1,0:T(8,128)(2,1)}, bf16[4,128,640]{2,1,0:T(8,128)(2,1)}) custom-call(s32[10]{0:T(128)S(1)} %stack.51.info, f32[4,2,128,640]{3,2,1,0:T(8,128)S(1)} %get-tuple-element.32.acc, bf16[640,1920]{1,0:T(8,128)(2,1)S(1)} %get-tuple-element.33.w0, bf16[640,1920]{1,0:T(8,128)(2,1)S(1)} %get-tuple-element.34.w2, ...), custom_call_target="tpu_custom_call" | custom-call | flops 2516582400 | tf_op jit(solution)/shard_map/pallas_call | solution.py:245
  (6 shorter events, 0.0 us)
Async XLA Ops:
  0.6 4.5 %copy-start.3 = (bf16[9,640,160]{1,2,0:T(8,128)(2,1)S(1)}, bf16[9,640,160]{1,2,0:T(8,128)(2,1)}, u32[]{:S(2)}) copy-start(bf16[9,640,160]{1,2,0:T(8,128)(2,1)} %param.11) | copy-start | bytes 5529604
  0.6 19.7 %copy-start = (bf16[1,4,128,640]{3,2,1,0:T(8,128)(2,1)S(1)}, bf16[1,4,128,640]{3,2,1,0:T(8,128)(2,1)}, u32[]{:S(2)}) copy-start(bf16[1,4,128,640]{3,2,1,0:T(8,128)(2,1)} %param.6) | copy-start | bytes 1966084
  0.7 19.7 %copy-start.1 = (bf16[1,4,128,640]{3,2,1,0:T(8,128)(2,1)S(1)}, bf16[1,4,128,640]{3,2,1,0:T(8,128)(2,1)}, u32[]{:S(2)}) copy-start(bf16[1,4,128,640]{3,2,1,0:T(8,128)(2,1)} %param.7) | copy-start | bytes 1966084
  2.1 61.3 %copy-start.5 = (f32[640]{0:T(1024)S(1)}, f32[640]{0:T(1024)}, u32[]{:S(2)}) copy-start(f32[640]{0:T(1024)} %param.8) | copy-start | bytes 7684
  2.1 14.6 %collective-permute-start.3 = (bf16[9,80,640]{2,1,0:T(8,128)(2,1)S(1)}, bf16[9,80,640]{2,1,0:T(8,128)(2,1)}, u32[]{:S(2)}, u32[]{:S(2)}) collective-permute-start(bf16[9,80,640]{2,1,0:T(8,128)(2,1)S(1)} %dynamic-slice_bitcast_fusion.1), channel_id=1, source_target_pairs={{0,1},{1,0},{2,3},{3,2},{4,6},{5,7},{6,4},{7,5},{8,10},{9,11},{10,... | collective-permute-start | bytes 2764808 | tf_op jit(solution)/shard_map/ppermute | solution.py:274
  6.2 63.1 %copy-start.2 = (bf16[9,640,160]{1,2,0:T(8,128)(2,1)S(1)}, bf16[9,640,160]{1,2,0:T(8,128)(2,1)}, u32[]{:S(2)}) copy-start(bf16[9,640,160]{1,2,0:T(8,128)(2,1)} %param.9) | copy-start | bytes 5529604
  6.2 33.5 %collective-permute-start.14 = (bf16[9,80,640]{2,1,0:T(8,128)(2,1)}, bf16[9,80,640]{2,1,0:T(8,128)(2,1)}, u32[]{:S(2)}, u32[]{:S(2)}) collective-permute-start(bf16[9,80,640]{2,1,0:T(8,128)(2,1)} %dynamic-slice_bitcast_fusion), channel_id=1, source_target_pairs={{0,1},{1,0},{2,3},{3,2},{4,6},{5,7},{6,4},{7,5},{8,10},{9,11},{10,... | collective-permute-start | bytes 2764808 | tf_op jit(solution)/shard_map/ppermute | solution.py:274
  16.7 26.0 %collective-permute-start.5 = (bf16[9,80,640]{2,1,0:T(8,128)(2,1)}, bf16[9,80,640]{2,1,0:T(8,128)(2,1)}, u32[]{:S(2)}, u32[]{:S(2)}) collective-permute-start(bf16[9,80,640]{2,1,0:T(8,128)(2,1)} %collective-permute-done.3.refs_1_), channel_id=1, source_target_pairs={{0,2},{1,3},{2,0},{3,1},{4,5},{5,4},{6,7},{7,6},{8,9},{9,8},{10,11... | collective-permute-start | bytes 2764808 | tf_op jit(solution)/shard_map/ppermute | solution.py:274
  18.7 23.9 %collective-permute-start.7 = (bf16[9,80,640]{2,1,0:T(8,128)(2,1)}, bf16[9,80,640]{2,1,0:T(8,128)(2,1)}, u32[]{:S(2)}, u32[]{:S(2)}) collective-permute-start(bf16[9,80,640]{2,1,0:T(8,128)(2,1)} %collective-permute-done.3.refs_1_), channel_id=1, source_target_pairs={{0,8},{1,9},{2,10},{3,11},{4,12},{5,13},{6,14},{7,15},{8,0},{9,1},... | collective-permute-start | bytes 2764808 | tf_op jit(solution)/shard_map/ppermute | solution.py:274
  21.7 12.9 %collective-permute-start = (bf16[16,640]{1,0:T(8,128)(2,1)S(1)}, bf16[16,640]{1,0:T(8,128)(2,1)S(1)}, u32[]{:S(2)}, u32[]{:S(2)}) collective-permute-start(bf16[16,640]{1,0:T(8,128)(2,1)S(1)} %get-tuple-element.21.refs_2_), channel_id=1, source_target_pairs={{0,1},{1,0},{2,3},{3,2},{4,5},{5,4},{6,7},{7,6},{8,9},{9,8},{10,11... | collective-permute-start | bytes 61448 | tf_op jit(solution)/shard_map/ppermute | solution.py:274
  22.3 15.6 %collective-permute-start.1 = (bf16[16,640]{1,0:T(8,128)(2,1)S(1)}, bf16[16,640]{1,0:T(8,128)(2,1)S(1)}, u32[]{:S(2)}, u32[]{:S(2)}) collective-permute-start(bf16[16,640]{1,0:T(8,128)(2,1)S(1)} %get-tuple-element.21.refs_2_), channel_id=1, source_target_pairs={{0,2},{1,3},{2,0},{3,1},{4,6},{5,7},{6,4},{7,5},{8,10},{9,11},{10,... | collective-permute-start | bytes 61448 | tf_op jit(solution)/shard_map/ppermute | solution.py:274
  34.6 5.6 %collective-permute-start.2 = (bf16[16,640]{1,0:T(8,128)(2,1)S(1)}, bf16[16,640]{1,0:T(8,128)(2,1)S(1)}, u32[]{:S(2)}, u32[]{:S(2)}) collective-permute-start(bf16[16,640]{1,0:T(8,128)(2,1)S(1)} %get-tuple-element.21.refs_2_), channel_id=1, source_target_pairs={{0,3},{1,2},{2,1},{3,0},{4,7},{5,6},{6,5},{7,4},{8,11},{9,10},{10,... | collective-permute-start | bytes 61448 | tf_op jit(solution)/shard_map/ppermute | solution.py:274
  37.8 5.3 %collective-permute-start.4 = (bf16[9,80,640]{2,1,0:T(8,128)(2,1)}, bf16[9,80,640]{2,1,0:T(8,128)(2,1)S(1)}, u32[]{:S(2)}, u32[]{:S(2)}) collective-permute-start(bf16[9,80,640]{2,1,0:T(8,128)(2,1)} %collective-permute-done.3.refs_1_), channel_id=1, source_target_pairs={{0,4},{1,5},{2,6},{3,7},{4,0},{5,1},{6,2},{7,3},{8,12},{9,13},{10,... | collective-permute-start | bytes 2764808 | tf_op jit(solution)/shard_map/ppermute | solution.py:274
  39.7 13.6 %collective-permute-start.16 = (bf16[9,80,640]{2,1,0:T(8,128)(2,1)}, bf16[9,80,640]{2,1,0:T(8,128)(2,1)S(1)}, u32[]{:S(2)}, u32[]{:S(2)}) collective-permute-start(bf16[9,80,640]{2,1,0:T(8,128)(2,1)} %collective-permute-done.14.refs_1_), channel_id=1, source_target_pairs={{0,2},{1,3},{2,0},{3,1},{4,5},{5,4},{6,7},{7,6},{8,9},{9,8},{10,11... | collective-permute-start | bytes 2764808 | tf_op jit(solution)/shard_map/ppermute | solution.py:274
  40.2 23.2 %collective-permute-start.18 = (bf16[9,80,640]{2,1,0:T(8,128)(2,1)}, bf16[9,80,640]{2,1,0:T(8,128)(2,1)S(1)}, u32[]{:S(2)}, u32[]{:S(2)}) collective-permute-start(bf16[9,80,640]{2,1,0:T(8,128)(2,1)} %collective-permute-done.14.refs_1_), channel_id=1, source_target_pairs={{0,8},{1,9},{2,10},{3,11},{4,12},{5,13},{6,14},{7,15},{8,0},{9,1},... | collective-permute-start | bytes 2764808 | tf_op jit(solution)/shard_map/ppermute | solution.py:274
  42.6 23.4 %collective-permute-start.6 = (bf16[9,80,640]{2,1,0:T(8,128)(2,1)}, bf16[9,80,640]{2,1,0:T(8,128)(2,1)S(1)}, u32[]{:S(2)}, u32[]{:S(2)}) collective-permute-start(bf16[9,80,640]{2,1,0:T(8,128)(2,1)} %collective-permute-done.5.refs_3_), channel_id=1, source_target_pairs={{0,4},{1,5},{2,6},{3,7},{4,0},{5,1},{6,2},{7,3},{8,12},{9,13},{10,... | collective-permute-start | bytes 2764808 | tf_op jit(solution)/shard_map/ppermute | solution.py:274
  42.6 26.1 %collective-permute-start.8 = (bf16[9,80,640]{2,1,0:T(8,128)(2,1)}, bf16[9,80,640]{2,1,0:T(8,128)(2,1)S(1)}, u32[]{:S(2)}, u32[]{:S(2)}) collective-permute-start(bf16[9,80,640]{2,1,0:T(8,128)(2,1)} %collective-permute-done.7.refs_5_), channel_id=1, source_target_pairs={{0,4},{1,5},{2,6},{3,7},{4,0},{5,1},{6,2},{7,3},{8,12},{9,13},{10,... | collective-permute-start | bytes 2764808 | tf_op jit(solution)/shard_map/ppermute | solution.py:274
  43.2 57.4 %collective-permute-start.15 = (bf16[9,80,640]{2,1,0:T(8,128)(2,1)}, bf16[9,80,640]{2,1,0:T(8,128)(2,1)S(1)}, u32[]{:S(2)}, u32[]{:S(2)}) collective-permute-start(bf16[9,80,640]{2,1,0:T(8,128)(2,1)} %collective-permute-done.14.refs_1_), channel_id=1, source_target_pairs={{0,4},{1,5},{2,6},{3,7},{4,0},{5,1},{6,2},{7,3},{8,12},{9,13},{10,... | collective-permute-start | bytes 2764808 | tf_op jit(solution)/shard_map/ppermute | solution.py:274
  53.3 47.2 %collective-permute-start.17 = (bf16[9,80,640]{2,1,0:T(8,128)(2,1)S(1)}, bf16[9,80,640]{2,1,0:T(8,128)(2,1)S(1)}, u32[]{:S(2)}, u32[]{:S(2)}) collective-permute-start(bf16[9,80,640]{2,1,0:T(8,128)(2,1)S(1)} %collective-permute-done.16.refs_3_), channel_id=1, source_target_pairs={{0,4},{1,5},{2,6},{3,7},{4,0},{5,1},{6,2},{7,3},{8,12},{9,13},{10,... | collective-permute-start | bytes 2764808 | tf_op jit(solution)/shard_map/ppermute | solution.py:274
  63.4 37.1 %collective-permute-start.19 = (bf16[9,80,640]{2,1,0:T(8,128)(2,1)S(1)}, bf16[9,80,640]{2,1,0:T(8,128)(2,1)S(1)}, u32[]{:S(2)}, u32[]{:S(2)}) collective-permute-start(bf16[9,80,640]{2,1,0:T(8,128)(2,1)S(1)} %collective-permute-done.18.refs_5_), channel_id=1, source_target_pairs={{0,4},{1,5},{2,6},{3,7},{4,0},{5,1},{6,2},{7,3},{8,12},{9,13},{10,... | collective-permute-start | bytes 2764808 | tf_op jit(solution)/shard_map/ppermute | solution.py:274
  66.0 13.6 %collective-permute-start.10 = (bf16[2,128,640]{2,1,0:T(8,128)(2,1)S(1)}, bf16[2,128,640]{2,1,0:T(8,128)(2,1)S(1)}, u32[]{:S(2)}, u32[]{:S(2)}) collective-permute-start(bf16[2,128,640]{2,1,0:T(8,128)(2,1)S(1)} %get-tuple-element.27), channel_id=1, source_target_pairs={{0,3},{1,2},{2,1},{3,0},{4,7},{5,6},{6,5},{7,4},{8,11},{9,10},{10,... | collective-permute-start | bytes 983048 | tf_op jit(solution)/shard_map/ppermute | solution.py:274
  68.7 15.6 %collective-permute-start.9 = (bf16[2,128,640]{2,1,0:T(8,128)(2,1)S(1)}, bf16[2,128,640]{2,1,0:T(8,128)(2,1)S(1)}, u32[]{:S(2)}, u32[]{:S(2)}) collective-permute-start(bf16[2,128,640]{2,1,0:T(8,128)(2,1)S(1)} %get-tuple-element.26), channel_id=1, source_target_pairs={{0,1},{1,0},{2,3},{3,2},{4,5},{5,4},{6,7},{7,6},{8,9},{9,8},{10,11... | collective-permute-start | bytes 983048 | tf_op jit(solution)/shard_map/ppermute | solution.py:274
  84.4 8.6 %copy-start.6 = (f32[640]{0:T(1024)S(1)}, f32[640]{0:T(1024)}, u32[]{:S(2)}) copy-start(f32[640]{0:T(1024)} %param.10) | copy-start | bytes 7684
  84.4 16.1 %copy-start.4 = (bf16[9,640,160]{1,2,0:T(8,128)(2,1)S(1)}, bf16[9,640,160]{1,2,0:T(8,128)(2,1)}, u32[]{:S(2)}) copy-start(bf16[9,640,160]{1,2,0:T(8,128)(2,1)} %param.11) | copy-start | bytes 5529604
  87.7 3.8 %collective-permute-start.11 = (bf16[16,640]{1,0:T(8,128)(2,1)S(1)}, bf16[16,640]{1,0:T(8,128)(2,1)S(1)}, u32[]{:S(2)}, u32[]{:S(2)}) collective-permute-start(bf16[16,640]{1,0:T(8,128)(2,1)S(1)} %get-tuple-element.30.refs_1_), channel_id=1, source_target_pairs={{0,1},{1,0},{2,3},{3,2},{4,5},{5,4},{6,7},{7,6},{8,9},{9,8},{10,11... | collective-permute-start | bytes 61448 | tf_op jit(solution)/shard_map/ppermute | solution.py:274
  89.3 3.8 %collective-permute-start.12 = (bf16[16,640]{1,0:T(8,128)(2,1)S(1)}, bf16[16,640]{1,0:T(8,128)(2,1)S(1)}, u32[]{:S(2)}, u32[]{:S(2)}) collective-permute-start(bf16[16,640]{1,0:T(8,128)(2,1)S(1)} %get-tuple-element.30.refs_1_), channel_id=1, source_target_pairs={{0,2},{1,3},{2,0},{3,1},{4,6},{5,7},{6,4},{7,5},{8,10},{9,11},{10,... | collective-permute-start | bytes 61448 | tf_op jit(solution)/shard_map/ppermute | solution.py:274
  91.6 4.9 %collective-permute-start.13 = (bf16[16,640]{1,0:T(8,128)(2,1)S(1)}, bf16[16,640]{1,0:T(8,128)(2,1)S(1)}, u32[]{:S(2)}, u32[]{:S(2)}) collective-permute-start(bf16[16,640]{1,0:T(8,128)(2,1)S(1)} %get-tuple-element.30.refs_1_), channel_id=1, source_target_pairs={{0,3},{1,2},{2,1},{3,0},{4,7},{5,6},{6,5},{7,4},{8,11},{9,10},{10,... | collective-permute-start | bytes 61448 | tf_op jit(solution)/shard_map/ppermute | solution.py:274
  93.1 17.3 %collective-permute-start.20 = (bf16[2,128,640]{2,1,0:T(8,128)(2,1)S(1)}, bf16[2,128,640]{2,1,0:T(8,128)(2,1)S(1)}, u32[]{:S(2)}, u32[]{:S(2)}) collective-permute-start(bf16[2,128,640]{2,1,0:T(8,128)(2,1)S(1)} %get-tuple-element.35), channel_id=1, source_target_pairs={{0,1},{1,0},{2,3},{3,2},{4,5},{5,4},{6,7},{7,6},{8,9},{9,8},{10,11... | collective-permute-start | bytes 983048 | tf_op jit(solution)/shard_map/ppermute | solution.py:274
  96.5 13.9 %collective-permute-start.21 = (bf16[2,128,640]{2,1,0:T(8,128)(2,1)S(1)}, bf16[2,128,640]{2,1,0:T(8,128)(2,1)S(1)}, u32[]{:S(2)}, u32[]{:S(2)}) collective-permute-start(bf16[2,128,640]{2,1,0:T(8,128)(2,1)S(1)} %get-tuple-element.36), channel_id=1, source_target_pairs={{0,3},{1,2},{2,1},{3,0},{4,7},{5,6},{6,5},{7,4},{8,11},{9,10},{10,... | collective-permute-start | bytes 983048 | tf_op jit(solution)/shard_map/ppermute | solution.py:274

commit v3 on v2

--- a/solution.py
+++ b/solution.py
@@ -67,9 +67,8 @@
     return sums[0:8] + (sums[8:16] + sums[16:24])
 
 
-def coefficients(stats, gain, count, total):
+def coefficients(stats, matrix, gain, count, total):
     chans = gain.shape[1]
-    matrix = group_matrix(chans)
     first = stats[0][0:2]
     for s in stats[1:]:
         first = first + s[0:2]
@@ -117,7 +116,7 @@
         hd[k] = jnp.where(odd, last[k], first[k])
 
 
-def sums_kernel(info, lat, tan, sums, hx, hd):
+def sums_kernel(info, lat, tan, sums, hx, hd, matrix):
     rows, cols, _ = lat.shape
     sums[...] = local_stats(
         [functools.partial(lambda r: lat[r].astype(F32), r) for r in range(rows)],
@@ -125,6 +124,7 @@
         float(rows * cols),
     )
     send_rows(info, (lat[0], tan[0]), (lat[rows - 1], tan[rows - 1]), hx, hd)
+    matrix[...] = group_matrix(lat.shape[2])
 
 
 def put(xs, row, h, dh):
@@ -146,10 +146,10 @@
         lat, tan = refs.pop(0), refs.pop(0)
         rows, cols, chans = lat.shape
         load = lambda r: (lat[r].astype(F32), tan[r].astype(F32))
-    s0, s1, s2, s3, gain, xs, coeff_out = refs
+    s0, s1, s2, s3, matrix, gain, xs, coeff_out = refs
     count = float(rows * cols)
     total = count * n_devices * (chans // GROUPS)
-    coeff = coefficients([unpack_stats(s[...]) for s in (s0, s1, s2, s3)], gain[...], count, total)
+    coeff = coefficients([unpack_stats(s[...]) for s in (s0, s1, s2, s3)], matrix[...], gain[...], count, total)
     coeff_out[...] = jnp.concatenate(list(coeff) + [jnp.zeros((4, chans), F32)], 0)
     for r in range(rows):
         put(xs, r, *activate(*load(r), coeff))
@@ -288,12 +288,12 @@
         plane_s = permute(plane, core_to)
         return [w, first, first_s, relay, relay_s, plane, plane_s]
 
-    def exchange(sums, hx, hd):
+    def exchange(k, sums, hx, hd):
         xs = permute(sums, lambda a, i: (a, i ^ 1))
         ds = permute(sums, lambda a, i: (a, i ^ 3))
         ys = permute(sums, lambda a, i: (a, i ^ 2))
         xr = permute(hx, lambda a, i: (a, i ^ 1))
-        dr = permute(hd, lambda a, i: (a, i ^ 3))
+        dr = permute(hd, lambda a, i: (a, i ^ 3), lambda a, i: k == 2 or 0 < i < n - 1)
         return (sums, xs, ys, ds), (xr, dr)
 
     role = core ^ plane
@@ -322,11 +322,11 @@
     wrow = ((chans, 3 * chans), BF)
     work = 2 * rows * 2 * cols * 3 * chans * chans
 
-    def block(k, source, gain, sums, hx, hd, pieces, extra, outs):
-        stats, edges = exchange(sums, hx, hd)
+    def block(k, source, matrix, gain, sums, hx, hd, pieces, extra, outs):
+        stats, edges = exchange(k, sums, hx, hd)
         xs, coeff = call(
             functools.partial(act_kernel, n, len(source) == 1),
-            [*source, *stats, gain[None]],
+            [*source, *stats, matrix, gain[None]],
             [wide, ((8, chans), F32)],
             flops=work // 4,
         )
@@ -342,12 +342,12 @@
 
     pieces1 = gather(weight_first)
     pieces2 = gather(weight_second)
-    sums, hx, hd = call(sums_kernel, [info, lat, tan], [small, edge, edge], flops=work // 4)
+    sums, hx, hd, matrix = call(sums_kernel, [info, lat, tan], [small, edge, edge, ((chans, chans), BF)], flops=work // 4)
     middle, sums, hx, hd = block(
-        1, [lat, tan], gain_first, sums, hx, hd, pieces1, [], [((rows, 2, cols, chans), BF), small, edge, edge]
+        1, [lat, tan], matrix, gain_first, sums, hx, hd, pieces1, [], [((rows, 2, cols, chans), BF), small, edge, edge]
     )
     out = ((rows, cols, chans), BF)
-    result, dresult = block(2, [middle], gain_second, sums, hx, hd, pieces2, [lat, tan], [out, out])
+    result, dresult = block(2, [middle], matrix, gain_second, sums, hx, hd, pieces2, [lat, tan], [out, out])
     return result[None], dresult[None]
 
 

time: 114 us -> 116 us (1.018)
  starting transfers between devices: 26.3 us -> 28.4 us
    ppermute x22, starting transfers between devices: 26.3 us -> 28.4 us  [permute(): return lax.ppermute(x, AXES, pairs)]
  transfers between devices with their start and end apart: 22 -> 22, of which waited for: 8 -> 7; matrix products, arithmetic and copies ran while one was open for 1% -> 1% of each run, Pallas kernels for 26% -> 26%
where the time goes in v3:
time: 116 us
  waiting for transfers between devices  50.2 us (43%)
  Pallas kernels  33.8 us (29%)
  starting transfers between devices  28.4 us (24%)
  local copies, waits for them, and re-layouts  2.56 us (2%)
    ppermute x22, waiting for transfers between devices, permute(): return lax.ppermute(x, AXES, pairs)  50.2 us
    pallas_call x7, Pallas kernels, call(): pl.pallas_call(kernel, out_shape=tuple((jax.ShapeDtypeStruct(s, d) for s,...  33.8 us
    ppermute x22, starting transfers between devices, permute(): return lax.ppermute(x, AXES, pairs)  28.4 us
    dynamic_slice x2, local copies, waits for them, and re-layouts, gather(): part = lax.dynamic_slice_in_dim(w, half * core, half, axis=1)  2.43 us
  transfers between devices with their start and end apart: 22, of which 7 were waited for; matrix products, arithmetic and copies ran while one was open for 1% of the time, Pallas kernels for 26%

profile of v3, /device:TPU:0, one launch (start us, length us, event | category | flops | bytes accessed | tf_op | source)
XLA Modules:
  0.0 116.0 jit_solution(12820830369913038559)
XLA Ops:
  0.6 0.0 copy-start.3
  0.6 0.0 copy-start
  0.7 0.0 copy-start.1
  0.7 1.4 %dynamic-slice_bitcast_fusion.1 = bf16[9,80,640]{2,1,0:T(8,128)(2,1)S(1)} fusion(bf16[9,640,160]{1,2,0:T(8,128)(2,1)} %param.9, s32[]{:T(128)S(6)} %select_n.27), kind=kLoop, calls=%fused_computation.1 | loop fusion | bytes 1843204 | tf_op jit(solution)/shard_map/dynamic_slice | solution.py:282
  2.1 0.0 copy-start.5
  2.1 3.0 %collective-permute-start.3 = (bf16[9,80,640]{2,1,0:T(8,128)(2,1)S(1)}, bf16[9,80,640]{2,1,0:T(8,128)(2,1)}, u32[]{:S(2)}, u32[]{:S(2)}) collective-permute-start(bf16[9,80,640]{2,1,0:T(8,128)(2,1)S(1)} %dynamic-slice_bitcast_fusion.1), channel_id=1, source_target_pairs={{0,1},{1,0},{2,3},{3,2},{4,6},{5,7},{6,4},{7,5},{8,10},{9,11},{10,... | collective-permute-start | bytes 2764808 | tf_op jit(solution)/shard_map/ppermute | solution.py:274
  5.2 0.0 copy-done.3
  5.2 1.0 dynamic-slice_bitcast_fusion
  6.2 0.2 collective-permute-start.14
  6.4 10.3 %collective-permute-done.3.refs_1_ = bf16[9,80,640]{2,1,0:T(8,128)(2,1)} collective-permute-done((bf16[9,80,640]{2,1,0:T(8,128)(2,1)S(1)}, bf16[9,80,640]{2,1,0:T(8,128)(2,1)}, u32[]{:S(2)}, u32[]{:S(2)}) %collective-permute-start.3) | collective-permute-done | bytes 921632 | tf_op jit(solution)/shard_map/ppermute | solution.py:274
  16.7 2.0 %collective-permute-start.5 = (bf16[9,80,640]{2,1,0:T(8,128)(2,1)}, bf16[9,80,640]{2,1,0:T(8,128)(2,1)}, u32[]{:S(2)}, u32[]{:S(2)}) collective-permute-start(bf16[9,80,640]{2,1,0:T(8,128)(2,1)} %collective-permute-done.3.refs_1_), channel_id=1, source_target_pairs={{0,2},{1,3},{2,0},{3,1},{4,5},{5,4},{6,7},{7,6},{8,9},{9,8},{10,11... | collective-permute-start | bytes 2764808 | tf_op jit(solution)/shard_map/ppermute | solution.py:274
  18.7 1.5 %collective-permute-start.7 = (bf16[9,80,640]{2,1,0:T(8,128)(2,1)}, bf16[9,80,640]{2,1,0:T(8,128)(2,1)}, u32[]{:S(2)}, u32[]{:S(2)}) collective-permute-start(bf16[9,80,640]{2,1,0:T(8,128)(2,1)} %collective-permute-done.3.refs_1_), channel_id=1, source_target_pairs={{0,8},{1,9},{2,10},{3,11},{4,12},{5,13},{6,14},{7,15},{8,0},{9,1},... | collective-permute-start | bytes 2764808 | tf_op jit(solution)/shard_map/ppermute | solution.py:274
  20.3 0.1 stack.51.info
  20.4 0.0 copy-done
  20.4 0.0 copy-done.1
  20.4 1.5 %shard_map.77 = (bf16[16,640]{1,0:T(8,128)(2,1)S(1)}, bf16[2,128,640]{2,1,0:T(8,128)(2,1)S(1)}, bf16[2,128,640]{2,1,0:T(8,128)(2,1)S(1)}, bf16[640,640]{1,0:T(8,128)(2,1)S(1)}) custom-call(s32[10]{0:T(128)S(1)} %stack.51.info, bf16[4,128,640]{2,1,0:T(8,128)(2,1)S(1)} %bitcast.20, bf16[4,128,640]{2,1,0:T(8,128)(2,1)S(1)} %bitcast.23), custom_call_target="tpu_custom_call" | custom-call | flops 629145600 | tf_op jit(solution)/shard_map/pallas_call | solution.py:245
  21.9 0.6 collective-permute-start
  22.5 1.5 %collective-permute-start.1 = (bf16[16,640]{1,0:T(8,128)(2,1)S(1)}, bf16[16,640]{1,0:T(8,128)(2,1)S(1)}, u32[]{:S(2)}, u32[]{:S(2)}) collective-permute-start(bf16[16,640]{1,0:T(8,128)(2,1)S(1)} %get-tuple-element.22.refs_2_), channel_id=1, source_target_pairs={{0,2},{1,3},{2,0},{3,1},{4,6},{5,7},{6,4},{7,5},{8,10},{9,11},{10,... | collective-permute-start | bytes 61448 | tf_op jit(solution)/shard_map/ppermute | solution.py:274
  24.0 10.6 %collective-permute-done.refs_3_ = bf16[16,640]{1,0:T(8,128)(2,1)S(1)} collective-permute-done((bf16[16,640]{1,0:T(8,128)(2,1)S(1)}, bf16[16,640]{1,0:T(8,128)(2,1)S(1)}, u32[]{:S(2)}, u32[]{:S(2)}) %collective-permute-start) | collective-permute-done | bytes 20512 | tf_op jit(solution)/shard_map/ppermute | solution.py:274
  34.6 3.3 %collective-permute-start.2 = (bf16[16,640]{1,0:T(8,128)(2,1)S(1)}, bf16[16,640]{1,0:T(8,128)(2,1)S(1)}, u32[]{:S(2)}, u32[]{:S(2)}) collective-permute-start(bf16[16,640]{1,0:T(8,128)(2,1)S(1)} %get-tuple-element.22.refs_2_), channel_id=1, source_target_pairs={{0,3},{1,2},{2,1},{3,0},{4,7},{5,6},{6,5},{7,4},{8,11},{9,10},{10,... | collective-permute-start | bytes 61448 | tf_op jit(solution)/shard_map/ppermute | solution.py:274
  37.8 0.0 collective-permute-done.1.refs_4_
  37.8 1.8 %collective-permute-start.4 = (bf16[9,80,640]{2,1,0:T(8,128)(2,1)}, bf16[9,80,640]{2,1,0:T(8,128)(2,1)S(1)}, u32[]{:S(2)}, u32[]{:S(2)}) collective-permute-start(bf16[9,80,640]{2,1,0:T(8,128)(2,1)} %collective-permute-done.3.refs_1_), channel_id=1, source_target_pairs={{0,4},{1,5},{2,6},{3,7},{4,0},{5,1},{6,2},{7,3},{8,12},{9,13},{10,... | collective-permute-start | bytes 2764808 | tf_op jit(solution)/shard_map/ppermute | solution.py:274
  39.7 0.0 collective-permute-done.14.refs_1_
  39.7 0.5 collective-permute-start.16
  40.2 0.0 collective-permute-done.2.refs_5_
  40.2 2.4 %collective-permute-start.18 = (bf16[9,80,640]{2,1,0:T(8,128)(2,1)}, bf16[9,80,640]{2,1,0:T(8,128)(2,1)S(1)}, u32[]{:S(2)}, u32[]{:S(2)}) collective-permute-start(bf16[9,80,640]{2,1,0:T(8,128)(2,1)} %collective-permute-done.14.refs_1_), channel_id=1, source_target_pairs={{0,8},{1,9},{2,10},{3,11},{4,12},{5,13},{6,14},{7,15},{8,0},{9,1},... | collective-permute-start | bytes 2764808 | tf_op jit(solution)/shard_map/ppermute | solution.py:274
  42.6 0.0 collective-permute-done.5.refs_3_
  42.6 0.0 collective-permute-start.6
  42.6 0.0 collective-permute-done.7.refs_5_
  42.6 0.5 collective-permute-start.8
  43.1 0.0 collective-permute-done.4.refs_2_
  43.2 0.1 collective-permute-start.15
  43.2 10.1 %collective-permute-done.16.refs_3_ = bf16[9,80,640]{2,1,0:T(8,128)(2,1)S(1)} collective-permute-done((bf16[9,80,640]{2,1,0:T(8,128)(2,1)}, bf16[9,80,640]{2,1,0:T(8,128)(2,1)S(1)}, u32[]{:S(2)}, u32[]{:S(2)}) %collective-permute-start.16) | collective-permute-done | bytes 921632 | tf_op jit(solution)/shard_map/ppermute | solution.py:274
  53.3 0.0 collective-permute-start.17
  53.3 10.1 %collective-permute-done.18.refs_5_ = bf16[9,80,640]{2,1,0:T(8,128)(2,1)S(1)} collective-permute-done((bf16[9,80,640]{2,1,0:T(8,128)(2,1)}, bf16[9,80,640]{2,1,0:T(8,128)(2,1)S(1)}, u32[]{:S(2)}, u32[]{:S(2)}) %collective-permute-start.18) | collective-permute-done | bytes 921632 | tf_op jit(solution)/shard_map/ppermute | solution.py:274
  63.4 0.0 collective-permute-start.19
  63.4 0.0 copy-done.5
  63.4 2.5 %shard_map.78 = (bf16[4,2,128,1920]{3,2,1,0:T(8,128)(2,1)S(1)}, f32[8,640]{1,0:T(8,128)S(1)}) custom-call(bf16[4,128,640]{2,1,0:T(8,128)(2,1)S(1)} %bitcast.21, bf16[4,128,640]{2,1,0:T(8,128)(2,1)S(1)} %bitcast.24, bf16[16,640]{1,0:T(8,128)(2,1)S(1)} %get-tuple-element.22.refs_2_, bf16[16,640]{1,0:T(8,128)(2,1)S(1)} %collective-permute-done.refs_3_, ...), custom_call_target="tpu_custom_call" | custom-call | flops 629145600 | tf_op jit(solution)/shard_map/pallas_call | solution.py:245
  65.9 0.0 collective-permute-done.6.refs_4_
  65.9 0.9 collective-permute-start.10
  66.8 0.0 collective-permute-done.8.refs_6_
  66.8 4.5 %collective-permute-start.9 = (bf16[2,128,640]{2,1,0:T(8,128)(2,1)S(1)}, bf16[2,128,640]{2,1,0:T(8,128)(2,1)S(1)}, u32[]{:S(2)}, u32[]{:S(2)}) collective-permute-start(bf16[2,128,640]{2,1,0:T(8,128)(2,1)S(1)} %get-tuple-element.28), channel_id=1, source_target_pairs={{0,1},{1,0},{2,3},{3,2},{4,5},{5,4},{6,7},{7,6},{8,9},{9,8},{10,11... | collective-permute-start | bytes 983048 | tf_op jit(solution)/shard_map/ppermute | solution.py:274
  71.3 0.0 copy-done.2
  71.3 10.4 %shard_map.79 = (f32[4,2,128,640]{3,2,1,0:T(8,128)S(1)}, bf16[640,1920]{1,0:T(8,128)(2,1)S(1)}, bf16[640,1920]{1,0:T(8,128)(2,1)S(1)}) custom-call(s32[10]{0:T(128)S(1)} %stack.51.info, bf16[4,2,128,1920]{3,2,1,0:T(8,128)(2,1)S(1)} %get-tuple-element.24.xs, bf16[9,160,640]{2,1,0:T(8,128)(2,1)S(1)} %bitcast.26, ...), custom_call_target="tpu_custom_call" | custom-call | flops 5033164800 | tf_op jit(solution)/shard_map/pallas_call | solution.py:245
  81.6 0.0 collective-permute-done.10.hd
  81.6 4.5 %collective-permute-done.9.hx = bf16[2,128,640]{2,1,0:T(8,128)(2,1)S(1)} collective-permute-done((bf16[2,128,640]{2,1,0:T(8,128)(2,1)S(1)}, bf16[2,128,640]{2,1,0:T(8,128)(2,1)S(1)}, u32[]{:S(2)}, u32[]{:S(2)}) %collective-permute-start.9) | collective-permute-done | bytes 327712 | tf_op jit(solution)/shard_map/ppermute | solution.py:274
  86.1 3.2 %shard_map.80 = (bf16[4,2,128,640]{3,2,1,0:T(8,128)(2,1)S(1)}, bf16[16,640]{1,0:T(8,128)(2,1)S(1)}, bf16[2,128,640]{2,1,0:T(8,128)(2,1)S(1)}, bf16[2,128,640]{2,1,0:T(8,128)(2,1)S(1)}) custom-call(s32[10]{0:T(128)S(1)} %stack.51.info, f32[4,2,128,640]{3,2,1,0:T(8,128)S(1)} %get-tuple-element.25.acc, bf16[640,1920]{1,0:T(8,128)(2,1)S(1)} %get-tuple-element.26.w0, ...), custom_call_target="tpu_custom_call" | custom-call | flops 2516582400 | tf_op jit(solution)/shard_map/pallas_call | solution.py:245
  89.3 0.1 collective-permute-start.11
  89.4 2.0 %collective-permute-start.12 = (bf16[16,640]{1,0:T(8,128)(2,1)S(1)}, bf16[16,640]{1,0:T(8,128)(2,1)S(1)}, u32[]{:S(2)}, u32[]{:S(2)}) collective-permute-start(bf16[16,640]{1,0:T(8,128)(2,1)S(1)} %get-tuple-element.32.refs_1_), channel_id=1, source_target_pairs={{0,2},{1,3},{2,0},{3,1},{4,6},{5,7},{6,4},{7,5},{8,10},{9,11},{10,... | collective-permute-start | bytes 61448 | tf_op jit(solution)/shard_map/ppermute | solution.py:274
  91.4 1.8 %collective-permute-done.11.refs_2_ = bf16[16,640]{1,0:T(8,128)(2,1)S(1)} collective-permute-done((bf16[16,640]{1,0:T(8,128)(2,1)S(1)}, bf16[16,640]{1,0:T(8,128)(2,1)S(1)}, u32[]{:S(2)}, u32[]{:S(2)}) %collective-permute-start.11) | collective-permute-done | bytes 20512 | tf_op jit(solution)/shard_map/ppermute | solution.py:274
  93.2 1.4 %collective-permute-start.13 = (bf16[16,640]{1,0:T(8,128)(2,1)S(1)}, bf16[16,640]{1,0:T(8,128)(2,1)S(1)}, u32[]{:S(2)}, u32[]{:S(2)}) collective-permute-start(bf16[16,640]{1,0:T(8,128)(2,1)S(1)} %get-tuple-element.32.refs_1_), channel_id=1, source_target_pairs={{0,3},{1,2},{2,1},{3,0},{4,7},{5,6},{6,5},{7,4},{8,11},{9,10},{10,... | collective-permute-start | bytes 61448 | tf_op jit(solution)/shard_map/ppermute | solution.py:274
  94.6 0.0 collective-permute-done.12.refs_3_
  94.6 0.6 collective-permute-start.20
  95.2 2.9 %collective-permute-done.13.refs_4_ = bf16[16,640]{1,0:T(8,128)(2,1)S(1)} collective-permute-done((bf16[16,640]{1,0:T(8,128)(2,1)S(1)}, bf16[16,640]{1,0:T(8,128)(2,1)S(1)}, u32[]{:S(2)}, u32[]{:S(2)}) %collective-permute-start.13) | collective-permute-done | bytes 20512 | tf_op jit(solution)/shard_map/ppermute | solution.py:274
  98.1 1.4 %collective-permute-start.21 = (bf16[2,128,640]{2,1,0:T(8,128)(2,1)S(1)}, bf16[2,128,640]{2,1,0:T(8,128)(2,1)S(1)}, u32[]{:S(2)}, u32[]{:S(2)}) collective-permute-start(bf16[2,128,640]{2,1,0:T(8,128)(2,1)S(1)} %get-tuple-element.38), channel_id=1, source_target_pairs={{0,3},{1,2},{2,1},{3,0},{4,7},{5,6},{6,5},{7,4},{8,11},{9,10},{10,... | collective-permute-start | bytes 983048 | tf_op jit(solution)/shard_map/ppermute | solution.py:274
  99.5 2.5 %shard_map.81 = (bf16[4,2,128,1920]{3,2,1,0:T(8,128)(2,1)S(1)}, f32[8,640]{1,0:T(8,128)S(1)}) custom-call(bf16[4,2,128,640]{3,2,1,0:T(8,128)(2,1)S(1)} %get-tuple-element.31.refs_0_, bf16[16,640]{1,0:T(8,128)(2,1)S(1)} %get-tuple-element.32.refs_1_, bf16[16,640]{1,0:T(8,128)(2,1)S(1)} %collective-permute-done.11.refs_2_, ...), custom_call_target="tpu_custom_call" | custom-call | flops 629145600 | tf_op jit(solution)/shard_map/pallas_call | solution.py:245
  102.0 0.0 collective-permute-done.15.refs_2_
  102.0 0.0 collective-permute-done.17.refs_4_
  102.0 0.0 collective-permute-done.19.refs_6_
  102.1 0.0 copy-done.4
  102.1 10.0 %shard_map.82 = (f32[4,2,128,640]{3,2,1,0:T(8,128)S(1)}, bf16[640,1920]{1,0:T(8,128)(2,1)S(1)}, bf16[640,1920]{1,0:T(8,128)(2,1)S(1)}) custom-call(s32[10]{0:T(128)S(1)} %stack.51.info, bf16[4,2,128,1920]{3,2,1,0:T(8,128)(2,1)S(1)} %get-tuple-element.33.xs, bf16[9,160,640]{2,1,0:T(8,128)(2,1)S(1)} %bitcast.27, ...), custom_call_target="tpu_custom_call" | custom-call | flops 5033164800 | tf_op jit(solution)/shard_map/pallas_call | solution.py:245
  112.1 0.0 collective-permute-done.20.hx
  112.1 0.0 collective-permute-done.21.hd
  112.1 3.7 %shard_map.83 = (bf16[4,128,640]{2,1,0:T(8,128)(2,1)}, bf16[4,128,640]{2,1,0:T(8,128)(2,1)}) custom-call(s32[10]{0:T(128)S(1)} %stack.51.info, f32[4,2,128,640]{3,2,1,0:T(8,128)S(1)} %get-tuple-element.34.acc, bf16[640,1920]{1,0:T(8,128)(2,1)S(1)} %get-tuple-element.35.w0, bf16[640,1920]{1,0:T(8,128)(2,1)S(1)} %get-tuple-element.36.w2, ...), custom_call_target="tpu_custom_call" | custom-call | flops 2516582400 | tf_op jit(solution)/shard_map/pallas_call | solution.py:245
  (6 shorter events, 0.0 us)
Async XLA Ops:
  0.6 4.5 %copy-start.3 = (bf16[9,640,160]{1,2,0:T(8,128)(2,1)S(1)}, bf16[9,640,160]{1,2,0:T(8,128)(2,1)}, u32[]{:S(2)}) copy-start(bf16[9,640,160]{1,2,0:T(8,128)(2,1)} %param.11) | copy-start | bytes 5529604
  0.6 19.7 %copy-start = (bf16[1,4,128,640]{3,2,1,0:T(8,128)(2,1)S(1)}, bf16[1,4,128,640]{3,2,1,0:T(8,128)(2,1)}, u32[]{:S(2)}) copy-start(bf16[1,4,128,640]{3,2,1,0:T(8,128)(2,1)} %param.6) | copy-start | bytes 1966084
  0.7 19.7 %copy-start.1 = (bf16[1,4,128,640]{3,2,1,0:T(8,128)(2,1)S(1)}, bf16[1,4,128,640]{3,2,1,0:T(8,128)(2,1)}, u32[]{:S(2)}) copy-start(bf16[1,4,128,640]{3,2,1,0:T(8,128)(2,1)} %param.7) | copy-start | bytes 1966084
  2.1 61.3 %copy-start.5 = (f32[640]{0:T(1024)S(1)}, f32[640]{0:T(1024)}, u32[]{:S(2)}) copy-start(f32[640]{0:T(1024)} %param.8) | copy-start | bytes 7684
  2.1 14.6 %collective-permute-start.3 = (bf16[9,80,640]{2,1,0:T(8,128)(2,1)S(1)}, bf16[9,80,640]{2,1,0:T(8,128)(2,1)}, u32[]{:S(2)}, u32[]{:S(2)}) collective-permute-start(bf16[9,80,640]{2,1,0:T(8,128)(2,1)S(1)} %dynamic-slice_bitcast_fusion.1), channel_id=1, source_target_pairs={{0,1},{1,0},{2,3},{3,2},{4,6},{5,7},{6,4},{7,5},{8,10},{9,11},{10,... | collective-permute-start | bytes 2764808 | tf_op jit(solution)/shard_map/ppermute | solution.py:274
  6.2 65.1 %copy-start.2 = (bf16[9,640,160]{1,2,0:T(8,128)(2,1)S(1)}, bf16[9,640,160]{1,2,0:T(8,128)(2,1)}, u32[]{:S(2)}) copy-start(bf16[9,640,160]{1,2,0:T(8,128)(2,1)} %param.9) | copy-start | bytes 5529604
  6.2 33.5 %collective-permute-start.14 = (bf16[9,80,640]{2,1,0:T(8,128)(2,1)}, bf16[9,80,640]{2,1,0:T(8,128)(2,1)}, u32[]{:S(2)}, u32[]{:S(2)}) collective-permute-start(bf16[9,80,640]{2,1,0:T(8,128)(2,1)} %dynamic-slice_bitcast_fusion), channel_id=1, source_target_pairs={{0,1},{1,0},{2,3},{3,2},{4,6},{5,7},{6,4},{7,5},{8,10},{9,11},{10,... | collective-permute-start | bytes 2764808 | tf_op jit(solution)/shard_map/ppermute | solution.py:274
  16.7 26.0 %collective-permute-start.5 = (bf16[9,80,640]{2,1,0:T(8,128)(2,1)}, bf16[9,80,640]{2,1,0:T(8,128)(2,1)}, u32[]{:S(2)}, u32[]{:S(2)}) collective-permute-start(bf16[9,80,640]{2,1,0:T(8,128)(2,1)} %collective-permute-done.3.refs_1_), channel_id=1, source_target_pairs={{0,2},{1,3},{2,0},{3,1},{4,5},{5,4},{6,7},{7,6},{8,9},{9,8},{10,11... | collective-permute-start | bytes 2764808 | tf_op jit(solution)/shard_map/ppermute | solution.py:274
  18.7 23.9 %collective-permute-start.7 = (bf16[9,80,640]{2,1,0:T(8,128)(2,1)}, bf16[9,80,640]{2,1,0:T(8,128)(2,1)}, u32[]{:S(2)}, u32[]{:S(2)}) collective-permute-start(bf16[9,80,640]{2,1,0:T(8,128)(2,1)} %collective-permute-done.3.refs_1_), channel_id=1, source_target_pairs={{0,8},{1,9},{2,10},{3,11},{4,12},{5,13},{6,14},{7,15},{8,0},{9,1},... | collective-permute-start | bytes 2764808 | tf_op jit(solution)/shard_map/ppermute | solution.py:274
  21.9 12.7 %collective-permute-start = (bf16[16,640]{1,0:T(8,128)(2,1)S(1)}, bf16[16,640]{1,0:T(8,128)(2,1)S(1)}, u32[]{:S(2)}, u32[]{:S(2)}) collective-permute-start(bf16[16,640]{1,0:T(8,128)(2,1)S(1)} %get-tuple-element.22.refs_2_), channel_id=1, source_target_pairs={{0,1},{1,0},{2,3},{3,2},{4,5},{5,4},{6,7},{7,6},{8,9},{9,8},{10,11... | collective-permute-start | bytes 61448 | tf_op jit(solution)/shard_map/ppermute | solution.py:274
  22.5 15.4 %collective-permute-start.1 = (bf16[16,640]{1,0:T(8,128)(2,1)S(1)}, bf16[16,640]{1,0:T(8,128)(2,1)S(1)}, u32[]{:S(2)}, u32[]{:S(2)}) collective-permute-start(bf16[16,640]{1,0:T(8,128)(2,1)S(1)} %get-tuple-element.22.refs_2_), channel_id=1, source_target_pairs={{0,2},{1,3},{2,0},{3,1},{4,6},{5,7},{6,4},{7,5},{8,10},{9,11},{10,... | collective-permute-start | bytes 61448 | tf_op jit(solution)/shard_map/ppermute | solution.py:274
  34.6 5.6 %collective-permute-start.2 = (bf16[16,640]{1,0:T(8,128)(2,1)S(1)}, bf16[16,640]{1,0:T(8,128)(2,1)S(1)}, u32[]{:S(2)}, u32[]{:S(2)}) collective-permute-start(bf16[16,640]{1,0:T(8,128)(2,1)S(1)} %get-tuple-element.22.refs_2_), channel_id=1, source_target_pairs={{0,3},{1,2},{2,1},{3,0},{4,7},{5,6},{6,5},{7,4},{8,11},{9,10},{10,... | collective-permute-start | bytes 61448 | tf_op jit(solution)/shard_map/ppermute | solution.py:274
  37.8 5.3 %collective-permute-start.4 = (bf16[9,80,640]{2,1,0:T(8,128)(2,1)}, bf16[9,80,640]{2,1,0:T(8,128)(2,1)S(1)}, u32[]{:S(2)}, u32[]{:S(2)}) collective-permute-start(bf16[9,80,640]{2,1,0:T(8,128)(2,1)} %collective-permute-done.3.refs_1_), channel_id=1, source_target_pairs={{0,4},{1,5},{2,6},{3,7},{4,0},{5,1},{6,2},{7,3},{8,12},{9,13},{10,... | collective-permute-start | bytes 2764808 | tf_op jit(solution)/shard_map/ppermute | solution.py:274
  39.7 13.6 %collective-permute-start.16 = (bf16[9,80,640]{2,1,0:T(8,128)(2,1)}, bf16[9,80,640]{2,1,0:T(8,128)(2,1)S(1)}, u32[]{:S(2)}, u32[]{:S(2)}) collective-permute-start(bf16[9,80,640]{2,1,0:T(8,128)(2,1)} %collective-permute-done.14.refs_1_), channel_id=1, source_target_pairs={{0,2},{1,3},{2,0},{3,1},{4,5},{5,4},{6,7},{7,6},{8,9},{9,8},{10,11... | collective-permute-start | bytes 2764808 | tf_op jit(solution)/shard_map/ppermute | solution.py:274
  40.2 23.2 %collective-permute-start.18 = (bf16[9,80,640]{2,1,0:T(8,128)(2,1)}, bf16[9,80,640]{2,1,0:T(8,128)(2,1)S(1)}, u32[]{:S(2)}, u32[]{:S(2)}) collective-permute-start(bf16[9,80,640]{2,1,0:T(8,128)(2,1)} %collective-permute-done.14.refs_1_), channel_id=1, source_target_pairs={{0,8},{1,9},{2,10},{3,11},{4,12},{5,13},{6,14},{7,15},{8,0},{9,1},... | collective-permute-start | bytes 2764808 | tf_op jit(solution)/shard_map/ppermute | solution.py:274
  42.6 23.3 %collective-permute-start.6 = (bf16[9,80,640]{2,1,0:T(8,128)(2,1)}, bf16[9,80,640]{2,1,0:T(8,128)(2,1)S(1)}, u32[]{:S(2)}, u32[]{:S(2)}) collective-permute-start(bf16[9,80,640]{2,1,0:T(8,128)(2,1)} %collective-permute-done.5.refs_3_), channel_id=1, source_target_pairs={{0,4},{1,5},{2,6},{3,7},{4,0},{5,1},{6,2},{7,3},{8,12},{9,13},{10,... | collective-permute-start | bytes 2764808 | tf_op jit(solution)/shard_map/ppermute | solution.py:274
  42.6 24.1 %collective-permute-start.8 = (bf16[9,80,640]{2,1,0:T(8,128)(2,1)}, bf16[9,80,640]{2,1,0:T(8,128)(2,1)S(1)}, u32[]{:S(2)}, u32[]{:S(2)}) collective-permute-start(bf16[9,80,640]{2,1,0:T(8,128)(2,1)} %collective-permute-done.7.refs_5_), channel_id=1, source_target_pairs={{0,4},{1,5},{2,6},{3,7},{4,0},{5,1},{6,2},{7,3},{8,12},{9,13},{10,... | collective-permute-start | bytes 2764808 | tf_op jit(solution)/shard_map/ppermute | solution.py:274
  43.2 58.9 %collective-permute-start.15 = (bf16[9,80,640]{2,1,0:T(8,128)(2,1)}, bf16[9,80,640]{2,1,0:T(8,128)(2,1)S(1)}, u32[]{:S(2)}, u32[]{:S(2)}) collective-permute-start(bf16[9,80,640]{2,1,0:T(8,128)(2,1)} %collective-permute-done.14.refs_1_), channel_id=1, source_target_pairs={{0,4},{1,5},{2,6},{3,7},{4,0},{5,1},{6,2},{7,3},{8,12},{9,13},{10,... | collective-permute-start | bytes 2764808 | tf_op jit(solution)/shard_map/ppermute | solution.py:274
  53.3 48.7 %collective-permute-start.17 = (bf16[9,80,640]{2,1,0:T(8,128)(2,1)S(1)}, bf16[9,80,640]{2,1,0:T(8,128)(2,1)S(1)}, u32[]{:S(2)}, u32[]{:S(2)}) collective-permute-start(bf16[9,80,640]{2,1,0:T(8,128)(2,1)S(1)} %collective-permute-done.16.refs_3_), channel_id=1, source_target_pairs={{0,4},{1,5},{2,6},{3,7},{4,0},{5,1},{6,2},{7,3},{8,12},{9,13},{10,... | collective-permute-start | bytes 2764808 | tf_op jit(solution)/shard_map/ppermute | solution.py:274
  63.4 38.6 %collective-permute-start.19 = (bf16[9,80,640]{2,1,0:T(8,128)(2,1)S(1)}, bf16[9,80,640]{2,1,0:T(8,128)(2,1)S(1)}, u32[]{:S(2)}, u32[]{:S(2)}) collective-permute-start(bf16[9,80,640]{2,1,0:T(8,128)(2,1)S(1)} %collective-permute-done.18.refs_5_), channel_id=1, source_target_pairs={{0,4},{1,5},{2,6},{3,7},{4,0},{5,1},{6,2},{7,3},{8,12},{9,13},{10,... | collective-permute-start | bytes 2764808 | tf_op jit(solution)/shard_map/ppermute | solution.py:274
  65.9 15.7 %collective-permute-start.10 = (bf16[2,128,640]{2,1,0:T(8,128)(2,1)S(1)}, bf16[2,128,640]{2,1,0:T(8,128)(2,1)S(1)}, u32[]{:S(2)}, u32[]{:S(2)}) collective-permute-start(bf16[2,128,640]{2,1,0:T(8,128)(2,1)S(1)} %get-tuple-element.29), channel_id=1, source_target_pairs={{1,2},{2,1},{5,6},{6,5},{9,10},{10,9},{13,14},{14,13},{17,18},{18,... | collective-permute-start | bytes 983048 | tf_op jit(solution)/shard_map/ppermute | solution.py:274
  66.8 19.3 %collective-permute-start.9 = (bf16[2,128,640]{2,1,0:T(8,128)(2,1)S(1)}, bf16[2,128,640]{2,1,0:T(8,128)(2,1)S(1)}, u32[]{:S(2)}, u32[]{:S(2)}) collective-permute-start(bf16[2,128,640]{2,1,0:T(8,128)(2,1)S(1)} %get-tuple-element.28), channel_id=1, source_target_pairs={{0,1},{1,0},{2,3},{3,2},{4,5},{5,4},{6,7},{7,6},{8,9},{9,8},{10,11... | collective-permute-start | bytes 983048 | tf_op jit(solution)/shard_map/ppermute | solution.py:274
  86.1 8.5 %copy-start.6 = (f32[640]{0:T(1024)S(1)}, f32[640]{0:T(1024)}, u32[]{:S(2)}) copy-start(f32[640]{0:T(1024)} %param.10) | copy-start | bytes 7684
  86.1 16.0 %copy-start.4 = (bf16[9,640,160]{1,2,0:T(8,128)(2,1)S(1)}, bf16[9,640,160]{1,2,0:T(8,128)(2,1)}, u32[]{:S(2)}) copy-start(bf16[9,640,160]{1,2,0:T(8,128)(2,1)} %param.11) | copy-start | bytes 5529604
  89.3 3.8 %collective-permute-start.11 = (bf16[16,640]{1,0:T(8,128)(2,1)S(1)}, bf16[16,640]{1,0:T(8,128)(2,1)S(1)}, u32[]{:S(2)}, u32[]{:S(2)}) collective-permute-start(bf16[16,640]{1,0:T(8,128)(2,1)S(1)} %get-tuple-element.32.refs_1_), channel_id=1, source_target_pairs={{0,1},{1,0},{2,3},{3,2},{4,5},{5,4},{6,7},{7,6},{8,9},{9,8},{10,11... | collective-permute-start | bytes 61448 | tf_op jit(solution)/shard_map/ppermute | solution.py:274
  89.4 5.2 %collective-permute-start.12 = (bf16[16,640]{1,0:T(8,128)(2,1)S(1)}, bf16[16,640]{1,0:T(8,128)(2,1)S(1)}, u32[]{:S(2)}, u32[]{:S(2)}) collective-permute-start(bf16[16,640]{1,0:T(8,128)(2,1)S(1)} %get-tuple-element.32.refs_1_), channel_id=1, source_target_pairs={{0,2},{1,3},{2,0},{3,1},{4,6},{5,7},{6,4},{7,5},{8,10},{9,11},{10,... | collective-permute-start | bytes 61448 | tf_op jit(solution)/shard_map/ppermute | solution.py:274
  93.2 4.9 %collective-permute-start.13 = (bf16[16,640]{1,0:T(8,128)(2,1)S(1)}, bf16[16,640]{1,0:T(8,128)(2,1)S(1)}, u32[]{:S(2)}, u32[]{:S(2)}) collective-permute-start(bf16[16,640]{1,0:T(8,128)(2,1)S(1)} %get-tuple-element.32.refs_1_), channel_id=1, source_target_pairs={{0,3},{1,2},{2,1},{3,0},{4,7},{5,6},{6,5},{7,4},{8,11},{9,10},{10,... | collective-permute-start | bytes 61448 | tf_op jit(solution)/shard_map/ppermute | solution.py:274
  94.6 17.4 %collective-permute-start.20 = (bf16[2,128,640]{2,1,0:T(8,128)(2,1)S(1)}, bf16[2,128,640]{2,1,0:T(8,128)(2,1)S(1)}, u32[]{:S(2)}, u32[]{:S(2)}) collective-permute-start(bf16[2,128,640]{2,1,0:T(8,128)(2,1)S(1)} %get-tuple-element.37), channel_id=1, source_target_pairs={{0,1},{1,0},{2,3},{3,2},{4,5},{5,4},{6,7},{7,6},{8,9},{9,8},{10,11... | collective-permute-start | bytes 983048 | tf_op jit(solution)/shard_map/ppermute | solution.py:274
  98.1 14.0 %collective-permute-start.21 = (bf16[2,128,640]{2,1,0:T(8,128)(2,1)S(1)}, bf16[2,128,640]{2,1,0:T(8,128)(2,1)S(1)}, u32[]{:S(2)}, u32[]{:S(2)}) collective-permute-start(bf16[2,128,640]{2,1,0:T(8,128)(2,1)S(1)} %get-tuple-element.38), channel_id=1, source_target_pairs={{0,3},{1,2},{2,1},{3,0},{4,7},{5,6},{6,5},{7,4},{8,11},{9,10},{10,... | collective-permute-start | bytes 983048 | tf_op jit(solution)/shard_map/ppermute | solution.py:274

commit v4 on v3

--- a/solution.py
+++ b/solution.py
@@ -14,6 +14,7 @@
 BF = jnp.bfloat16
 F32 = jnp.float32
 STAT_ROWS = 16
+BLOCK = 256
 VMEM_LIMIT = 18 * 1024 * 1024
 
 
@@ -174,15 +175,24 @@
 
 def main_kernel(info, xs, *refs):
     pieces = refs[:7]
-    acc, w0, w2, w1 = refs[7:]
-    rows = xs.shape[0]
+    acc, w0, w2, w1, pair = refs[7:]
+    rows, chans = xs.shape[0], acc.shape[3]
+    block = pair.shape[0]
+    full = chans // block * block
+    tail = chans - full
     for p, wv in ((1, w1), (0, w0), (2, w2)):
         for k, piece in enumerate(pieces):
             fill(wv, piece, 3 * p, info[OFFSETS + k])
+        part = wv.at[0:full]
         if p == 1:
-            acc[...] = rows_product(xs, 0, rows, wv)
+            acc[..., 0:full] = rows_product(xs, 0, rows, part)
+            pair[0:tail] = wv[full:chans]
         elif p == 0:
-            acc[1:rows] = acc[1:rows] + rows_product(xs, 0, rows - 1, wv)
+            acc[1:rows, :, :, 0:full] = acc[1:rows, :, :, 0:full] + rows_product(xs, 0, rows - 1, part)
+            pair[tail : 2 * tail] = wv[full:chans]
+            both = rows_product(xs, 0, rows, pair.at[0 : 2 * tail])
+            acc[..., full:chans] = both[..., 0:tail]
+            acc[1:rows, :, :, full:chans] = acc[1:rows, :, :, full:chans] + both[0 : rows - 1, :, :, tail : 2 * tail]
         else:
             acc[0 : rows - 1] = acc[0 : rows - 1] + rows_product(xs, 1, rows - 1, wv)
 
@@ -330,7 +340,7 @@
             [wide, ((8, chans), F32)],
             flops=work // 4,
         )
-        acc, w0, w2 = call(main_kernel, [info, xs, *pieces], [acc_t, wrow, wrow], [pltpu.VMEM(*wrow)], flops=2 * work)
+        acc, w0, w2 = call(main_kernel, [info, xs, *pieces], [acc_t, wrow, wrow], [pltpu.VMEM(*wrow), pltpu.VMEM((BLOCK, 3 * chans), BF)], flops=2 * work)
         halo = pltpu.VMEM((2, 2, cols, 3 * chans), BF)
         if k == 2:
             kernel, place = last_edge_kernel, HB

time: 116 us -> 116 us (level)
  Pallas kernels: 33.8 us -> 32.5 us
    pallas_call x7, Pallas kernels: 33.8 us -> 32.5 us  [call(): pl.pallas_call(kernel, out_shape=tuple((jax.ShapeDtypeStruct(s, d) for s,...]
  transfers between devices with their start and end apart: 22 -> 22, of which waited for: 7 -> 7; matrix products, arithmetic and copies ran while one was open for 1% -> 1% of each run, Pallas kernels for 26% -> 25%
where the time goes in v4:
time: 116 us; the launch traced here: 115 us
  waiting for transfers between devices  50.8 us (44%)
  Pallas kernels  32.5 us (28%)
  starting transfers between devices  28.4 us (24%)
  local copies, waits for them, and re-layouts  2.56 us (2%)
    ppermute x22, waiting for transfers between devices, permute(): return lax.ppermute(x, AXES, pairs)  50.8 us
    pallas_call x7, Pallas kernels, call(): pl.pallas_call(kernel, out_shape=tuple((jax.ShapeDtypeStruct(s, d) for s,...  32.5 us
    ppermute x22, starting transfers between devices, permute(): return lax.ppermute(x, AXES, pairs)  28.4 us
    dynamic_slice x2, local copies, waits for them, and re-layouts, gather(): part = lax.dynamic_slice_in_dim(w, half * core, half, axis=1)  2.43 us
  transfers between devices with their start and end apart: 22, of which 7 were waited for; matrix products, arithmetic and copies ran while one was open for 1% of the time, Pallas kernels for 25%

profile of v4, /device:TPU:0, one launch (start us, length us, event | category | flops | bytes accessed | tf_op | source)
XLA Modules:
  0.0 115.4 jit_solution(17389293604143444661)
XLA Ops:
  0.6 0.0 copy-start.3
  0.6 0.0 copy-start
  0.7 0.0 copy-start.1
  0.7 1.4 %dynamic-slice_bitcast_fusion.1 = bf16[9,80,640]{2,1,0:T(8,128)(2,1)S(1)} fusion(bf16[9,640,160]{1,2,0:T(8,128)(2,1)} %param.9, s32[]{:T(128)S(6)} %select_n.27), kind=kLoop, calls=%fused_computation.1 | loop fusion | bytes 1843204 | tf_op jit(solution)/shard_map/dynamic_slice | solution.py:292
  2.1 0.0 copy-start.5
  2.1 3.0 %collective-permute-start.3 = (bf16[9,80,640]{2,1,0:T(8,128)(2,1)S(1)}, bf16[9,80,640]{2,1,0:T(8,128)(2,1)}, u32[]{:S(2)}, u32[]{:S(2)}) collective-permute-start(bf16[9,80,640]{2,1,0:T(8,128)(2,1)S(1)} %dynamic-slice_bitcast_fusion.1), channel_id=1, source_target_pairs={{0,1},{1,0},{2,3},{3,2},{4,6},{5,7},{6,4},{7,5},{8,10},{9,11},{10,... | collective-permute-start | bytes 2764808 | tf_op jit(solution)/shard_map/ppermute | solution.py:284
  5.2 0.0 copy-done.3
  5.2 1.0 dynamic-slice_bitcast_fusion
  6.2 0.2 collective-permute-start.14
  6.4 10.3 %collective-permute-done.3.refs_1_ = bf16[9,80,640]{2,1,0:T(8,128)(2,1)} collective-permute-done((bf16[9,80,640]{2,1,0:T(8,128)(2,1)S(1)}, bf16[9,80,640]{2,1,0:T(8,128)(2,1)}, u32[]{:S(2)}, u32[]{:S(2)}) %collective-permute-start.3) | collective-permute-done | bytes 921632 | tf_op jit(solution)/shard_map/ppermute | solution.py:284
  16.7 2.0 %collective-permute-start.5 = (bf16[9,80,640]{2,1,0:T(8,128)(2,1)}, bf16[9,80,640]{2,1,0:T(8,128)(2,1)}, u32[]{:S(2)}, u32[]{:S(2)}) collective-permute-start(bf16[9,80,640]{2,1,0:T(8,128)(2,1)} %collective-permute-done.3.refs_1_), channel_id=1, source_target_pairs={{0,2},{1,3},{2,0},{3,1},{4,5},{5,4},{6,7},{7,6},{8,9},{9,8},{10,11... | collective-permute-start | bytes 2764808 | tf_op jit(solution)/shard_map/ppermute | solution.py:284
  18.7 1.5 %collective-permute-start.7 = (bf16[9,80,640]{2,1,0:T(8,128)(2,1)}, bf16[9,80,640]{2,1,0:T(8,128)(2,1)}, u32[]{:S(2)}, u32[]{:S(2)}) collective-permute-start(bf16[9,80,640]{2,1,0:T(8,128)(2,1)} %collective-permute-done.3.refs_1_), channel_id=1, source_target_pairs={{0,8},{1,9},{2,10},{3,11},{4,12},{5,13},{6,14},{7,15},{8,0},{9,1},... | collective-permute-start | bytes 2764808 | tf_op jit(solution)/shard_map/ppermute | solution.py:284
  20.3 0.1 stack.51.info
  20.4 0.0 copy-done
  20.4 0.0 copy-done.1
  20.4 1.5 %shard_map.77 = (bf16[16,640]{1,0:T(8,128)(2,1)S(1)}, bf16[2,128,640]{2,1,0:T(8,128)(2,1)S(1)}, bf16[2,128,640]{2,1,0:T(8,128)(2,1)S(1)}, bf16[640,640]{1,0:T(8,128)(2,1)S(1)}) custom-call(s32[10]{0:T(128)S(1)} %stack.51.info, bf16[4,128,640]{2,1,0:T(8,128)(2,1)S(1)} %bitcast.20, bf16[4,128,640]{2,1,0:T(8,128)(2,1)S(1)} %bitcast.23), custom_call_target="tpu_custom_call" | custom-call | flops 629145600 | tf_op jit(solution)/shard_map/pallas_call | solution.py:255
  21.9 0.6 collective-permute-start
  22.5 1.5 %collective-permute-start.1 = (bf16[16,640]{1,0:T(8,128)(2,1)S(1)}, bf16[16,640]{1,0:T(8,128)(2,1)S(1)}, u32[]{:S(2)}, u32[]{:S(2)}) collective-permute-start(bf16[16,640]{1,0:T(8,128)(2,1)S(1)} %get-tuple-element.22.refs_2_), channel_id=1, source_target_pairs={{0,2},{1,3},{2,0},{3,1},{4,6},{5,7},{6,4},{7,5},{8,10},{9,11},{10,... | collective-permute-start | bytes 61448 | tf_op jit(solution)/shard_map/ppermute | solution.py:284
  24.0 10.6 %collective-permute-done.refs_3_ = bf16[16,640]{1,0:T(8,128)(2,1)S(1)} collective-permute-done((bf16[16,640]{1,0:T(8,128)(2,1)S(1)}, bf16[16,640]{1,0:T(8,128)(2,1)S(1)}, u32[]{:S(2)}, u32[]{:S(2)}) %collective-permute-start) | collective-permute-done | bytes 20512 | tf_op jit(solution)/shard_map/ppermute | solution.py:284
  34.6 3.3 %collective-permute-start.2 = (bf16[16,640]{1,0:T(8,128)(2,1)S(1)}, bf16[16,640]{1,0:T(8,128)(2,1)S(1)}, u32[]{:S(2)}, u32[]{:S(2)}) collective-permute-start(bf16[16,640]{1,0:T(8,128)(2,1)S(1)} %get-tuple-element.22.refs_2_), channel_id=1, source_target_pairs={{0,3},{1,2},{2,1},{3,0},{4,7},{5,6},{6,5},{7,4},{8,11},{9,10},{10,... | collective-permute-start | bytes 61448 | tf_op jit(solution)/shard_map/ppermute | solution.py:284
  37.8 0.0 collective-permute-done.1.refs_4_
  37.8 1.8 %collective-permute-start.4 = (bf16[9,80,640]{2,1,0:T(8,128)(2,1)}, bf16[9,80,640]{2,1,0:T(8,128)(2,1)S(1)}, u32[]{:S(2)}, u32[]{:S(2)}) collective-permute-start(bf16[9,80,640]{2,1,0:T(8,128)(2,1)} %collective-permute-done.3.refs_1_), channel_id=1, source_target_pairs={{0,4},{1,5},{2,6},{3,7},{4,0},{5,1},{6,2},{7,3},{8,12},{9,13},{10,... | collective-permute-start | bytes 2764808 | tf_op jit(solution)/shard_map/ppermute | solution.py:284
  39.7 0.0 collective-permute-done.14.refs_1_
  39.7 0.5 collective-permute-start.16
  40.2 0.0 collective-permute-done.2.refs_5_
  40.2 2.4 %collective-permute-start.18 = (bf16[9,80,640]{2,1,0:T(8,128)(2,1)}, bf16[9,80,640]{2,1,0:T(8,128)(2,1)S(1)}, u32[]{:S(2)}, u32[]{:S(2)}) collective-permute-start(bf16[9,80,640]{2,1,0:T(8,128)(2,1)} %collective-permute-done.14.refs_1_), channel_id=1, source_target_pairs={{0,8},{1,9},{2,10},{3,11},{4,12},{5,13},{6,14},{7,15},{8,0},{9,1},... | collective-permute-start | bytes 2764808 | tf_op jit(solution)/shard_map/ppermute | solution.py:284
  42.6 0.0 collective-permute-done.5.refs_3_
  42.6 0.0 collective-permute-start.6
  42.6 0.0 collective-permute-done.7.refs_5_
  42.6 0.5 collective-permute-start.8
  43.1 0.0 collective-permute-done.4.refs_2_
  43.2 0.1 collective-permute-start.15
  43.2 10.1 %collective-permute-done.16.refs_3_ = bf16[9,80,640]{2,1,0:T(8,128)(2,1)S(1)} collective-permute-done((bf16[9,80,640]{2,1,0:T(8,128)(2,1)}, bf16[9,80,640]{2,1,0:T(8,128)(2,1)S(1)}, u32[]{:S(2)}, u32[]{:S(2)}) %collective-permute-start.16) | collective-permute-done | bytes 921632 | tf_op jit(solution)/shard_map/ppermute | solution.py:284
  53.3 0.0 collective-permute-start.17
  53.3 10.1 %collective-permute-done.18.refs_5_ = bf16[9,80,640]{2,1,0:T(8,128)(2,1)S(1)} collective-permute-done((bf16[9,80,640]{2,1,0:T(8,128)(2,1)}, bf16[9,80,640]{2,1,0:T(8,128)(2,1)S(1)}, u32[]{:S(2)}, u32[]{:S(2)}) %collective-permute-start.18) | collective-permute-done | bytes 921632 | tf_op jit(solution)/shard_map/ppermute | solution.py:284
  63.4 0.0 collective-permute-start.19
  63.4 0.0 copy-done.5
  63.4 2.5 %shard_map.78 = (bf16[4,2,128,1920]{3,2,1,0:T(8,128)(2,1)S(1)}, f32[8,640]{1,0:T(8,128)S(1)}) custom-call(bf16[4,128,640]{2,1,0:T(8,128)(2,1)S(1)} %bitcast.21, bf16[4,128,640]{2,1,0:T(8,128)(2,1)S(1)} %bitcast.24, bf16[16,640]{1,0:T(8,128)(2,1)S(1)} %get-tuple-element.22.refs_2_, bf16[16,640]{1,0:T(8,128)(2,1)S(1)} %collective-permute-done.refs_3_, ...), custom_call_target="tpu_custom_call" | custom-call | flops 629145600 | tf_op jit(solution)/shard_map/pallas_call | solution.py:255
  65.9 0.0 collective-permute-done.6.refs_4_
  65.9 0.9 collective-permute-start.10
  66.8 0.0 collective-permute-done.8.refs_6_
  66.8 4.5 %collective-permute-start.9 = (bf16[2,128,640]{2,1,0:T(8,128)(2,1)S(1)}, bf16[2,128,640]{2,1,0:T(8,128)(2,1)S(1)}, u32[]{:S(2)}, u32[]{:S(2)}) collective-permute-start(bf16[2,128,640]{2,1,0:T(8,128)(2,1)S(1)} %get-tuple-element.28), channel_id=1, source_target_pairs={{0,1},{1,0},{2,3},{3,2},{4,5},{5,4},{6,7},{7,6},{8,9},{9,8},{10,11... | collective-permute-start | bytes 983048 | tf_op jit(solution)/shard_map/ppermute | solution.py:284
  71.3 0.0 copy-done.2
  71.3 9.7 %shard_map.79 = (f32[4,2,128,640]{3,2,1,0:T(8,128)S(1)}, bf16[640,1920]{1,0:T(8,128)(2,1)S(1)}, bf16[640,1920]{1,0:T(8,128)(2,1)S(1)}) custom-call(s32[10]{0:T(128)S(1)} %stack.51.info, bf16[4,2,128,1920]{3,2,1,0:T(8,128)(2,1)S(1)} %get-tuple-element.24.xs, bf16[9,160,640]{2,1,0:T(8,128)(2,1)S(1)} %bitcast.26, ...), custom_call_target="tpu_custom_call" | custom-call | flops 5033164800 | tf_op jit(solution)/shard_map/pallas_call | solution.py:255
  81.0 0.0 collective-permute-done.10.hd
  81.0 5.1 %collective-permute-done.9.hx = bf16[2,128,640]{2,1,0:T(8,128)(2,1)S(1)} collective-permute-done((bf16[2,128,640]{2,1,0:T(8,128)(2,1)S(1)}, bf16[2,128,640]{2,1,0:T(8,128)(2,1)S(1)}, u32[]{:S(2)}, u32[]{:S(2)}) %collective-permute-start.9) | collective-permute-done | bytes 327712 | tf_op jit(solution)/shard_map/ppermute | solution.py:284
  86.1 3.2 %shard_map.80 = (bf16[4,2,128,640]{3,2,1,0:T(8,128)(2,1)S(1)}, bf16[16,640]{1,0:T(8,128)(2,1)S(1)}, bf16[2,128,640]{2,1,0:T(8,128)(2,1)S(1)}, bf16[2,128,640]{2,1,0:T(8,128)(2,1)S(1)}) custom-call(s32[10]{0:T(128)S(1)} %stack.51.info, f32[4,2,128,640]{3,2,1,0:T(8,128)S(1)} %get-tuple-element.25.acc, bf16[640,1920]{1,0:T(8,128)(2,1)S(1)} %get-tuple-element.26.w0, ...), custom_call_target="tpu_custom_call" | custom-call | flops 2516582400 | tf_op jit(solution)/shard_map/pallas_call | solution.py:255
  89.3 0.1 collective-permute-start.11
  89.4 2.0 %collective-permute-start.12 = (bf16[16,640]{1,0:T(8,128)(2,1)S(1)}, bf16[16,640]{1,0:T(8,128)(2,1)S(1)}, u32[]{:S(2)}, u32[]{:S(2)}) collective-permute-start(bf16[16,640]{1,0:T(8,128)(2,1)S(1)} %get-tuple-element.32.refs_1_), channel_id=1, source_target_pairs={{0,2},{1,3},{2,0},{3,1},{4,6},{5,7},{6,4},{7,5},{8,10},{9,11},{10,... | collective-permute-start | bytes 61448 | tf_op jit(solution)/shard_map/ppermute | solution.py:284
  91.4 1.8 %collective-permute-done.11.refs_2_ = bf16[16,640]{1,0:T(8,128)(2,1)S(1)} collective-permute-done((bf16[16,640]{1,0:T(8,128)(2,1)S(1)}, bf16[16,640]{1,0:T(8,128)(2,1)S(1)}, u32[]{:S(2)}, u32[]{:S(2)}) %collective-permute-start.11) | collective-permute-done | bytes 20512 | tf_op jit(solution)/shard_map/ppermute | solution.py:284
  93.2 1.4 %collective-permute-start.13 = (bf16[16,640]{1,0:T(8,128)(2,1)S(1)}, bf16[16,640]{1,0:T(8,128)(2,1)S(1)}, u32[]{:S(2)}, u32[]{:S(2)}) collective-permute-start(bf16[16,640]{1,0:T(8,128)(2,1)S(1)} %get-tuple-element.32.refs_1_), channel_id=1, source_target_pairs={{0,3},{1,2},{2,1},{3,0},{4,7},{5,6},{6,5},{7,4},{8,11},{9,10},{10,... | collective-permute-start | bytes 61448 | tf_op jit(solution)/shard_map/ppermute | solution.py:284
  94.6 0.0 collective-permute-done.12.refs_3_
  94.6 0.6 collective-permute-start.20
  95.2 2.9 %collective-permute-done.13.refs_4_ = bf16[16,640]{1,0:T(8,128)(2,1)S(1)} collective-permute-done((bf16[16,640]{1,0:T(8,128)(2,1)S(1)}, bf16[16,640]{1,0:T(8,128)(2,1)S(1)}, u32[]{:S(2)}, u32[]{:S(2)}) %collective-permute-start.13) | collective-permute-done | bytes 20512 | tf_op jit(solution)/shard_map/ppermute | solution.py:284
  98.1 1.4 %collective-permute-start.21 = (bf16[2,128,640]{2,1,0:T(8,128)(2,1)S(1)}, bf16[2,128,640]{2,1,0:T(8,128)(2,1)S(1)}, u32[]{:S(2)}, u32[]{:S(2)}) collective-permute-start(bf16[2,128,640]{2,1,0:T(8,128)(2,1)S(1)} %get-tuple-element.38), channel_id=1, source_target_pairs={{0,3},{1,2},{2,1},{3,0},{4,7},{5,6},{6,5},{7,4},{8,11},{9,10},{10,... | collective-permute-start | bytes 983048 | tf_op jit(solution)/shard_map/ppermute | solution.py:284
  99.5 2.5 %shard_map.81 = (bf16[4,2,128,1920]{3,2,1,0:T(8,128)(2,1)S(1)}, f32[8,640]{1,0:T(8,128)S(1)}) custom-call(bf16[4,2,128,640]{3,2,1,0:T(8,128)(2,1)S(1)} %get-tuple-element.31.refs_0_, bf16[16,640]{1,0:T(8,128)(2,1)S(1)} %get-tuple-element.32.refs_1_, bf16[16,640]{1,0:T(8,128)(2,1)S(1)} %collective-permute-done.11.refs_2_, ...), custom_call_target="tpu_custom_call" | custom-call | flops 629145600 | tf_op jit(solution)/shard_map/pallas_call | solution.py:255
  102.0 0.0 collective-permute-done.15.refs_2_
  102.0 0.0 collective-permute-done.17.refs_4_
  102.0 0.0 collective-permute-done.19.refs_6_
  102.1 0.0 copy-done.4
  102.1 9.4 %shard_map.82 = (f32[4,2,128,640]{3,2,1,0:T(8,128)S(1)}, bf16[640,1920]{1,0:T(8,128)(2,1)S(1)}, bf16[640,1920]{1,0:T(8,128)(2,1)S(1)}) custom-call(s32[10]{0:T(128)S(1)} %stack.51.info, bf16[4,2,128,1920]{3,2,1,0:T(8,128)(2,1)S(1)} %get-tuple-element.33.xs, bf16[9,160,640]{2,1,0:T(8,128)(2,1)S(1)} %bitcast.27, ...), custom_call_target="tpu_custom_call" | custom-call | flops 5033164800 | tf_op jit(solution)/shard_map/pallas_call | solution.py:255
  111.4 0.0 collective-permute-done.20.hx
  111.5 0.0 collective-permute-done.21.hd
  111.5 3.7 %shard_map.83 = (bf16[4,128,640]{2,1,0:T(8,128)(2,1)}, bf16[4,128,640]{2,1,0:T(8,128)(2,1)}) custom-call(s32[10]{0:T(128)S(1)} %stack.51.info, f32[4,2,128,640]{3,2,1,0:T(8,128)S(1)} %get-tuple-element.34.acc, bf16[640,1920]{1,0:T(8,128)(2,1)S(1)} %get-tuple-element.35.w0, bf16[640,1920]{1,0:T(8,128)(2,1)S(1)} %get-tuple-element.36.w2, ...), custom_call_target="tpu_custom_call" | custom-call | flops 2516582400 | tf_op jit(solution)/shard_map/pallas_call | solution.py:255
  (6 shorter events, 0.0 us)
Async XLA Ops:
  0.6 4.5 %copy-start.3 = (bf16[9,640,160]{1,2,0:T(8,128)(2,1)S(1)}, bf16[9,640,160]{1,2,0:T(8,128)(2,1)}, u32[]{:S(2)}) copy-start(bf16[9,640,160]{1,2,0:T(8,128)(2,1)} %param.11) | copy-start | bytes 5529604
  0.6 19.7 %copy-start = (bf16[1,4,128,640]{3,2,1,0:T(8,128)(2,1)S(1)}, bf16[1,4,128,640]{3,2,1,0:T(8,128)(2,1)}, u32[]{:S(2)}) copy-start(bf16[1,4,128,640]{3,2,1,0:T(8,128)(2,1)} %param.6) | copy-start | bytes 1966084
  0.7 19.7 %copy-start.1 = (bf16[1,4,128,640]{3,2,1,0:T(8,128)(2,1)S(1)}, bf16[1,4,128,640]{3,2,1,0:T(8,128)(2,1)}, u32[]{:S(2)}) copy-start(bf16[1,4,128,640]{3,2,1,0:T(8,128)(2,1)} %param.7) | copy-start | bytes 1966084
  2.1 61.3 %copy-start.5 = (f32[640]{0:T(1024)S(1)}, f32[640]{0:T(1024)}, u32[]{:S(2)}) copy-start(f32[640]{0:T(1024)} %param.8) | copy-start | bytes 7684
  2.1 14.6 %collective-permute-start.3 = (bf16[9,80,640]{2,1,0:T(8,128)(2,1)S(1)}, bf16[9,80,640]{2,1,0:T(8,128)(2,1)}, u32[]{:S(2)}, u32[]{:S(2)}) collective-permute-start(bf16[9,80,640]{2,1,0:T(8,128)(2,1)S(1)} %dynamic-slice_bitcast_fusion.1), channel_id=1, source_target_pairs={{0,1},{1,0},{2,3},{3,2},{4,6},{5,7},{6,4},{7,5},{8,10},{9,11},{10,... | collective-permute-start | bytes 2764808 | tf_op jit(solution)/shard_map/ppermute | solution.py:284
  6.2 65.1 %copy-start.2 = (bf16[9,640,160]{1,2,0:T(8,128)(2,1)S(1)}, bf16[9,640,160]{1,2,0:T(8,128)(2,1)}, u32[]{:S(2)}) copy-start(bf16[9,640,160]{1,2,0:T(8,128)(2,1)} %param.9) | copy-start | bytes 5529604
  6.2 33.5 %collective-permute-start.14 = (bf16[9,80,640]{2,1,0:T(8,128)(2,1)}, bf16[9,80,640]{2,1,0:T(8,128)(2,1)}, u32[]{:S(2)}, u32[]{:S(2)}) collective-permute-start(bf16[9,80,640]{2,1,0:T(8,128)(2,1)} %dynamic-slice_bitcast_fusion), channel_id=1, source_target_pairs={{0,1},{1,0},{2,3},{3,2},{4,6},{5,7},{6,4},{7,5},{8,10},{9,11},{10,... | collective-permute-start | bytes 2764808 | tf_op jit(solution)/shard_map/ppermute | solution.py:284
  16.7 26.0 %collective-permute-start.5 = (bf16[9,80,640]{2,1,0:T(8,128)(2,1)}, bf16[9,80,640]{2,1,0:T(8,128)(2,1)}, u32[]{:S(2)}, u32[]{:S(2)}) collective-permute-start(bf16[9,80,640]{2,1,0:T(8,128)(2,1)} %collective-permute-done.3.refs_1_), channel_id=1, source_target_pairs={{0,2},{1,3},{2,0},{3,1},{4,5},{5,4},{6,7},{7,6},{8,9},{9,8},{10,11... | collective-permute-start | bytes 2764808 | tf_op jit(solution)/shard_map/ppermute | solution.py:284
  18.7 23.9 %collective-permute-start.7 = (bf16[9,80,640]{2,1,0:T(8,128)(2,1)}, bf16[9,80,640]{2,1,0:T(8,128)(2,1)}, u32[]{:S(2)}, u32[]{:S(2)}) collective-permute-start(bf16[9,80,640]{2,1,0:T(8,128)(2,1)} %collective-permute-done.3.refs_1_), channel_id=1, source_target_pairs={{0,8},{1,9},{2,10},{3,11},{4,12},{5,13},{6,14},{7,15},{8,0},{9,1},... | collective-permute-start | bytes 2764808 | tf_op jit(solution)/shard_map/ppermute | solution.py:284
  21.9 12.7 %collective-permute-start = (bf16[16,640]{1,0:T(8,128)(2,1)S(1)}, bf16[16,640]{1,0:T(8,128)(2,1)S(1)}, u32[]{:S(2)}, u32[]{:S(2)}) collective-permute-start(bf16[16,640]{1,0:T(8,128)(2,1)S(1)} %get-tuple-element.22.refs_2_), channel_id=1, source_target_pairs={{0,1},{1,0},{2,3},{3,2},{4,5},{5,4},{6,7},{7,6},{8,9},{9,8},{10,11... | collective-permute-start | bytes 61448 | tf_op jit(solution)/shard_map/ppermute | solution.py:284
  22.5 15.4 %collective-permute-start.1 = (bf16[16,640]{1,0:T(8,128)(2,1)S(1)}, bf16[16,640]{1,0:T(8,128)(2,1)S(1)}, u32[]{:S(2)}, u32[]{:S(2)}) collective-permute-start(bf16[16,640]{1,0:T(8,128)(2,1)S(1)} %get-tuple-element.22.refs_2_), channel_id=1, source_target_pairs={{0,2},{1,3},{2,0},{3,1},{4,6},{5,7},{6,4},{7,5},{8,10},{9,11},{10,... | collective-permute-start | bytes 61448 | tf_op jit(solution)/shard_map/ppermute | solution.py:284
  34.6 5.6 %collective-permute-start.2 = (bf16[16,640]{1,0:T(8,128)(2,1)S(1)}, bf16[16,640]{1,0:T(8,128)(2,1)S(1)}, u32[]{:S(2)}, u32[]{:S(2)}) collective-permute-start(bf16[16,640]{1,0:T(8,128)(2,1)S(1)} %get-tuple-element.22.refs_2_), channel_id=1, source_target_pairs={{0,3},{1,2},{2,1},{3,0},{4,7},{5,6},{6,5},{7,4},{8,11},{9,10},{10,... | collective-permute-start | bytes 61448 | tf_op jit(solution)/shard_map/ppermute | solution.py:284
  37.8 5.3 %collective-permute-start.4 = (bf16[9,80,640]{2,1,0:T(8,128)(2,1)}, bf16[9,80,640]{2,1,0:T(8,128)(2,1)S(1)}, u32[]{:S(2)}, u32[]{:S(2)}) collective-permute-start(bf16[9,80,640]{2,1,0:T(8,128)(2,1)} %collective-permute-done.3.refs_1_), channel_id=1, source_target_pairs={{0,4},{1,5},{2,6},{3,7},{4,0},{5,1},{6,2},{7,3},{8,12},{9,13},{10,... | collective-permute-start | bytes 2764808 | tf_op jit(solution)/shard_map/ppermute | solution.py:284
  39.7 13.6 %collective-permute-start.16 = (bf16[9,80,640]{2,1,0:T(8,128)(2,1)}, bf16[9,80,640]{2,1,0:T(8,128)(2,1)S(1)}, u32[]{:S(2)}, u32[]{:S(2)}) collective-permute-start(bf16[9,80,640]{2,1,0:T(8,128)(2,1)} %collective-permute-done.14.refs_1_), channel_id=1, source_target_pairs={{0,2},{1,3},{2,0},{3,1},{4,5},{5,4},{6,7},{7,6},{8,9},{9,8},{10,11... | collective-permute-start | bytes 2764808 | tf_op jit(solution)/shard_map/ppermute | solution.py:284
  40.2 23.2 %collective-permute-start.18 = (bf16[9,80,640]{2,1,0:T(8,128)(2,1)}, bf16[9,80,640]{2,1,0:T(8,128)(2,1)S(1)}, u32[]{:S(2)}, u32[]{:S(2)}) collective-permute-start(bf16[9,80,640]{2,1,0:T(8,128)(2,1)} %collective-permute-done.14.refs_1_), channel_id=1, source_target_pairs={{0,8},{1,9},{2,10},{3,11},{4,12},{5,13},{6,14},{7,15},{8,0},{9,1},... | collective-permute-start | bytes 2764808 | tf_op jit(solution)/shard_map/ppermute | solution.py:284
  42.6 23.3 %collective-permute-start.6 = (bf16[9,80,640]{2,1,0:T(8,128)(2,1)}, bf16[9,80,640]{2,1,0:T(8,128)(2,1)S(1)}, u32[]{:S(2)}, u32[]{:S(2)}) collective-permute-start(bf16[9,80,640]{2,1,0:T(8,128)(2,1)} %collective-permute-done.5.refs_3_), channel_id=1, source_target_pairs={{0,4},{1,5},{2,6},{3,7},{4,0},{5,1},{6,2},{7,3},{8,12},{9,13},{10,... | collective-permute-start | bytes 2764808 | tf_op jit(solution)/shard_map/ppermute | solution.py:284
  42.6 24.1 %collective-permute-start.8 = (bf16[9,80,640]{2,1,0:T(8,128)(2,1)}, bf16[9,80,640]{2,1,0:T(8,128)(2,1)S(1)}, u32[]{:S(2)}, u32[]{:S(2)}) collective-permute-start(bf16[9,80,640]{2,1,0:T(8,128)(2,1)} %collective-permute-done.7.refs_5_), channel_id=1, source_target_pairs={{0,4},{1,5},{2,6},{3,7},{4,0},{5,1},{6,2},{7,3},{8,12},{9,13},{10,... | collective-permute-start | bytes 2764808 | tf_op jit(solution)/shard_map/ppermute | solution.py:284
  43.2 58.9 %collective-permute-start.15 = (bf16[9,80,640]{2,1,0:T(8,128)(2,1)}, bf16[9,80,640]{2,1,0:T(8,128)(2,1)S(1)}, u32[]{:S(2)}, u32[]{:S(2)}) collective-permute-start(bf16[9,80,640]{2,1,0:T(8,128)(2,1)} %collective-permute-done.14.refs_1_), channel_id=1, source_target_pairs={{0,4},{1,5},{2,6},{3,7},{4,0},{5,1},{6,2},{7,3},{8,12},{9,13},{10,... | collective-permute-start | bytes 2764808 | tf_op jit(solution)/shard_map/ppermute | solution.py:284
  53.3 48.7 %collective-permute-start.17 = (bf16[9,80,640]{2,1,0:T(8,128)(2,1)S(1)}, bf16[9,80,640]{2,1,0:T(8,128)(2,1)S(1)}, u32[]{:S(2)}, u32[]{:S(2)}) collective-permute-start(bf16[9,80,640]{2,1,0:T(8,128)(2,1)S(1)} %collective-permute-done.16.refs_3_), channel_id=1, source_target_pairs={{0,4},{1,5},{2,6},{3,7},{4,0},{5,1},{6,2},{7,3},{8,12},{9,13},{10,... | collective-permute-start | bytes 2764808 | tf_op jit(solution)/shard_map/ppermute | solution.py:284
  63.4 38.6 %collective-permute-start.19 = (bf16[9,80,640]{2,1,0:T(8,128)(2,1)S(1)}, bf16[9,80,640]{2,1,0:T(8,128)(2,1)S(1)}, u32[]{:S(2)}, u32[]{:S(2)}) collective-permute-start(bf16[9,80,640]{2,1,0:T(8,128)(2,1)S(1)} %collective-permute-done.18.refs_5_), channel_id=1, source_target_pairs={{0,4},{1,5},{2,6},{3,7},{4,0},{5,1},{6,2},{7,3},{8,12},{9,13},{10,... | collective-permute-start | bytes 2764808 | tf_op jit(solution)/shard_map/ppermute | solution.py:284
  65.9 15.1 %collective-permute-start.10 = (bf16[2,128,640]{2,1,0:T(8,128)(2,1)S(1)}, bf16[2,128,640]{2,1,0:T(8,128)(2,1)S(1)}, u32[]{:S(2)}, u32[]{:S(2)}) collective-permute-start(bf16[2,128,640]{2,1,0:T(8,128)(2,1)S(1)} %get-tuple-element.29), channel_id=1, source_target_pairs={{1,2},{2,1},{5,6},{6,5},{9,10},{10,9},{13,14},{14,13},{17,18},{18,... | collective-permute-start | bytes 983048 | tf_op jit(solution)/shard_map/ppermute | solution.py:284
  66.8 19.3 %collective-permute-start.9 = (bf16[2,128,640]{2,1,0:T(8,128)(2,1)S(1)}, bf16[2,128,640]{2,1,0:T(8,128)(2,1)S(1)}, u32[]{:S(2)}, u32[]{:S(2)}) collective-permute-start(bf16[2,128,640]{2,1,0:T(8,128)(2,1)S(1)} %get-tuple-element.28), channel_id=1, source_target_pairs={{0,1},{1,0},{2,3},{3,2},{4,5},{5,4},{6,7},{7,6},{8,9},{9,8},{10,11... | collective-permute-start | bytes 983048 | tf_op jit(solution)/shard_map/ppermute | solution.py:284
  86.1 8.5 %copy-start.6 = (f32[640]{0:T(1024)S(1)}, f32[640]{0:T(1024)}, u32[]{:S(2)}) copy-start(f32[640]{0:T(1024)} %param.10) | copy-start | bytes 7684
  86.1 16.0 %copy-start.4 = (bf16[9,640,160]{1,2,0:T(8,128)(2,1)S(1)}, bf16[9,640,160]{1,2,0:T(8,128)(2,1)}, u32[]{:S(2)}) copy-start(bf16[9,640,160]{1,2,0:T(8,128)(2,1)} %param.11) | copy-start | bytes 5529604
  89.3 3.8 %collective-permute-start.11 = (bf16[16,640]{1,0:T(8,128)(2,1)S(1)}, bf16[16,640]{1,0:T(8,128)(2,1)S(1)}, u32[]{:S(2)}, u32[]{:S(2)}) collective-permute-start(bf16[16,640]{1,0:T(8,128)(2,1)S(1)} %get-tuple-element.32.refs_1_), channel_id=1, source_target_pairs={{0,1},{1,0},{2,3},{3,2},{4,5},{5,4},{6,7},{7,6},{8,9},{9,8},{10,11... | collective-permute-start | bytes 61448 | tf_op jit(solution)/shard_map/ppermute | solution.py:284
  89.4 5.2 %collective-permute-start.12 = (bf16[16,640]{1,0:T(8,128)(2,1)S(1)}, bf16[16,640]{1,0:T(8,128)(2,1)S(1)}, u32[]{:S(2)}, u32[]{:S(2)}) collective-permute-start(bf16[16,640]{1,0:T(8,128)(2,1)S(1)} %get-tuple-element.32.refs_1_), channel_id=1, source_target_pairs={{0,2},{1,3},{2,0},{3,1},{4,6},{5,7},{6,4},{7,5},{8,10},{9,11},{10,... | collective-permute-start | bytes 61448 | tf_op jit(solution)/shard_map/ppermute | solution.py:284
  93.2 4.9 %collective-permute-start.13 = (bf16[16,640]{1,0:T(8,128)(2,1)S(1)}, bf16[16,640]{1,0:T(8,128)(2,1)S(1)}, u32[]{:S(2)}, u32[]{:S(2)}) collective-permute-start(bf16[16,640]{1,0:T(8,128)(2,1)S(1)} %get-tuple-element.32.refs_1_), channel_id=1, source_target_pairs={{0,3},{1,2},{2,1},{3,0},{4,7},{5,6},{6,5},{7,4},{8,11},{9,10},{10,... | collective-permute-start | bytes 61448 | tf_op jit(solution)/shard_map/ppermute | solution.py:284
  94.6 16.8 %collective-permute-start.20 = (bf16[2,128,640]{2,1,0:T(8,128)(2,1)S(1)}, bf16[2,128,640]{2,1,0:T(8,128)(2,1)S(1)}, u32[]{:S(2)}, u32[]{:S(2)}) collective-permute-start(bf16[2,128,640]{2,1,0:T(8,128)(2,1)S(1)} %get-tuple-element.37), channel_id=1, source_target_pairs={{0,1},{1,0},{2,3},{3,2},{4,5},{5,4},{6,7},{7,6},{8,9},{9,8},{10,11... | collective-permute-start | bytes 983048 | tf_op jit(solution)/shard_map/ppermute | solution.py:284
  98.1 13.4 %collective-permute-start.21 = (bf16[2,128,640]{2,1,0:T(8,128)(2,1)S(1)}, bf16[2,128,640]{2,1,0:T(8,128)(2,1)S(1)}, u32[]{:S(2)}, u32[]{:S(2)}) collective-permute-start(bf16[2,128,640]{2,1,0:T(8,128)(2,1)S(1)} %get-tuple-element.38), channel_id=1, source_target_pairs={{0,3},{1,2},{2,1},{3,0},{4,7},{5,6},{6,5},{7,4},{8,11},{9,10},{10,... | collective-permute-start | bytes 983048 | tf_op jit(solution)/shard_map/ppermute | solution.py:284
